TPU v7x, 32 devices: a whole 2x2x4 slice. The times are simulated.
32 devices in a mesh: section: 4 (over x, core), wide: 8 (over z, y).
Axes of the slice: x: 2, y: 2, z: 4, core: 2. Of those that a mesh axis runs over, the one named last changes fastest.
Arguments:
- tokens_in: bfloat16 [2, 2048, 1024], P(None, 'wide', 'section'), may hold values from -6 to 6
- cotangent: bfloat16 [2, 2048, 1024], P(None, 'wide', 'section'), may hold values from -6 to 6
- routes: int32 [2, 2048, 1], P(None, 'wide'), may hold values from 0 to 7; in each aligned block of 256 rows (0 to 255, 256 to 511, ..., all dimensions but the last counted through in order) at most 40 rows name the same one
- seq_lengths: int32 [2], replicated, may hold values from 128 to 256, as said below
- qkv_weight: bfloat16 [1024, 3072], P(('section', 'wide')), may hold values from -0.1875 to 0.1875
- out_weight: bfloat16 [1024, 1024], P(('section', 'wide')), may hold values from -0.75 to 0.75
- attn_gain: bfloat16 [1024], P(('section', 'wide')), may hold values from 0.5 to 1.5
- ffn_in: bfloat16 [1024, 4096], P(('section', 'wide')), may hold values from -0.1875 to 0.1875
- ffn_back: bfloat16 [4096, 1024], P(('section', 'wide')), may hold values from -0.09375 to 0.09375
- ffn_gain: bfloat16 [1024], P(('section', 'wide')), may hold values from 0.5 to 1.5
- centroids: bfloat16 [8, 1024], P('wide', 'section'), may hold values from -0.1875 to 0.1875
- first_gain: bfloat16 [8, 1024], P('wide', 'section'), may hold values from 0.5 to 1.5
- first_in: bfloat16 [8, 1024, 4096], P('wide', 'section'), may hold values from -0.1875 to 0.1875
- first_back: bfloat16 [8, 4096, 1024], P('wide', 'section'), may hold values from -0.09375 to 0.09375
- second_gain: bfloat16 [8, 1024], P('wide', 'section'), may hold values from 0.5 to 1.5
- second_in: bfloat16 [8, 1024, 4096], P('wide', 'section'), may hold values from -0.1875 to 0.1875
- second_back: bfloat16 [8, 4096, 1024], P('wide', 'section'), may hold values from -0.09375 to 0.09375
Outputs:
- block_out: bfloat16 [2, 2048, 1024], P(None, 'wide', 'section')
- tokens_grad: float32 [2, 2048, 1024], P(None, 'wide', 'section')
- qkv_grad: float32 [1024, 3072], P(('section', 'wide'))
- out_grad: float32 [1024, 1024], P(('section', 'wide'))
- attn_gain_grad: float32 [1024], P(('section', 'wide'))
- ffn_in_grad: float32 [1024, 4096], P(('section', 'wide'))
- ffn_back_grad: float32 [4096, 1024], P(('section', 'wide'))
- ffn_gain_grad: float32 [1024], P(('section', 'wide'))
- centroids_grad: float32 [8, 1024], P('wide', 'section')
- first_gain_grad: float32 [8, 1024], P('wide', 'section')
- first_in_grad: float32 [8, 1024, 4096], P('wide', 'section')
- first_back_grad: float32 [8, 4096, 1024], P('wide', 'section')
- second_gain_grad: float32 [8, 1024], P('wide', 'section')
- second_in_grad: float32 [8, 1024, 4096], P('wide', 'section')
- second_back_grad: float32 [8, 4096, 1024], P('wide', 'section')
Inputs may be any that keep to these rules, and one draw needn't show every extreme that they name: `routes`: in each micro-batch, at most 40 of one device's 256 rows name the same expert. `seq_lengths`: each micro-batch holds sequences of one length, 128 or 256; a device's 256 rows of a micro-batch are whole sequences in order; both lengths occur.
All inputs are finite; a program needn't handle non-finite values.
Results may differ from a plain program's by a relative error of at most 0.015.
Values may be sent and summed in bfloat16 or wider, within the bound.
A program may use at most 512 MiB of HBM per device.

v0:
```python
import jax
import jax.numpy as jnp
from jax import lax
from jax.sharding import PartitionSpec as P

HEADS = 16


def as_sent(x):
    return jax.tree.map(lambda a: a.astype(jnp.bfloat16) if a.dtype == jnp.float32 else a, x)


def shifted(value, axis, steps):
    count = lax.axis_size(axis)
    initial, last = (max(0, -steps), min(count, count - steps))
    return lax.ppermute(value, axis, [(source, source + steps) for source in range(initial, last)])


def product(left, right):
    return jnp.dot(left, right, preferred_element_type=jnp.float32)


def product_nt(left, right):
    return lax.dot_general(
        left, right, (((1,), (1,)), ((), ())), preferred_element_type=jnp.float32
    )


def product_tn(left, right):
    return lax.dot_general(
        left, right, (((0,), (0,)), ((), ())), preferred_element_type=jnp.float32
    )


def gelu_value(values_in):
    return 0.5 * values_in * (1.0 + lax.erf(values_in * 0.7071067811865476))


def gelu_slope(values_in):
    return (
        0.5 * (1.0 + lax.erf(values_in * 0.7071067811865476))
        + values_in * jnp.exp(-0.5 * values_in * values_in) * 0.3989422804014327
    )


def layer_norm(values_in, gain_vec):
    centred = values_in - jnp.mean(values_in, axis=-1, keepdims=True)
    norm_scale = lax.rsqrt(jnp.mean(centred * centred, axis=-1, keepdims=True) + 1e-05)
    unit_vals = centred * norm_scale
    return (unit_vals * gain_vec, unit_vals, norm_scale)


def norm_back(d_normed, gain_vec, unit_vals, norm_scale):
    d_unit = d_normed * gain_vec
    d_gain = jnp.sum(d_normed * unit_vals, axis=0)
    d_rows = norm_scale * (
        d_unit
        - jnp.mean(d_unit, axis=-1, keepdims=True)
        - unit_vals * jnp.mean(d_unit * unit_vals, axis=-1, keepdims=True)
    )
    return (d_rows, d_gain)


def ffn_parts(rows_in, first_w, gain_vec):
    normed, unit_vals, norm_scale = layer_norm(rows_in, gain_vec)
    normed_b = normed.astype(jnp.bfloat16)
    before = product(normed_b, first_w)
    hidden_b = gelu_value(before).astype(jnp.bfloat16)
    return (normed_b, unit_vals, norm_scale, before, hidden_b)


def ffn_output(rows_in, saved, second_w):
    return rows_in + product(saved[4], second_w)


def ffn_gradients(grad_b, saved, first_w, second_w, gain_vec):
    normed_b, unit_vals, norm_scale, before, hidden_b = saved
    d_second = product_tn(hidden_b, grad_b)
    d_before = (product_nt(grad_b, second_w) * gelu_slope(before)).astype(jnp.bfloat16)
    d_first = product_tn(normed_b, d_before)
    d_normed = product_nt(d_before, first_w)
    d_rows, d_gain = norm_back(d_normed, gain_vec, unit_vals, norm_scale)
    return (d_rows, d_first, d_second, d_gain)


def attention_parts(rows_in, qkv_w, gain_vec, head_count):
    row_count, model_width = rows_in.shape
    normed, unit_vals, norm_scale = layer_norm(rows_in, gain_vec)
    normed_b = normed.astype(jnp.bfloat16)
    packed = product(normed_b, qkv_w).astype(jnp.bfloat16)
    head_size = model_width // head_count
    queries = packed[:, :model_width].reshape(row_count, head_count, head_size)
    keys_all = packed[:, model_width : 2 * model_width].reshape(row_count, head_count, head_size)
    values_all = packed[:, 2 * model_width :].reshape(row_count, head_count, head_size)
    return (normed_b, unit_vals, norm_scale, queries, keys_all, values_all)


def block_probs(query_rows, keys_all, first_row, length):
    raw = jnp.einsum("qhd,khd->hqk", query_rows, keys_all, preferred_element_type=jnp.float32)
    row_pos = first_row + jnp.arange(query_rows.shape[0], dtype=jnp.int32)
    col_pos = jnp.arange(keys_all.shape[0], dtype=jnp.int32)
    allowed = (row_pos[:, None] >= col_pos[None, :]) & (
        row_pos[:, None] // length == col_pos[None, :] // length
    )
    scores = jnp.where(allowed[None], raw * query_rows.shape[2] ** (-0.5), -1e30)
    highest = jnp.max(scores, axis=-1, keepdims=True)
    expo_vals = jnp.exp(scores - highest)
    return expo_vals / jnp.sum(expo_vals, axis=-1, keepdims=True)


def attention_forward(rows_in, length, qkv_w, out_w, gain_vec, head_count):
    parts = attention_parts(rows_in, qkv_w, gain_vec, head_count)
    queries, keys_all, values_all = (parts[3], parts[4], parts[5])
    row_count = queries.shape[0]
    block_span = min(row_count, 512)
    pieces = []
    for first_row in range(0, row_count, block_span):
        attn_probs = block_probs(
            queries[first_row : first_row + block_span], keys_all, first_row, length
        )
        mixed_rows = jnp.einsum(
            "hqk,khd->qhd",
            attn_probs.astype(jnp.bfloat16),
            values_all,
            preferred_element_type=jnp.float32,
        )
        pieces.append(mixed_rows.reshape(block_span, -1).astype(jnp.bfloat16))
    mixed_all = jnp.concatenate(pieces, axis=0)
    return (rows_in + product(mixed_all, out_w)).astype(jnp.bfloat16)


def attention_backward(rows_in, length, grad_b, qkv_w, out_w, gain_vec, head_count):
    normed_b, unit_vals, norm_scale, queries, keys_all, values_all = attention_parts(
        rows_in, qkv_w, gain_vec, head_count
    )
    row_count, model_width = rows_in.shape
    d_mixed = product_nt(grad_b, out_w).astype(jnp.bfloat16).reshape(queries.shape)
    block_span = min(row_count, 512)
    inv_root = queries.shape[2] ** (-0.5)
    d_keys = jnp.zeros(keys_all.shape, jnp.float32)
    d_values = jnp.zeros(values_all.shape, jnp.float32)
    d_queries = []
    pieces = []
    for first_row in range(0, row_count, block_span):
        query_rows = queries[first_row : first_row + block_span]
        grad_rows = d_mixed[first_row : first_row + block_span]
        attn_probs = block_probs(query_rows, keys_all, first_row, length)
        probs_b = attn_probs.astype(jnp.bfloat16)
        mixed_rows = jnp.einsum(
            "hqk,khd->qhd", probs_b, values_all, preferred_element_type=jnp.float32
        )
        pieces.append(mixed_rows.reshape(block_span, -1).astype(jnp.bfloat16))
        d_probs = jnp.einsum(
            "qhd,khd->hqk", grad_rows, values_all, preferred_element_type=jnp.float32
        )
        row_delta = jnp.sum(attn_probs * d_probs, axis=-1, keepdims=True)
        d_scores = (attn_probs * (d_probs - row_delta) * inv_root).astype(jnp.bfloat16)
        d_queries.append(
            jnp.einsum("hqk,khd->qhd", d_scores, keys_all, preferred_element_type=jnp.float32)
        )
        d_keys = d_keys + jnp.einsum(
            "hqk,qhd->khd", d_scores, query_rows, preferred_element_type=jnp.float32
        )
        d_values = d_values + jnp.einsum(
            "hqk,qhd->khd", probs_b, grad_rows, preferred_element_type=jnp.float32
        )
    mixed_all = jnp.concatenate(pieces, axis=0)
    d_out = product_tn(mixed_all, grad_b)
    d_packed = jnp.concatenate(
        [
            jnp.concatenate(d_queries, axis=0).reshape(row_count, model_width),
            d_keys.reshape(row_count, model_width),
            d_values.reshape(row_count, model_width),
        ],
        axis=1,
    ).astype(jnp.bfloat16)
    d_qkv = product_tn(normed_b, d_packed)
    d_normed = product_nt(d_packed, qkv_w)
    d_rows, d_gain = norm_back(d_normed, gain_vec, unit_vals, norm_scale)
    return (grad_b.astype(jnp.float32) + d_rows, d_qkv, d_out, d_gain)


def body(
    tokens_in,
    cotangent,
    routes,
    seq_lengths,
    qkv_weight,
    out_weight,
    attn_gain,
    ffn_in,
    ffn_back,
    ffn_gain,
    centroids,
    first_gain,
    first_in,
    first_back,
    second_gain,
    second_in,
    second_back,
):
    sections = lax.axis_size("section")
    wide_count = lax.axis_size("wide")
    section_id = lax.axis_index("section")
    micro, row_count = (tokens_in.shape[0], tokens_in.shape[1])
    model_width = tokens_in.shape[2] * sections
    capacity = 5 * row_count // (4 * wide_count)
    expert_rows = wide_count * capacity
    first_section = sections - 2
    last_section = sections - 1
    whole_in, whole_cot = (
        lax.all_gather(tokens_in, "section", axis=2, tiled=True),
        lax.all_gather(cotangent, "section", axis=2, tiled=True),
    )
    dense = (
        lax.all_gather(qkv_weight, ("section", "wide"), axis=0, tiled=True),
        lax.all_gather(out_weight, ("section", "wide"), axis=0, tiled=True),
        lax.all_gather(ffn_in, ("section", "wide"), axis=0, tiled=True),
        lax.all_gather(ffn_back, ("section", "wide"), axis=0, tiled=True),
        lax.all_gather(attn_gain, ("section", "wide"), axis=0, tiled=True),
        lax.all_gather(ffn_gain, ("section", "wide"), axis=0, tiled=True),
    )
    qkv_full, out_full, in_full, back_full = (dense[0], dense[1], dense[2], dense[3])
    gain_attn = dense[4].astype(jnp.float32)
    gain_ffn = dense[5].astype(jnp.float32)
    got = (
        lax.all_gather(first_in, "section", axis=1, tiled=True),
        lax.all_gather(first_back, "section", axis=1, tiled=True),
        lax.all_gather(second_in, "section", axis=1, tiled=True),
        lax.all_gather(second_back, "section", axis=1, tiled=True),
        lax.all_gather(first_gain, "section", axis=1, tiled=True),
        lax.all_gather(second_gain, "section", axis=1, tiled=True),
        lax.all_gather(centroids, "section", axis=1, tiled=True),
    )
    first_set = (got[0][0], got[1][0], got[4][0].astype(jnp.float32))
    second_set = (got[2][0], got[3][0], got[5][0].astype(jnp.float32))
    centre = got[6][0].astype(jnp.float32)
    expert_ids = jnp.arange(wide_count, dtype=jnp.int32)
    choose = (routes == expert_ids).astype(jnp.int32)
    ranking = jnp.cumsum(choose, axis=1) - 1
    slot_table = routes[:, :, 0] * capacity + jnp.sum(ranking * choose, axis=2)

    def pack(token_rows, slot_idx):
        buffer_rows = (
            jnp.zeros((wide_count * capacity, model_width), token_rows.dtype)
            .at[slot_idx]
            .set(token_rows)
        )
        return buffer_rows.reshape(wide_count, capacity, model_width)

    def unpack(buffer_rows, slot_idx):
        return jnp.take(buffer_rows.reshape(wide_count * capacity, model_width), slot_idx, axis=0)

    def place(token_rows):
        return (
            jnp.zeros((2, expert_rows, model_width), jnp.bfloat16).at[0, :row_count].set(token_rows)
        )

    def run_attention(token_rows, received, incoming, length):
        return place(
            attention_forward(
                token_rows.astype(jnp.float32), length, qkv_full, out_full, gain_attn, HEADS
            )
        )

    def run_dense(token_rows, received, incoming, length):
        rows_f = token_rows.astype(jnp.float32)
        saved = ffn_parts(rows_f, in_full, gain_ffn)
        return place(ffn_output(rows_f, saved, back_full).astype(jnp.bfloat16))

    def run_first(token_rows, received, incoming, length):
        rows_f = received.astype(jnp.float32)
        saved = ffn_parts(rows_f, first_set[0], first_set[2])
        return jnp.stack([ffn_output(rows_f, saved, first_set[1]).astype(jnp.bfloat16), received])

    def run_second(token_rows, received, incoming, length):
        first_rows = incoming[0].astype(jnp.float32)
        routed_rows = incoming[1].astype(jnp.float32)
        saved = ffn_parts(first_rows, second_set[0], second_set[2])
        second_rows = ffn_output(first_rows, saved, second_set[1])
        gate_vals = jax.nn.sigmoid(jnp.sum(routed_rows * centre, axis=-1, keepdims=True))
        mixed_rows = routed_rows + gate_vals * second_rows
        return jnp.stack([mixed_rows.astype(jnp.bfloat16), jnp.zeros_like(received)])

    ticks = micro + sections - 1
    incoming = jnp.zeros((2, expert_rows, model_width), jnp.bfloat16)
    kept_in = jnp.zeros((micro, 2, expert_rows, model_width), jnp.bfloat16)
    kept_routed = jnp.zeros((micro, expert_rows, model_width), jnp.bfloat16)
    result_rows = jnp.zeros((micro, row_count, model_width), jnp.bfloat16)
    for tick_num in range(ticks):
        micro_idx = tick_num - section_id
        active = (micro_idx >= 0) & (micro_idx < micro)
        picked = jnp.clip(micro_idx, 0, micro - 1)
        length = seq_lengths[picked]
        slot_idx = slot_table[picked]
        token_rows = jnp.where(section_id == 0, whole_in[picked], incoming[0, :row_count])
        received = lax.all_to_all(
            as_sent(pack(token_rows, slot_idx)), "wide", split_axis=0, concat_axis=0, tiled=True
        ).reshape(expert_rows, model_width)
        outgoing = lax.switch(
            section_id,
            [run_attention, run_dense, run_first, run_second],
            token_rows,
            received,
            incoming,
            length,
        )
        returned = unpack(
            lax.all_to_all(
                as_sent(outgoing[0].reshape(wide_count, capacity, model_width)),
                "wide",
                split_axis=0,
                concat_axis=0,
                tiled=True,
            ),
            slot_idx,
        )
        kept_in = kept_in.at[picked].set(jnp.where(active, incoming, kept_in[picked]))
        kept_routed = kept_routed.at[picked].set(jnp.where(active, received, kept_routed[picked]))
        result_rows = result_rows.at[picked].set(
            jnp.where(active & (section_id == last_section), returned, result_rows[picked])
        )
        if tick_num + 1 < ticks:
            incoming = jax.tree.map(
                lambda part, own: part.astype(own.dtype),
                shifted(as_sent(outgoing), "section", 1),
                outgoing,
            )
    zeros_rows = jnp.zeros((expert_rows, model_width), jnp.bfloat16)
    zeros_tokens = jnp.zeros((row_count, model_width), jnp.float32)
    blank = jnp.zeros((2, expert_rows, model_width), jnp.bfloat16)

    def grow(active, total, extra):
        return jnp.where(active, total + extra, total)

    def back_attention(stored, routed, token_rows, grads_in, grad_z, length, active, totals):
        d_tokens, d_qkv, d_out, d_gain = attention_backward(
            token_rows.astype(jnp.float32),
            length,
            grads_in[0, :row_count],
            qkv_full,
            out_full,
            gain_attn,
            HEADS,
        )
        totals = (
            grow(active, totals[0], d_qkv),
            grow(active, totals[1], d_out),
            grow(active, totals[2], d_gain),
        ) + totals[3:]
        return (blank, zeros_rows, d_tokens, totals)

    def back_dense(stored, routed, token_rows, grads_in, grad_z, length, active, totals):
        grad_rows = grads_in[0, :row_count]
        saved = ffn_parts(stored[0, :row_count].astype(jnp.float32), in_full, gain_ffn)
        d_norm, d_first, d_second, d_gain = ffn_gradients(
            grad_rows, saved, in_full, back_full, gain_ffn
        )
        d_tokens = grad_rows.astype(jnp.float32) + d_norm
        totals = (
            totals[:3]
            + (
                grow(active, totals[3], d_first),
                grow(active, totals[4], d_second),
                grow(active, totals[5], d_gain),
            )
            + totals[6:]
        )
        return (place(d_tokens.astype(jnp.bfloat16)), zeros_rows, zeros_tokens, totals)

    def back_first(stored, routed, token_rows, grads_in, grad_z, length, active, totals):
        saved = ffn_parts(routed.astype(jnp.float32), first_set[0], first_set[2])
        d_norm, d_first, d_second, d_gain = ffn_gradients(
            grads_in[0], saved, first_set[0], first_set[1], first_set[2]
        )
        d_routed = grads_in[0].astype(jnp.float32) + d_norm + grads_in[1].astype(jnp.float32)
        totals = totals[:6] + (
            grow(active, totals[6], d_first),
            grow(active, totals[7], d_second),
            grow(active, totals[8], d_gain),
            totals[9],
        )
        return (blank, d_routed.astype(jnp.bfloat16), zeros_tokens, totals)

    def back_second(stored, routed, token_rows, grads_in, grad_z, length, active, totals):
        first_rows = stored[0].astype(jnp.float32)
        routed_rows = stored[1].astype(jnp.float32)
        saved = ffn_parts(first_rows, second_set[0], second_set[2])
        second_rows = ffn_output(first_rows, saved, second_set[1])
        gate_vals = jax.nn.sigmoid(jnp.sum(routed_rows * centre, axis=-1, keepdims=True))
        d_mixed = grad_z.astype(jnp.float32)
        d_second_rows = gate_vals * d_mixed
        d_norm, d_first, d_second, d_gain = ffn_gradients(
            d_second_rows.astype(jnp.bfloat16), saved, second_set[0], second_set[1], second_set[2]
        )
        d_first_rows = d_second_rows + d_norm
        d_logit = (
            jnp.sum(d_mixed * second_rows, axis=-1, keepdims=True) * gate_vals * (1.0 - gate_vals)
        )
        d_centre = jnp.sum(d_logit * routed_rows, axis=0)
        d_routed = d_mixed + d_logit * centre
        totals = totals[:6] + (
            grow(active, totals[6], d_first),
            grow(active, totals[7], d_second),
            grow(active, totals[8], d_gain),
            grow(active, totals[9], d_centre),
        )
        return (
            jnp.stack([d_first_rows.astype(jnp.bfloat16), d_routed.astype(jnp.bfloat16)]),
            zeros_rows,
            zeros_tokens,
            totals,
        )

    totals = (
        jnp.zeros(qkv_full.shape, jnp.float32),
        jnp.zeros(out_full.shape, jnp.float32),
        jnp.zeros((model_width,), jnp.float32),
        jnp.zeros(in_full.shape, jnp.float32),
        jnp.zeros(back_full.shape, jnp.float32),
        jnp.zeros((model_width,), jnp.float32),
        jnp.zeros(first_set[0].shape, jnp.float32),
        jnp.zeros(first_set[1].shape, jnp.float32),
        jnp.zeros((model_width,), jnp.float32),
        jnp.zeros((model_width,), jnp.float32),
    )
    grads_in = blank
    grad_tokens = jnp.zeros((micro, row_count, model_width), jnp.float32)
    for tick_num in range(ticks):
        micro_idx = tick_num - (last_section - section_id)
        active = (micro_idx >= 0) & (micro_idx < micro)
        picked = jnp.clip(micro_idx, 0, micro - 1)
        length = seq_lengths[picked]
        slot_idx = slot_table[picked]
        grad_z = lax.all_to_all(
            pack(whole_cot[picked], slot_idx), "wide", split_axis=0, concat_axis=0, tiled=True
        ).reshape(expert_rows, model_width)
        outgoing, routed_grad, d_tokens, totals = lax.switch(
            section_id,
            [back_attention, back_dense, back_first, back_second],
            kept_in[picked],
            kept_routed[picked],
            whole_in[picked],
            grads_in,
            grad_z,
            length,
            active,
            totals,
        )
        token_grad = unpack(
            lax.all_to_all(
                as_sent(routed_grad.reshape(wide_count, capacity, model_width)),
                "wide",
                split_axis=0,
                concat_axis=0,
                tiled=True,
            ),
            slot_idx,
        )
        outgoing = jnp.where(section_id == first_section, place(token_grad), outgoing)
        grad_tokens = grad_tokens.at[picked].set(
            jnp.where(active & (section_id == 0), d_tokens, grad_tokens[picked])
        )
        if tick_num + 1 < ticks:
            grads_in = shifted(as_sent(outgoing), "section", -1).astype(outgoing.dtype)
    sent = (
        lax.all_to_all(
            result_rows.astype(jnp.float32)[None].astype(jnp.bfloat16),
            "section",
            split_axis=3,
            concat_axis=0,
            tiled=True,
        ).astype(jnp.float32),
        lax.all_to_all(
            grad_tokens[None].astype(jnp.bfloat16),
            "section",
            split_axis=3,
            concat_axis=0,
            tiled=True,
        ).astype(jnp.float32),
    )
    block_out = sent[0][last_section].astype(jnp.bfloat16)
    tokens_grad = sent[1][0]
    dense_grads = (
        lax.psum_scatter(totals[0], ("section", "wide"), scatter_dimension=0, tiled=True),
        lax.psum_scatter(totals[1], ("section", "wide"), scatter_dimension=0, tiled=True),
        lax.psum_scatter(totals[3], ("section", "wide"), scatter_dimension=0, tiled=True),
        lax.psum_scatter(totals[4], ("section", "wide"), scatter_dimension=0, tiled=True),
        lax.psum_scatter(totals[2], ("section", "wide"), scatter_dimension=0, tiled=True),
        lax.psum_scatter(totals[5], ("section", "wide"), scatter_dimension=0, tiled=True),
    )
    qkv_grad, out_grad, ffn_in_grad, ffn_back_grad = (
        dense_grads[0],
        dense_grads[1],
        dense_grads[2],
        dense_grads[3],
    )
    attn_gain_grad, ffn_gain_grad = (dense_grads[4], dense_grads[5])
    on_first = section_id == first_section
    on_last = section_id == last_section
    parts = (
        lax.psum_scatter(
            jnp.where(on_first, totals[6], 0.0)[None].astype(jnp.bfloat16),
            "section",
            scatter_dimension=1,
            tiled=True,
        ).astype(jnp.float32),
        lax.psum_scatter(
            jnp.where(on_first, totals[7], 0.0)[None].astype(jnp.bfloat16),
            "section",
            scatter_dimension=1,
            tiled=True,
        ).astype(jnp.float32),
        lax.psum_scatter(
            jnp.where(on_last, totals[6], 0.0)[None].astype(jnp.bfloat16),
            "section",
            scatter_dimension=1,
            tiled=True,
        ).astype(jnp.float32),
        lax.psum_scatter(
            jnp.where(on_last, totals[7], 0.0)[None].astype(jnp.bfloat16),
            "section",
            scatter_dimension=1,
            tiled=True,
        ).astype(jnp.float32),
        lax.psum_scatter(
            jnp.where(on_first, totals[8], 0.0)[None].astype(jnp.bfloat16),
            "section",
            scatter_dimension=1,
            tiled=True,
        ).astype(jnp.float32),
        lax.psum_scatter(
            jnp.where(on_last, totals[8], 0.0)[None].astype(jnp.bfloat16),
            "section",
            scatter_dimension=1,
            tiled=True,
        ).astype(jnp.float32),
        lax.psum_scatter(
            totals[9][None].astype(jnp.bfloat16), "section", scatter_dimension=1, tiled=True
        ).astype(jnp.float32),
    )
    first_in_grad, first_back_grad, second_in_grad, second_back_grad = (
        parts[0],
        parts[1],
        parts[2],
        parts[3],
    )
    first_gain_grad, second_gain_grad, centroids_grad = (parts[4], parts[5], parts[6])
    return (
        block_out,
        tokens_grad,
        qkv_grad,
        out_grad,
        attn_gain_grad,
        ffn_in_grad,
        ffn_back_grad,
        ffn_gain_grad,
        centroids_grad,
        first_gain_grad,
        first_in_grad,
        first_back_grad,
        second_gain_grad,
        second_in_grad,
        second_back_grad,
    )


def solution(mesh):
    in_specs = (
        P(None, "wide", "section"),
        P(None, "wide", "section"),
        P(None, "wide", None),
        P(),
        P(("section", "wide"), None),
        P(("section", "wide"), None),
        P(("section", "wide")),
        P(("section", "wide"), None),
        P(("section", "wide"), None),
        P(("section", "wide")),
        P("wide", "section"),
        P("wide", "section"),
        P("wide", "section", None),
        P("wide", "section", None),
        P("wide", "section"),
        P("wide", "section", None),
        P("wide", "section", None),
    )
    out_specs = (
        P(None, "wide", "section"),
        P(None, "wide", "section"),
        P(("section", "wide"), None),
        P(("section", "wide"), None),
        P(("section", "wide")),
        P(("section", "wide"), None),
        P(("section", "wide"), None),
        P(("section", "wide")),
        P("wide", "section"),
        P("wide", "section"),
        P("wide", "section", None),
        P("wide", "section", None),
        P("wide", "section"),
        P("wide", "section", None),
        P("wide", "section", None),
    )
    return jax.shard_map(body, mesh=mesh, in_specs=in_specs, out_specs=out_specs, check_vma=False)
```

profile of v0, /device:TPU:12, one launch (start us, length us, event | category | flops | bytes accessed | tf_op | source)
XLA Modules:
  0.0 2870.3 jit_solution(15000168588098860994)
XLA Ops:
  15.7 11.8 all-gather.11.cloned.1.call-done
  37.0 41.1 %all-reduce.28 = (bf16[1024]{0:T(1024)(128)(2,1)S(1)}, bf16[1024]{0:T(1024)(128)(2,1)S(1)}) all-reduce(bf16[1024]{0:T(1024)(128)(2,1)S(1)} %dynamic-update-slice.116, bf16[1024]{0:T(1024)(128)(2,1)S(1)} %dynamic-update-slice.117), channel_id=1, replica_groups=mesh['section'=4,'wide'=8] {'section','wide'}, use_global_device_ids=true, to_apply=%add.23 | all-reduce | flops 2048 | bytes 8192
  94.5 66.3 %all-gather.13.cloned.1.call-done = bf16[1024,3072]{1,0:T(8,128)(2,1)} async-done(((bf16[32,3072]{1,0:T(8,128)(2,1)}), bf16[1024,3072]{1,0:T(8,128)(2,1)}) %all-gather.13.cloned.1.call-update) | async-done | bytes 6291472 | tf_op jit(solution)/shard_map/all_gather | solution.py:216
  160.8 58.2 %all-gather.25.cloned.1.call-done = bf16[1,1024,4096]{2,1,0:T(8,128)(2,1)} async-done(((bf16[1,256,4096]{2,1,0:T(8,128)(2,1)}), bf16[1,1024,4096]{2,1,0:T(8,128)(2,1)}) %all-gather.25.cloned.1.call-update) | async-done | bytes 8388624 | tf_op jit(solution)/shard_map/all_gather | solution.py:229
  219.0 59.7 %all-gather.27.cloned.1.call-done = bf16[1,4096,1024]{2,1,0:T(8,128)(2,1)} async-done(((bf16[1,1024,1024]{2,1,0:T(8,128)(2,1)}), bf16[1,4096,1024]{2,1,0:T(8,128)(2,1)}) %all-gather.27.cloned.1.call-update) | async-done | bytes 8388624 | tf_op jit(solution)/shard_map/all_gather | solution.py:230
  278.7 59.7 %all-gather.21.cloned.1.call-done = bf16[1,1024,4096]{2,1,0:T(8,128)(2,1)} async-done(((bf16[1,256,4096]{2,1,0:T(8,128)(2,1)}), bf16[1,1024,4096]{2,1,0:T(8,128)(2,1)}) %all-gather.21.cloned.1.call-update) | async-done | bytes 8388624 | tf_op jit(solution)/shard_map/all_gather | solution.py:227
  338.4 59.9 %all-gather.23.cloned.1.call-done = bf16[1,4096,1024]{2,1,0:T(8,128)(2,1)} async-done(((bf16[1,1024,1024]{2,1,0:T(8,128)(2,1)}), bf16[1,4096,1024]{2,1,0:T(8,128)(2,1)}) %all-gather.23.cloned.1.call-update) | async-done | bytes 8388624 | tf_op jit(solution)/shard_map/all_gather | solution.py:228
  398.3 80.1 %all-gather.17.cloned.1.call-done = bf16[1024,4096]{1,0:T(8,128)(2,1)} async-done(((bf16[32,4096]{1,0:T(8,128)(2,1)}), bf16[1024,4096]{1,0:T(8,128)(2,1)}) %all-gather.17.cloned.1.call-update) | async-done | bytes 8388624 | tf_op jit(solution)/shard_map/all_gather | solution.py:218
  478.4 78.7 %all-gather.19.cloned.1.call-done = bf16[4096,1024]{1,0:T(8,128)(2,1)} async-done(((bf16[128,1024]{1,0:T(8,128)(2,1)}), bf16[4096,1024]{1,0:T(8,128)(2,1)}) %all-gather.19.cloned.1.call-update) | async-done | bytes 8388624 | tf_op jit(solution)/shard_map/all_gather | solution.py:219
  557.1 29.4 %conditional.10 = (bf16[2,320,1024]{2,1,0:T(8,128)(2,1)}) conditional(s32[]{:T(128)} %clamp.2, (bf16[256,1024]{1,0:T(8,128)(2,1)S(1)}, f32[1024]{0:T(1024)S(1)}, bf16[1024,3072]{1,0:T(8,128)(2,1)}, s32[2]{0:T(128)S(1)}, s32[]{:T(128)}, /*index=5*/bf16[1024,1024]{1,0:T(8,128)(2,1)}) %tuple.729, ...), branch_computations={%region_5.10_spmd, %region_10.13_spmd, %region_13.16_spmd, %region... | conditional | flops 5380506112 | bytes 42384480 | solution.py:300
  599.0 13.1 all-to-all-done.2
  612.1 23.6 conditional.11
  640.9 8.4 scatter_custom_fusion.2
  656.5 9.5 all-to-all-done.4
  666.8 24.1 conditional.12
  725.8 34.2 %conditional.13 = (bf16[2,320,1024]{2,1,0:T(8,128)(2,1)}) conditional(s32[]{:T(128)} %clamp.2, (bf16[256,1024]{1,0:T(8,128)(2,1)S(1)}, f32[1024]{0:T(1024)S(1)}, bf16[1024,3072]{1,0:T(8,128)(2,1)}, s32[2]{0:T(128)}, s32[]{:T(128)}, /*index=5*/bf16[1024,1024]{1,0:T(8,128)(2,1)}) %tuple.343, ...), branch_computations={%region_54.60_spmd, %region_59.63_spmd, %region_62.66_spmd, %regio... | conditional | flops 5381817344 | bytes 40287296 | solution.py:300
  797.6 118.4 %conditional.15 = (bf16[2,320,1024]{2,1,0:T(8,128)(2,1)}, bf16[320,1024]{1,0:T(8,128)(2,1)S(1)}, f32[1024,3072]{1,0:T(8,128)}, f32[1024,1024]{1,0:T(8,128)}, f32...) conditional(s32[]{:T(128)} %clamp.2, ...), branch_computations={%region_92.102_spmd, %region_101.108_spmd, %region_107.114_spmd, %... | conditional | flops 16152529920 | bytes 229231584 | solution.py:438
  828.0 8.2 fusion.438
  836.1 8.3 fusion.435
  948.2 15.4 all-to-all-done.13
  963.7 88.4 %conditional.16 = (bf16[2,320,1024]{2,1,0:T(8,128)(2,1)}, bf16[320,1024]{1,0:T(8,128)(2,1)S(1)}, f32[1024,3072]{1,0:T(8,128)}, f32[1024,1024]{1,0:T(8,128)}, f32...) conditional(s32[]{:T(128)} %clamp.2, ...), branch_computations={%region_124.134_spmd, %region_133.140_spmd, %region_139.146_spmd, ... | conditional | flops 16167474176 | bytes 181521344 | solution.py:438
  1006.8 11.6 add_select_fusion
  1085.5 15.4 all-to-all-done.15
  1100.9 88.7 %conditional.17 = (bf16[2,320,1024]{2,1,0:T(8,128)(2,1)}, bf16[320,1024]{1,0:T(8,128)(2,1)S(1)}, f32[1024,3072]{1,0:T(8,128)}, f32[1024,1024]{1,0:T(8,128)}, f32...) conditional(s32[]{:T(128)} %clamp.2, ...), branch_computations={%region_156.166_spmd, %region_165.172_spmd, %region_171.178_spmd, ... | conditional | flops 16167474176 | bytes 181521344 | solution.py:438
  1136.1 8.2 fusion.725
  1144.3 11.6 add_select_fusion.13
  1223.1 15.4 all-to-all-done.17
  1238.6 95.6 %conditional.18 = (bf16[2,320,1024]{2,1,0:T(8,128)(2,1)}, bf16[320,1024]{1,0:T(8,128)(2,1)S(1)}, f32[1024,3072]{1,0:T(8,128)}, f32[1024,1024]{1,0:T(8,128)}, f32...) conditional(s32[]{:T(128)} %clamp.2, ...), branch_computations={%region_188.198_spmd, %region_197.204_spmd, %region_203.210_spmd, ... | conditional | flops 16167474176 | bytes 181521344 | solution.py:438
  1281.6 11.6 add_select_fusion.26
  1367.6 15.4 all-to-all-done.19
  1383.0 79.9 %conditional.19 = (f32[1024,3072]{1,0:T(8,128)}, f32[1024,1024]{1,0:T(8,128)}, f32[1024]{0:T(1024)}, f32[1024,4096]{1,0:T(8,128)}, f32[4096,1024]{1,0:T(8,128)},...) conditional(s32[]{:T(128)} %clamp.2, ...), branch_computations={%region_220.230_spmd, %region_229.234_spmd, %region_233.238_spmd, ... | conditional | flops 16161574912 | bytes 234842848 | solution.py:438
  1419.6 11.4 add_select_fusion.39
  1467.3 12.2 fusion.1126
  1479.6 12.4 fusion.1127
  1506.5 10.1 all-to-all-done.1
  1525.6 11.1 all-to-all-done.3
  1546.6 10.8 all-to-all-done.5
  1577.2 31.0 %conditional.14 = (bf16[2,320,1024]{2,1,0:T(8,128)(2,1)S(1)}) conditional(s32[]{:T(128)} %clamp.2, (bf16[256,1024]{1,0:T(8,128)(2,1)S(1)}, f32[1024]{0:T(1024)S(1)}, bf16[1024,3072]{1,0:T(8,128)(2,1)}, s32[2]{0:T(128)S(1)}, s32[]{:T(128)}, /*index=5*/bf16[1024,1024]{1,0:T(8,128)(2,1)S(1)}) %tuple.735, ...), branch_computations={%region_71.77_spmd, %region_76.80_spmd, %region_79.83_spmd, %regio... | conditional | flops 5381817344 | bytes 31898662 | solution.py:300
  1628.5 20.0 scatter.243
  1665.1 20.0 scatter.248
  1691.1 20.1 scatter.253
  1717.4 20.0 scatter.290
  1743.5 20.2 scatter.293
  1768.7 47.4 %all-reduce.27 = (f32[1024]{0:T(1024)S(1)}, f32[1024]{0:T(1024)S(1)}) all-reduce(f32[1024]{0:T(1024)} %get-tuple-element.2337, f32[1024]{0:T(1024)} %get-tuple-element.2340), channel_id=4, replica_groups=mesh['section'=4,'wide'=8] {'section','wide'}, use_global_device_ids=true, to_apply=%region_246.248.clone | all-reduce | flops 2048 | bytes 16384
  1842.1 138.3 %reduce-scatter.20.cloned.1.call-done = f32[32,1024]{1,0:T(8,128)} async-done(((f32[1024,1024]{1,0:T(8,128)}), f32[32,1024]{1,0:T(8,128)}) %reduce-scatter.20.cloned.1.call-update) | async-done | bytes 131088 | tf_op jit(solution)/shard_map/reduce_scatter | solution.py:486
  1980.4 163.8 %reduce-scatter.18.cloned.1.call-done = f32[32,3072]{1,0:T(8,128)} async-done(((f32[1024,3072]{1,0:T(8,128)}), f32[32,3072]{1,0:T(8,128)}) %reduce-scatter.18.cloned.1.call-update) | async-done | bytes 393232 | tf_op jit(solution)/shard_map/reduce_scatter | solution.py:485
  2144.2 358.7 %reduce-scatter.22.cloned.1.call-done = f32[32,4096]{1,0:T(8,128)} async-done(((f32[1024,4096]{1,0:T(8,128)}), f32[32,4096]{1,0:T(8,128)}) %reduce-scatter.22.cloned.1.call-update) | async-done | bytes 524304 | tf_op jit(solution)/shard_map/reduce_scatter | solution.py:487
  2503.0 360.3 %reduce-scatter.24.cloned.1.call-done = f32[128,1024]{1,0:T(8,128)} async-done(((f32[4096,1024]{1,0:T(8,128)}), f32[128,1024]{1,0:T(8,128)}) %reduce-scatter.24.cloned.1.call-update) | async-done | bytes 524304 | tf_op jit(solution)/shard_map/reduce_scatter | solution.py:488
  (673 shorter events, 812.6 us)
Async XLA Ops:
  7.2 20.3 all-gather.11.cloned.1.call-start
  7.9 86.6 %all-gather.15.cloned.1.call-start = ((), (), s32[]{:S(2)}) async-start(), calls=%async_computation.34 | async-start | bytes 2162688 | tf_op jit(solution)/shard_map/all_gather | solution.py:217
  8.7 152.1 %all-gather.13.cloned.1.call-start = ((), (), s32[]{:S(2)}) async-start(), calls=%async_computation.33 | async-start | bytes 6488064 | tf_op jit(solution)/shard_map/all_gather | solution.py:216
  9.4 209.6 %all-gather.25.cloned.1.call-start = ((), (), s32[]{:S(2)}) async-start(), calls=%async_computation.39 | async-start | bytes 10485760 | tf_op jit(solution)/shard_map/all_gather | solution.py:229
  10.0 268.7 %all-gather.27.cloned.1.call-start = ((), (), s32[]{:S(2)}) async-start(), calls=%async_computation.40 | async-start | bytes 10485760 | tf_op jit(solution)/shard_map/all_gather | solution.py:230
  10.6 327.8 %all-gather.21.cloned.1.call-start = ((), (), s32[]{:S(2)}) async-start(), calls=%async_computation.37 | async-start | bytes 10485760 | tf_op jit(solution)/shard_map/all_gather | solution.py:227
  11.2 387.1 %all-gather.23.cloned.1.call-start = ((), (), s32[]{:S(2)}) async-start(), calls=%async_computation.38 | async-start | bytes 10485760 | tf_op jit(solution)/shard_map/all_gather | solution.py:228
  12.0 466.4 %all-gather.17.cloned.1.call-start = ((), (), s32[]{:S(2)}) async-start(), calls=%async_computation.35 | async-start | bytes 8650752 | tf_op jit(solution)/shard_map/all_gather | solution.py:218
  12.7 544.4 %all-gather.19.cloned.1.call-start = ((), (), s32[]{:S(2)}) async-start(), calls=%async_computation.36 | async-start | bytes 8650752 | tf_op jit(solution)/shard_map/all_gather | solution.py:219
  30.5 248.2 %all-to-all-start = ((bf16[8,40,1024]{2,1,0:T(8,128)(2,1)}), bf16[8,40,1024]{2,1,0:T(8,128)(2,1)S(1)}, u32[]{:S(2)}, u32[]{:S(2)}) async-start(bf16[8,40,1024]{2,1,0:T(8,128)(2,1)} %bitcast.208), calls=%async_computation | async-start | bytes 1310720 | tf_op jit(solution)/shard_map/all_to_all | solution.py:297
  594.4 17.7 all-to-all-start.2
  649.4 16.5 all-to-all-start.4
  656.5 59.4 %all-gather.29.cloned.1.call-start = ((), (), s32[]{:S(2)}) async-start(), calls=%async_computation.41 | async-start | bytes 1310720 | tf_op jit(solution)/shard_map/all_gather | solution.py:213
  690.9 4.3 collective-permute-start.2
  699.0 20.8 all-to-all-start.6
  719.8 60.5 %all-to-all-start.11 = ((bf16[8,40,1024]{2,1,0:T(8,128)(2,1)}), bf16[8,40,1024]{2,1,0:T(8,128)(2,1)}, u32[]{:S(2)}, u32[]{:S(2)}) async-start(bf16[8,40,1024]{2,1,0:T(8,128)(2,1)} %bitcast.1726), calls=%async_computation.11 | async-start | bytes 1310720 | tf_op jit(solution)/shard_map/all_to_all | solution.py:435
  760.0 16.3 collective-permute-start.3
  780.3 16.4 all-to-all-start.8
  916.8 15.5 all-to-all-start.12
  938.4 25.3 collective-permute-start.4
  942.4 21.3 all-to-all-start.13
  1052.9 16.6 all-to-all-start.14
  1075.7 25.2 collective-permute-start.5
  1079.7 21.3 all-to-all-start.15
  1190.5 16.7 all-to-all-start.16
  1213.3 25.2 collective-permute-start.6
  1217.3 21.3 all-to-all-start.17
  1335.0 16.7 all-to-all-start.18
  1357.8 25.2 collective-permute-start.7
  1361.7 21.3 all-to-all-start.19
  1367.6 449.7 %reduce-scatter.34.cloned.1.call-start = ((), (), s32[]{:S(2)}) async-start(), calls=%async_computation.50 | async-start | bytes 327680
  1464.6 354.2 %reduce-scatter.36.cloned.1.call-start = ((), (), s32[]{:S(2)}) async-start(), calls=%async_computation.51 | async-start | bytes 327680
  1466.3 354.0 %reduce-scatter.38.cloned.1.call-start = ((), (), s32[]{:S(2)}) async-start(), calls=%async_computation.52 | async-start | bytes 327680
  1467.2 355.7 %reduce-scatter.26.cloned.1.call-start = ((), (), s32[]{:S(2)}) async-start(), calls=%async_computation.46 | async-start | bytes 10485760 | tf_op jit(solution)/shard_map/reduce_scatter | solution.py:502
  1479.5 347.6 %reduce-scatter.28.cloned.1.call-start = ((), (), s32[]{:S(2)}) async-start(), calls=%async_computation.47 | async-start | bytes 10485760 | tf_op jit(solution)/shard_map/reduce_scatter | solution.py:508
  1492.0 339.1 %reduce-scatter.30.cloned.1.call-start = ((), (), s32[]{:S(2)}) async-start(), calls=%async_computation.48 | async-start | bytes 10485760 | tf_op jit(solution)/shard_map/reduce_scatter | solution.py:514
  1492.6 345.5 %reduce-scatter.32.cloned.1.call-start = ((), (), s32[]{:S(2)}) async-start(), calls=%async_computation.49 | async-start | bytes 10485760 | tf_op jit(solution)/shard_map/reduce_scatter | solution.py:520
  1493.2 487.3 %reduce-scatter.20.cloned.1.call-start = ((), (), s32[]{:S(2)}) async-start(), calls=%async_computation.43 | async-start | bytes 4325376 | tf_op jit(solution)/shard_map/reduce_scatter | solution.py:486
  1493.8 650.5 %reduce-scatter.18.cloned.1.call-start = ((), (), s32[]{:S(2)}) async-start(), calls=%async_computation.42 | async-start | bytes 12976128 | tf_op jit(solution)/shard_map/reduce_scatter | solution.py:485
  1494.5 1008.5 %reduce-scatter.22.cloned.1.call-start = ((), (), s32[]{:S(2)}) async-start(), calls=%async_computation.44 | async-start | bytes 17301504 | tf_op jit(solution)/shard_map/reduce_scatter | solution.py:487
  1495.1 1368.1 %reduce-scatter.24.cloned.1.call-start = ((), (), s32[]{:S(2)}) async-start(), calls=%async_computation.45 | async-start | bytes 17301504 | tf_op jit(solution)/shard_map/reduce_scatter | solution.py:488
  1497.4 19.2 all-to-all-start.1
  1516.6 20.1 all-to-all-start.3
  1536.7 20.7 all-to-all-start.5
  1557.4 53.9 %all-to-all-start.7 = ((bf16[8,40,1024]{2,1,0:T(8,128)(2,1)}), bf16[8,40,1024]{2,1,0:T(8,128)(2,1)}, u32[]{:S(2)}, u32[]{:S(2)}) async-start(bf16[8,40,1024]{2,1,0:T(8,128)(2,1)} %bitcast.245), calls=%async_computation.7 | async-start | bytes 1310720 | tf_op jit(solution)/shard_map/all_to_all | solution.py:309
  1611.3 39.5 %all-to-all-start.9 = ((bf16[8,40,1024]{2,1,0:T(8,128)(2,1)}), bf16[8,40,1024]{2,1,0:T(8,128)(2,1)S(1)}, u32[]{:S(2)}, u32[]{:S(2)}) async-start(bf16[8,40,1024]{2,1,0:T(8,128)(2,1)} %bitcast.256), calls=%async_computation.9 | async-start | bytes 1310720 | tf_op jit(solution)/shard_map/all_to_all | solution.py:309
  1657.4 106.2 %all-to-all-start.10 = ((bf16[1,2,256,1024]{2,1,0,3:T(2,128)(2,1)}), bf16[1,2,256,1024]{2,1,0,3:T(2,128)(2,1)S(1)}, u32[]{:S(2)}, u32[]{:S(2)}) async-start(bf16[1,2,256,1024]{2,1,0,3:T(2,128)(2,1)} %copy.240), calls=%async_computation.10 | async-start | bytes 2097152 | tf_op jit(solution)/shard_map/all_to_all | solution.py:467
  1763.7 58.1 %all-to-all-start.20 = ((bf16[1,2,256,1024]{2,1,0,3:T(2,128)(2,1)}), bf16[1,2,256,1024]{2,1,0,3:T(2,128)(2,1)S(1)}, u32[]{:S(2)}, u32[]{:S(2)}) async-start(bf16[1,2,256,1024]{2,1,0,3:T(2,128)(2,1)} %scatter.293), calls=%async_computation.20 | async-start | bytes 2097152 | tf_op jit(solution)/shard_map/all_to_all | solution.py:474
  (99 other events, 2282.8 us)
Sparse Core Ops, SparseCore 0:
  9.5 17.9 all-gather.10
  30.5 58.0 all-gather.14
  91.5 69.2 all-gather.12
  162.2 56.7 all-gather.24
  220.4 58.2 all-gather.26
  280.1 58.2 all-gather.20
  340.0 58.2 all-gather.22
  401.2 77.1 all-gather.16
  481.4 75.6 all-gather.18
  693.5 22.2 all-gather.28
  1464.7 20.8 reduce-scatter.33
  1488.0 20.0 reduce-scatter.35
  1510.5 20.0 reduce-scatter.37
  1533.0 71.4 reduce-scatter.25
  1606.9 82.6 reduce-scatter.27
  1692.0 71.3 reduce-scatter.29
  1765.9 72.1 reduce-scatter.31
  1840.7 139.6 reduce-scatter.19
  1987.0 157.1 reduce-scatter.17
  2146.9 355.9 reduce-scatter.21
  2505.8 357.3 reduce-scatter.23
where the time goes:
time: 2900 us; the launch traced here: 2870 us
  waiting for transfers between devices  1660 us (57%)
  matrix products  340 us (12%)
  local copies, waits for them, and re-layouts  317 us (11%)
  other arithmetic  149 us (5%)
  starting transfers between devices  146 us (5%)
  loops' own time  137 us (5%)
  blocking collectives  104 us (4%)
    reduce_scatter x1, waiting for transfers between devices, body(): lax.psum_scatter(totals[4], ('section', 'wide'), scatter_dimension=0, til...  360 us
    reduce_scatter x1, waiting for transfers between devices, body(): lax.psum_scatter(totals[3], ('section', 'wide'), scatter_dimension=0, til...  359 us
    reduce_scatter x1, waiting for transfers between devices, body(): lax.psum_scatter(totals[0], ('section', 'wide'), scatter_dimension=0, til...  164 us
    reduce_scatter x1, waiting for transfers between devices, body(): lax.psum_scatter(totals[1], ('section', 'wide'), scatter_dimension=0, til...  138 us
    another operation x5, loops' own time, body(): lax.switch(section_id, [back_attention, back_dense, back_first, back_seco...  109 us
    scatter x5, local copies, waits for them, and re-layouts, body(): grad_tokens.at[picked]  100 us
    unnamed x2, blocking collectives  88.5 us
    all_gather x1, waiting for transfers between devices, body(): lax.all_gather(ffn_in, ('section', 'wide'), axis=0, tiled=True)  80.1 us
  transfers between devices with their start and end apart: 50, of which 30 were waited for; matrix products, arithmetic and copies ran while one was open for 11% of the time, Pallas kernels for 0%

commit v1 on v0

v1 whole, which is shorter than its diff:
```python
import jax
import jax.numpy as jnp
from jax import lax
from jax.sharding import PartitionSpec as P

HEAD_SIZE = 64
F32 = jnp.float32
BF16 = jnp.bfloat16


def dot(left, right):
    return jnp.dot(left, right, preferred_element_type=F32)


def dot_nt(left, right):
    return lax.dot_general(left, right, (((1,), (1,)), ((), ())), preferred_element_type=F32)


def dot_tn(left, right):
    return lax.dot_general(left, right, (((0,), (0,)), ((), ())), preferred_element_type=F32)


def gelu_value(v):
    return 0.5 * v * (1.0 + lax.erf(v * 0.7071067811865476))


def gelu_slope(v):
    return (
        0.5 * (1.0 + lax.erf(v * 0.7071067811865476))
        + v * jnp.exp(-0.5 * v * v) * 0.3989422804014327
    )


def unit_norm(v):
    centred = v - jnp.mean(v, axis=-1, keepdims=True)
    scale = lax.rsqrt(jnp.mean(centred * centred, axis=-1, keepdims=True) + 1e-05)
    return centred * scale, scale


def reduce_quarters(part):
    rows, width = part.shape
    return lax.psum_scatter(part.astype(BF16), "section", scatter_dimension=1, tiled=True).astype(F32)


def gather_quarters(quarter):
    return lax.all_gather(quarter, "section", axis=1, tiled=True)


def section_sum(v):
    return lax.psum(v, "section")


def wide_exchange(slots):
    return lax.all_to_all(slots, "wide", split_axis=0, concat_axis=0, tiled=True)


def attention_probs(queries, keys, lengths):
    rows = queries.shape[2]
    raw = jnp.einsum("mhqd,mhkd->mhqk", queries, keys, preferred_element_type=F32)
    pos = jnp.arange(rows, dtype=jnp.int32)
    same = pos[None, :, None] // lengths[:, None, None] == pos[None, None, :] // lengths[:, None, None]
    allowed = (pos[:, None] >= pos[None, :])[None] & same
    scores = jnp.where(allowed[:, None], raw * HEAD_SIZE ** (-0.5), -1e30)
    highest = jnp.max(scores, axis=-1, keepdims=True)
    expo = jnp.exp(scores - highest)
    return expo / jnp.sum(expo, axis=-1, keepdims=True)


def body(
    tokens_in,
    cotangent,
    routes,
    seq_lengths,
    qkv_weight,
    out_weight,
    attn_gain,
    ffn_in,
    ffn_back,
    ffn_gain,
    centroids,
    first_gain,
    first_in,
    first_back,
    second_gain,
    second_in,
    second_back,
):
    sections = lax.axis_size("section")
    wide = lax.axis_size("wide")
    section_id = lax.axis_index("section")
    wide_id = lax.axis_index("wide")
    micro, rows, quarter = tokens_in.shape
    width = quarter * sections
    cap = 5 * rows // (4 * wide)
    tok_rows = micro * rows
    hid = first_back.shape[1]
    small = qkv_weight.shape[0]
    qkv_cols = qkv_weight.shape[1] // sections

    qkv_cut = (
        qkv_weight.reshape(small, 3, sections, quarter).transpose(2, 0, 1, 3).reshape(sections, small, qkv_cols)
    )
    in_cut = ffn_in.reshape(small, sections, hid).transpose(1, 0, 2)
    cut = lax.all_to_all(jnp.concatenate([qkv_cut, in_cut], axis=2), "section", split_axis=0, concat_axis=0, tiled=True)

    def whole_rows(piece):
        got = lax.all_gather(piece, "wide", axis=0, tiled=False)
        return got.transpose(1, 0, 2, 3).reshape(width, piece.shape[2])

    vectors = jnp.concatenate([first_gain[0], second_gain[0], centroids[0], attn_gain, ffn_gain])
    vectors = jnp.pad(vectors, (0, 1024 - vectors.shape[0])).reshape(8, 128)
    vectors = lax.all_gather(vectors, ("section", "wide"), axis=0, tiled=False).reshape(sections, wide, 1024)
    own = lax.dynamic_index_in_dim(vectors, wide_id, axis=1, keepdims=False).astype(F32)
    gain_first = own[:, :quarter].reshape(1, width)
    gain_second = own[:, quarter : 2 * quarter].reshape(1, width)
    centre = own[:, 2 * quarter : 3 * quarter].reshape(1, width)
    gain_attn = vectors[:, :, 3 * quarter : 3 * quarter + small].reshape(1, width).astype(F32)
    gain_ffn = vectors[:, :, 3 * quarter + small : 3 * quarter + 2 * small].reshape(1, width).astype(F32)
    own_quarter = lambda v: lax.dynamic_slice_in_dim(v, section_id * quarter, quarter, axis=1)

    tokens_q = tokens_in.reshape(tok_rows, quarter)
    tokens = gather_quarters(tokens_q)
    qkv_w = whole_rows(cut[:, :, :qkv_cols])
    out_w = lax.all_gather(out_weight, "wide", axis=0, tiled=True)
    in_w = whole_rows(cut[:, :, qkv_cols:])
    back_w = lax.all_gather(ffn_back, "wide", axis=0, tiled=True)

    def slice_in(weight):
        pieces = weight[0].reshape(quarter, sections, hid).transpose(1, 0, 2)
        return lax.all_to_all(pieces, "section", split_axis=0, concat_axis=0, tiled=True).reshape(width, hid)

    first_w = slice_in(first_in)
    second_w = slice_in(second_in)
    first_b = first_back[0]
    second_b = second_back[0]

    experts = jnp.arange(wide, dtype=jnp.int32)
    choose = (routes == experts).astype(jnp.int32)
    upto = (jnp.arange(rows)[:, None] >= jnp.arange(rows)[None, :]).astype(BF16)
    ranking = jnp.einsum("rk,mke->mre", upto, choose.astype(BF16), preferred_element_type=F32).astype(jnp.int32) - 1
    slot_of = routes[:, :, 0] * cap + jnp.sum(ranking * choose, axis=2)
    onehot = (jnp.arange(wide * cap, dtype=jnp.int32)[None, :, None] == slot_of[:, None, :]).astype(BF16)

    def to_experts(rows_q):
        packed = jnp.einsum("msr,mrd->msd", onehot, rows_q.reshape(micro, rows, quarter), preferred_element_type=F32)
        packed = packed.astype(BF16).reshape(micro, wide, cap, quarter).transpose(1, 0, 2, 3)
        return wide_exchange(packed.reshape(wide, micro * cap, quarter)).reshape(wide * micro * cap, quarter)

    def to_tokens(slots_q):
        back = wide_exchange(slots_q.reshape(wide, micro * cap, quarter))
        back = back.reshape(wide, micro, cap, quarter).transpose(1, 0, 2, 3).reshape(micro, wide * cap, quarter)
        got = jnp.einsum("msr,msd->mrd", onehot, back, preferred_element_type=F32)
        return got.astype(BF16).reshape(tok_rows, quarter)

    unit_a, scale_a = unit_norm(tokens.astype(F32))
    normed_a = (unit_a * gain_attn).astype(BF16)
    packed = dot(normed_a, qkv_w).astype(BF16)
    heads = quarter // HEAD_SIZE

    def by_head(v):
        return v.reshape(micro, rows, heads, HEAD_SIZE).transpose(0, 2, 1, 3)

    def from_head(v):
        return v.transpose(0, 2, 1, 3).reshape(tok_rows, quarter)

    queries, keys, values = (by_head(packed[:, i * quarter : (i + 1) * quarter]) for i in range(3))
    probs = attention_probs(queries, keys, seq_lengths)
    probs_b = probs.astype(BF16)
    mixed = from_head(
        jnp.einsum("mhqk,mhkd->mhqd", probs_b, values, preferred_element_type=F32).astype(BF16)
    )
    attended_q = (tokens_q.astype(F32) + reduce_quarters(dot(mixed, out_w))).astype(BF16)
    attended = gather_quarters(attended_q)

    def branch(v, w_in, w_back, gain):
        unit, scale = unit_norm(v.astype(F32))
        normed = (unit * gain).astype(BF16)
        pre = dot(normed, w_in)
        hidden = gelu_value(pre).astype(BF16)
        return (normed, unit, scale, pre, hidden), dot(hidden, w_back)

    def branch_back(grad, saved, w_in, w_back, gain):
        normed, unit, scale, pre, hidden = saved
        d_back = dot_tn(hidden, grad)
        d_pre = (dot_nt(grad, w_back) * gelu_slope(pre)).astype(BF16)
        d_in = dot_tn(normed, d_pre)
        return d_in, d_back, norm_back(dot_nt(d_pre, w_in), unit, scale, gain)

    def norm_back(d_part, unit, scale, gain):
        d_unit = d_part * gain
        sums = section_sum(
            jnp.stack([jnp.sum(d_unit, axis=1), jnp.sum(d_unit * unit, axis=1)])
        ) / width
        d_q = reduce_quarters(d_part)
        unit_q = own_quarter(unit)
        d_rows = scale * (d_q * own_quarter(gain) - sums[0][:, None] - unit_q * sums[1][:, None])
        return d_rows, jnp.sum(d_q * unit_q, axis=0)

    saved_d, part = branch(attended, in_w, back_w, gain_ffn)
    fed_q = (attended_q.astype(F32) + reduce_quarters(part)).astype(BF16)
    routed_q = to_experts(fed_q)
    routed = gather_quarters(routed_q)
    d_mixed_q = to_experts(cotangent.reshape(tok_rows, quarter))
    d_mixed = gather_quarters(d_mixed_q).astype(F32)
    saved_1, part = branch(routed, first_w, first_b, gain_first)
    first_q = (routed_q.astype(F32) + reduce_quarters(part)).astype(BF16)
    first = gather_quarters(first_q)
    saved_2, part = branch(first, second_w, second_b, gain_second)
    gate = jax.nn.sigmoid(jnp.sum(routed.astype(F32) * centre, axis=-1, keepdims=True))
    second_q = first_q.astype(F32) + reduce_quarters(part)
    mixed_q = routed_q.astype(F32) + gate * second_q
    block_out = to_tokens(mixed_q.astype(BF16)).reshape(micro, rows, quarter)

    d_second = gate * d_mixed
    d_second_q = gate * d_mixed_q.astype(F32)
    d_logit = section_sum(jnp.sum(d_mixed_q.astype(F32) * second_q, axis=-1))[:, None] * gate * (1.0 - gate)
    centroids_grad = jnp.sum(d_logit * routed_q.astype(F32), axis=0)[None]
    d_gated_q = (d_mixed_q.astype(F32) + d_logit * own_quarter(centre)).astype(BF16)
    d_second_in, d_second_back, (norm_q, second_gain_grad) = branch_back(
        d_second.astype(BF16), saved_2, second_w, second_b, gain_second
    )
    d_first_q = (d_second_q + norm_q).astype(BF16)
    d_first_in, d_first_back, (norm_q, first_gain_grad) = branch_back(
        gather_quarters(d_first_q), saved_1, first_w, first_b, gain_first
    )
    d_routed_q = (d_first_q.astype(F32) + norm_q + d_gated_q.astype(F32)).astype(BF16)
    d_fed_q = to_tokens(d_routed_q)
    d_in, d_back, (norm_q, d_gain_ffn) = branch_back(gather_quarters(d_fed_q), saved_d, in_w, back_w, gain_ffn)
    d_attended_q = (d_fed_q.astype(F32) + norm_q).astype(BF16)
    d_attended = gather_quarters(d_attended_q)
    d_out = dot_tn(mixed, d_attended)
    d_mix = by_head(dot_nt(d_attended, out_w).astype(BF16))
    d_probs = jnp.einsum("mhqd,mhkd->mhqk", d_mix, values, preferred_element_type=F32)
    delta = jnp.sum(probs * d_probs, axis=-1, keepdims=True)
    d_scores = (probs * (d_probs - delta) * HEAD_SIZE ** (-0.5)).astype(BF16)
    d_queries = jnp.einsum("mhqk,mhkd->mhqd", d_scores, keys, preferred_element_type=F32)
    d_keys = jnp.einsum("mhqk,mhqd->mhkd", d_scores, queries, preferred_element_type=F32)
    d_values = jnp.einsum("mhqk,mhqd->mhkd", probs_b, d_mix, preferred_element_type=F32)
    d_packed = jnp.concatenate([from_head(v) for v in (d_queries, d_keys, d_values)], axis=1).astype(BF16)
    d_qkv = dot_tn(normed_a, d_packed)
    norm_q, d_gain_attn = norm_back(dot_nt(d_packed, qkv_w), unit_a, scale_a, gain_attn)
    tokens_grad = (d_attended_q.astype(F32) + norm_q).reshape(micro, rows, quarter)

    def own_in(grad):
        pieces = grad.astype(BF16).reshape(sections, quarter, hid)
        got = lax.all_to_all(pieces, "section", split_axis=0, concat_axis=0, tiled=True)
        return got.transpose(1, 0, 2).reshape(1, quarter, sections * hid).astype(F32)

    def sum_rows(grad):
        pieces = grad.astype(BF16).reshape(sections, wide, small, grad.shape[1]).transpose(1, 0, 2, 3)
        return lax.psum_scatter(pieces, "wide", scatter_dimension=0, tiled=True)[0]

    d_cut = jnp.concatenate([sum_rows(d_qkv), sum_rows(d_in)], axis=2)
    d_cut = lax.all_to_all(d_cut, "section", split_axis=0, concat_axis=0, tiled=True).astype(F32)
    qkv_grad = d_cut[:, :, :qkv_cols].reshape(sections, small, 3, quarter).transpose(1, 2, 0, 3)
    qkv_grad = qkv_grad.reshape(small, 3 * width)
    ffn_in_grad = d_cut[:, :, qkv_cols:].transpose(1, 0, 2).reshape(small, sections * hid)
    out_grad = lax.psum_scatter(d_out.astype(BF16), "wide", scatter_dimension=0, tiled=True).astype(F32)
    ffn_back_grad = lax.psum_scatter(d_back.astype(BF16), "wide", scatter_dimension=0, tiled=True).astype(F32)
    d_gains = jnp.stack([d_gain_attn.reshape(wide, small), d_gain_ffn.reshape(wide, small)], axis=1)
    d_gains = jnp.sum(lax.all_to_all(d_gains, "wide", split_axis=0, concat_axis=0, tiled=True), axis=0)
    return (
        block_out,
        tokens_grad,
        qkv_grad,
        out_grad,
        d_gains[0],
        ffn_in_grad,
        ffn_back_grad,
        d_gains[1],
        centroids_grad,
        first_gain_grad[None],
        own_in(d_first_in),
        d_first_back[None],
        second_gain_grad[None],
        own_in(d_second_in),
        d_second_back[None],
    )


def solution(mesh):
    dense = P(("section", "wide"), None)
    dense_gain = P(("section", "wide"))
    tokens = P(None, "wide", "section")
    gain = P("wide", "section")
    expert = P("wide", "section", None)
    in_specs = (
        (tokens, tokens, P(None, "wide", None), P(), dense, dense, dense_gain, dense, dense, dense_gain)
        + (gain, gain, expert, expert, gain, expert, expert)
    )
    out_specs = (
        (tokens, tokens, dense, dense, dense_gain, dense, dense, dense_gain)
        + (gain, gain, expert, expert, gain, expert, expert)
    )
    return jax.shard_map(body, mesh=mesh, in_specs=in_specs, out_specs=out_specs, check_vma=False)
```

time: 2900 us -> 1030 us (0.36)
  waiting for transfers between devices: 1660 us -> 584 us
  local copies, waits for them, and re-layouts: 317 us -> 64.1 us
  matrix products: 340 us -> 108 us
  loops' own time: 137 us -> 0 us
  other arithmetic: 149 us -> 34.2 us
  starting transfers between devices: 146 us -> 39.9 us
  blocking collectives: 104 us -> 172 us
    reduce_scatter x8 -> x12, waiting for transfers between devices: 1020 us -> 334 us  [the longest x8 164 us: reduce_quarters(): lax.psum_scatter(part.astype(BF16), 'section', scatter_dimension=1, tiled...]
    all_gather x10 -> x11, waiting for transfers between devices: 476 us -> 157 us  [the longest x8 65.9 us: gather_quarters(): return lax.all_gather(quarter, 'section', axis=1, tiled=True)]
    dot_general x65 -> x34, matrix products: 292 us -> 104 us  [the longest x8 29.6 us: dot_tn(): lax.dot_general(left, right, (((0,), (0,)), ((), ())), preferred_element_...]
    scatter x22 -> x0, local copies, waits for them, and re-layouts: 139 us -> none  [the longest x5 100 us: body(): grad_tokens.at[picked]]
    another operation x10 -> x0, loops' own time: 137 us -> none  [the longest x5 109 us: body(): lax.switch(section_id, [back_attention, back_dense, back_first, back_seco...]
    all_to_all x21 -> x8, starting transfers between devices: 129 us -> 38.2 us  [the longest x2 12.3 us: wide_exchange(): lax.all_to_all(slots, 'wide', split_axis=0, concat_axis=0, tiled=True)]
    unnamed x2 -> x0, blocking collectives: 88.5 us -> none
    all_gather x3 -> x2, blocking collectives: 15.2 us -> 93.9 us  [the longest x1 62 us: body(): lax.all_gather(vectors, ('section', 'wide'), axis=0, tiled=False)]
  transfers between devices with their start and end apart: 50 -> 31, of which waited for: 30 -> 20; matrix products, arithmetic and copies ran while one was open for 11% -> 11% of each run, Pallas kernels for 0% -> 0%
where the time goes in v1:
time: 1030 us; the launch traced here: 1020 us
  waiting for transfers between devices  584 us (57%)
  blocking collectives  172 us (17%)
  matrix products  108 us (10%)
  local copies, waits for them, and re-layouts  64.1 us (6%)
  starting transfers between devices  39.9 us (4%)
  other arithmetic  34.2 us (3%)
  between operations  15.7 us (2%)
    reduce_scatter x8, waiting for transfers between devices, reduce_quarters(): lax.psum_scatter(part.astype(BF16), 'section', scatter_dimension=1, tiled...  164 us
    all_gather x8, waiting for transfers between devices, gather_quarters(): return lax.all_gather(quarter, 'section', axis=1, tiled=True)  65.9 us
    reduce_scatter x1, waiting for transfers between devices, body(): lax.psum_scatter(d_out.astype(BF16), 'wide', scatter_dimension=0, tiled=T...  64.1 us
    all_gather x1, blocking collectives, body(): lax.all_gather(vectors, ('section', 'wide'), axis=0, tiled=False)  62 us
    all_to_all x2, waiting for transfers between devices, slice_in(): lax.all_to_all(pieces, 'section', split_axis=0, concat_axis=0, tiled=True)  61.6 us
    reduce_scatter x1, waiting for transfers between devices, body(): lax.psum_scatter(d_back.astype(BF16), 'wide', scatter_dimension=0, tiled=...  54.1 us
    reduce_scatter x2, waiting for transfers between devices, sum_rows(): return lax.psum_scatter(pieces, 'wide', scatter_dimension=0, tiled=True)[0]  52 us
    all_gather x2, waiting for transfers between devices, whole_rows(): got = lax.all_gather(piece, 'wide', axis=0, tiled=False)  48.4 us
  transfers between devices with their start and end apart: 31, of which 20 were waited for; matrix products, arithmetic and copies ran while one was open for 11% of the time, Pallas kernels for 0%

profile of v1, /device:TPU:12, one launch (start us, length us, event | category | flops | bytes accessed | tf_op | source)
XLA Modules:
  0.0 1017.0 jit_solution(10279651688977056723)
XLA Ops:
  11.0 12.6 %all_to_all.55 = bf16[4,32,1792]{2,1,0:T(8,128)(2,1)S(1)} all-to-all(bf16[4,32,1792]{2,1,0:T(8,128)(2,1)S(1)} %copy.225), channel_id=1, replica_groups=mesh['section'=4,'wide'=8] {'section'}, dimensions={0} | all-to-all | bytes 917504 | tf_op jit(solution)/shard_map/all_to_all | solution.py:104
  25.4 62.0 %all_gather.46 = bf16[32,8,128]{2,1,0:T(8,128)(2,1)S(1)} all-gather(bf16[1,8,128]{2,1,0:T(8,128)(2,1)S(1)} %pad_bitcast_fusion), channel_id=1, replica_groups=mesh['section'=4,'wide'=8] {'section','wide'}, dimensions={0}, use_global_device_ids=true | all-gather | bytes 67584 | tf_op jit(solution)/shard_map/all_gather | solution.py:112
  88.8 31.9 %all_gather.49 = bf16[256,1024]{1,0:T(8,128)(2,1)} all-gather(bf16[32,1024]{1,0:T(8,128)(2,1)S(1)} %copy-done.40), channel_id=1, replica_groups=mesh['section'=4,'wide'=8] {'wide'}, dimensions={0}, use_global_device_ids=true | all-gather | bytes 589824 | tf_op jit(solution)/shard_map/all_gather | solution.py:124
  136.1 28.8 %reduce-scatter.13.cloned.1.call-done = bf16[512,256]{1,0:T(8,128)(2,1)} async-done(((bf16[512,1024]{1,0:T(8,128)(2,1)}), bf16[512,256]{1,0:T(8,128)(2,1)}) %reduce-scatter.13.cloned.1.call-update) | async-done | bytes 262160 | tf_op jit(solution)/shard_map/reduce_scatter | solution.py:42
  167.3 48.3 %all-gather.34.cloned.1.call-done = bf16[32,32,1024]{2,1,0:T(8,128)(2,1)} async-done(((bf16[4,32,1024]{2,1,0:T(8,128)(2,1)}), bf16[32,32,1024]{2,1,0:T(8,128)(2,1)}) %all-gather.34.cloned.1.call-update) | async-done | bytes 2097168 | tf_op jit(solution)/shard_map/all_gather | solution.py:107
  218.9 15.0 %all-gather.16.cloned.1.call-done = bf16[512,1024]{1,0:T(8,128)(2,1)} async-done(((bf16[512,256]{1,0:T(8,128)(2,1)}), bf16[512,1024]{1,0:T(8,128)(2,1)}) %all-gather.16.cloned.1.call-update) | async-done | bytes 1048592 | tf_op jit(solution)/shard_map/all_gather | solution.py:46
  237.1 4.6 multiply_convert_fusion.6
  241.7 42.5 %all-gather.18.cloned.1.call-done = bf16[1024,1024]{1,0:T(8,128)(2,1)} async-done(((bf16[128,1024]{1,0:T(8,128)(2,1)}), bf16[1024,1024]{1,0:T(8,128)(2,1)}) %all-gather.18.cloned.1.call-update) | async-done | bytes 2097168 | tf_op jit(solution)/shard_map/all_gather | solution.py:126
  288.6 24.1 %reduce-scatter.15.cloned.1.call-done = bf16[512,256]{1,0:T(8,128)(2,1)} async-done(((bf16[512,1024]{1,0:T(8,128)(2,1)}), bf16[512,256]{1,0:T(8,128)(2,1)}) %reduce-scatter.15.cloned.1.call-update) | async-done | bytes 262160 | tf_op jit(solution)/shard_map/reduce_scatter | solution.py:42
  314.0 14.5 %all_to_all.56 = bf16[8,80,256]{2,1,0:T(8,128)(2,1)} all-to-all(bf16[8,80,256]{2,1,0:T(8,128)(2,1)S(1)} %bitcast.280), channel_id=1, replica_groups=mesh['section'=4,'wide'=8] {'wide'}, dimensions={0} | all-to-all | bytes 655360 | tf_op jit(solution)/shard_map/all_to_all | solution.py:54
  332.6 4.5 all-to-all-start.2
  337.4 29.7 %all-to-all-done.2 = bf16[4,256,1024]{1,2,0:T(8,128)(2,1)} async-done(((bf16[4,256,1024]{1,2,0:T(8,128)(2,1)}), bf16[4,256,1024]{1,2,0:T(8,128)(2,1)}, u32[]{:S(2)}, u32[]{:S(2)}) %all-to-all-start.2) | async-done | bytes 2097184 | tf_op jit(solution)/shard_map/all_to_all | solution.py:130
  373.5 4.9 multiply_convert_fusion.3
  382.2 26.6 %reduce-scatter.17.cloned.1.call-done = bf16[640,256]{1,0:T(8,128)(2,1)} async-done(((bf16[640,1024]{1,0:T(8,128)(2,1)}), bf16[640,256]{1,0:T(8,128)(2,1)}) %reduce-scatter.17.cloned.1.call-update) | async-done | bytes 327696 | tf_op jit(solution)/shard_map/reduce_scatter | solution.py:42
  411.6 6.1 all-to-all-start.5
  426.2 4.4 all-to-all-start.3
  431.4 32.0 %all-to-all-done.3 = bf16[4,256,1024]{1,2,0:T(8,128)(2,1)} async-done(((bf16[4,256,1024]{1,2,0:T(8,128)(2,1)}), bf16[4,256,1024]{1,2,0:T(8,128)(2,1)}, u32[]{:S(2)}, u32[]{:S(2)}) %all-to-all-start.3) | async-done | bytes 2097184 | tf_op jit(solution)/shard_map/all_to_all | solution.py:130
  469.6 5.0 multiply_convert_fusion.1
  474.6 4.3 fusion.14
  486.9 5.9 psum.35
  492.8 16.4 %reduce-scatter.21.cloned.1.call-done = bf16[640,256]{1,0:T(8,128)(2,1)} async-done(((bf16[640,1024]{1,0:T(8,128)(2,1)}), bf16[640,256]{1,0:T(8,128)(2,1)}) %reduce-scatter.21.cloned.1.call-update) | async-done | bytes 327696 | tf_op jit(solution)/shard_map/reduce_scatter | solution.py:42
  509.2 29.0 %reduce-scatter.19.cloned.1.call-done = bf16[640,256]{1,0:T(8,128)(2,1)} async-done(((bf16[640,1024]{1,0:T(8,128)(2,1)}), bf16[640,256]{1,0:T(8,128)(2,1)}) %reduce-scatter.19.cloned.1.call-update) | async-done | bytes 327696 | tf_op jit(solution)/shard_map/reduce_scatter | solution.py:42
  542.0 18.0 %all-gather.26.cloned.1.call-done = bf16[640,1024]{1,0:T(8,128)(2,1)} async-done(((bf16[640,256]{1,0:T(8,128)(2,1)}), bf16[640,1024]{1,0:T(8,128)(2,1)}) %all-gather.26.cloned.1.call-update) | async-done | bytes 1310736 | tf_op jit(solution)/shard_map/all_gather | solution.py:46
  560.0 5.1 fusion.20
  569.0 6.3 all-reduce.1
  575.3 20.1 %reduce-scatter.23.cloned.1.call-done = bf16[640,256]{1,0:T(8,128)(2,1)} async-done(((bf16[640,1024]{1,0:T(8,128)(2,1)}), bf16[640,256]{1,0:T(8,128)(2,1)}) %reduce-scatter.23.cloned.1.call-update) | async-done | bytes 327696 | tf_op jit(solution)/shard_map/reduce_scatter | solution.py:42
  597.6 14.4 %all_to_all.57 = bf16[8,80,256]{2,1,0:T(8,128)(2,1)S(1)} all-to-all(bf16[8,80,256]{2,1,0:T(8,128)(2,1)S(1)} %bitcast.277), channel_id=1, replica_groups=mesh['section'=4,'wide'=8] {'wide'}, dimensions={0} | all-to-all | bytes 655360 | tf_op jit(solution)/shard_map/all_to_all | solution.py:54
  613.2 16.1 %all-gather.28.cloned.1.call-done = bf16[512,1024]{1,0:T(8,128)(2,1)} async-done(((bf16[512,256]{1,0:T(8,128)(2,1)}), bf16[512,1024]{1,0:T(8,128)(2,1)}) %all-gather.28.cloned.1.call-update) | async-done | bytes 1048592 | tf_op jit(solution)/shard_map/all_gather | solution.py:46
  629.3 4.4 fusion.32
  637.1 6.1 psum.38
  643.2 18.7 %reduce-scatter.25.cloned.1.call-done = bf16[512,256]{1,0:T(8,128)(2,1)} async-done(((bf16[512,1024]{1,0:T(8,128)(2,1)}), bf16[512,256]{1,0:T(8,128)(2,1)}) %reduce-scatter.25.cloned.1.call-update) | async-done | bytes 262160 | tf_op jit(solution)/shard_map/reduce_scatter | solution.py:42
  664.3 16.8 %all-gather.30.cloned.1.call-done = bf16[512,1024]{1,0:T(8,128)(2,1)} async-done(((bf16[512,256]{1,0:T(8,128)(2,1)}), bf16[512,1024]{1,0:T(8,128)(2,1)}) %all-gather.30.cloned.1.call-update) | async-done | bytes 1048592 | tf_op jit(solution)/shard_map/all_gather | solution.py:46
  689.1 4.9 fusion.67
  713.9 4.7 convolution_convert_fusion.2
  722.2 25.5 %all-to-all-done.10 = bf16[4,256,1024]{2,1,0:T(8,128)(2,1)S(1)} async-done(((bf16[4,256,1024]{2,1,0:T(8,128)(2,1)}), bf16[4,256,1024]{2,1,0:T(8,128)(2,1)S(1)}, u32[]{:S(2)}, u32[]{:S(2)}) %all-to-all-start.10) | async-done | bytes 2097184 | tf_op jit(solution)/shard_map/all_to_all | solution.py:246
  747.8 6.3 all-to-all-start.4
  754.1 5.6 convolution_bitcast_fusion
  760.2 4.7 copy.259
  764.9 6.2 reshape.549
  772.3 4.8 convolution_convert_fusion.3
  781.5 5.6 convolution_bitcast_fusion.1
  789.6 18.2 %psum.39 = f32[2,512]{1,0:T(2,128)S(1)} all-reduce(f32[2,512]{1,0:T(2,128)S(1)} %pad_maximum_fusion.6), channel_id=1, replica_groups=mesh['section'=4,'wide'=8] {'section'}, use_global_device_ids=true, to_apply=%region_34.35 | all-reduce | flops 1024 | bytes 8192 | tf_op jit(solution)/shard_map/psum | solution.py:50
  810.8 6.0 all-to-all-start.8
  816.8 52.0 %reduce-scatter.29.cloned.1.call-done = bf16[1,4,32,768]{3,2,1,0:T(8,128)(2,1)} async-done(((bf16[8,4,32,768]{3,2,1,0:T(8,128)(2,1)}), bf16[1,4,32,768]{3,2,1,0:T(8,128)(2,1)}) %reduce-scatter.29.cloned.1.call-update) | async-done | bytes 196624 | tf_op jit(solution)/shard_map/reduce_scatter | solution.py:251
  874.8 4.7 copy.258
  879.5 6.1 reshape.548
  885.5 54.1 %reduce-scatter.35.cloned.1.call-done = bf16[128,1024]{1,0:T(8,128)(2,1)} async-done(((bf16[1024,1024]{1,0:T(8,128)(2,1)}), bf16[128,1024]{1,0:T(8,128)(2,1)}) %reduce-scatter.35.cloned.1.call-update) | async-done | bytes 262160 | tf_op jit(solution)/shard_map/reduce_scatter | solution.py:259
  941.5 64.1 %reduce-scatter.33.cloned.1.call-done = bf16[32,1024]{1,0:T(8,128)(2,1)} async-done(((bf16[256,1024]{1,0:T(8,128)(2,1)}), bf16[32,1024]{1,0:T(8,128)(2,1)}) %reduce-scatter.33.cloned.1.call-update) | async-done | bytes 65552 | tf_op jit(solution)/shard_map/reduce_scatter | solution.py:258
  (328 shorter events, 149.1 us)
Async XLA Ops:
  7.2 467.4 %copy-start = (bf16[1,1024,1024]{2,1,0:T(8,128)(2,1)S(1)}, bf16[1,1024,1024]{2,1,0:T(8,128)(2,1)}, u32[]{:S(2)}) copy-start(bf16[1,1024,1024]{2,1,0:T(8,128)(2,1)} %param.33) | copy-start | bytes 6291460
  7.2 113.5 %all-gather.14.cloned.1.call-start = ((), (), s32[]{:S(2)}) async-start(), calls=%async_computation.23 | async-start | bytes 1310720 | tf_op jit(solution)/shard_map/all_gather | solution.py:46
  7.9 116.0 %all-gather.32.cloned.1.call-start = ((), (), s32[]{:S(2)}) async-start(), calls=%async_computation.44 | async-start | bytes 1769472 | tf_op jit(solution)/shard_map/all_gather | solution.py:107
  10.3 14.9 %copy-start.44 = (bf16[1,256]{1,0:T(2,128)(2,1)S(1)}, bf16[1,256]{1,0:T(2,128)(2,1)}, u32[]{:S(2)}) copy-start(bf16[1,256]{1,0:T(2,128)(2,1)} %param.27) | copy-start | bytes 1540
  10.3 14.9 %copy-start.45 = (bf16[32]{0:T(256)(128)(2,1)S(1)}, bf16[32]{0:T(256)(128)(2,1)}, u32[]{:S(2)}) copy-start(bf16[32]{0:T(256)(128)(2,1)} %param.23) | copy-start | bytes 196
  10.3 14.9 %copy-start.46 = (bf16[32]{0:T(256)(128)(2,1)S(1)}, bf16[32]{0:T(256)(128)(2,1)}, u32[]{:S(2)}) copy-start(bf16[32]{0:T(256)(128)(2,1)} %param.26) | copy-start | bytes 196
  10.6 77.0 %copy-start.47 = (s32[2]{0:T(128)S(1)}, s32[2]{0:T(128)}, u32[]{:S(2)}) copy-start(s32[2]{0:T(128)} %param.20) | copy-start | bytes 28
  10.8 78.0 %copy-start.40 = (bf16[32,1024]{1,0:T(8,128)(2,1)S(1)}, bf16[32,1024]{1,0:T(8,128)(2,1)}, u32[]{:S(2)}) copy-start(bf16[32,1024]{1,0:T(8,128)(2,1)} %param.22) | copy-start | bytes 196612
  25.1 139.8 %reduce-scatter.13.cloned.1.call-start = ((), (), s32[]{:S(2)}) async-start(), calls=%async_computation.24 | async-start | bytes 1310720 | tf_op jit(solution)/shard_map/reduce_scatter | solution.py:42
  133.7 31.2 %copy-start.30 = (bf16[2,256,256]{2,1,0:T(8,128)(2,1)S(1)}, bf16[2,256,256]{2,1,0:T(8,128)(2,1)}, u32[]{:S(2)}) copy-start(bf16[2,256,256]{2,1,0:T(8,128)(2,1)} %param.17) | copy-start | bytes 786436
  135.3 80.4 %all-gather.34.cloned.1.call-start = ((), (), s32[]{:S(2)}) async-start(), calls=%async_computation.45 | async-start | bytes 2359296 | tf_op jit(solution)/shard_map/all_gather | solution.py:107
  136.1 97.9 %all-gather.16.cloned.1.call-start = ((), (), s32[]{:S(2)}) async-start(), calls=%async_computation.25 | async-start | bytes 1310720 | tf_op jit(solution)/shard_map/all_gather | solution.py:46
  166.6 117.5 %all-gather.18.cloned.1.call-start = ((), (), s32[]{:S(2)}) async-start(), calls=%async_computation.26 | async-start | bytes 2359296 | tf_op jit(solution)/shard_map/all_gather | solution.py:126
  167.2 145.5 %reduce-scatter.15.cloned.1.call-start = ((), (), s32[]{:S(2)}) async-start(), calls=%async_computation.27 | async-start | bytes 1310720 | tf_op jit(solution)/shard_map/reduce_scatter | solution.py:42
  284.2 28.6 %copy-start.17 = (bf16[512,256]{1,0:T(8,128)(2,1)S(1)}, bf16[512,256]{1,0:T(8,128)(2,1)}, u32[]{:S(2)}) copy-start(bf16[512,256]{1,0:T(8,128)(2,1)} %add_convert_fusion.1) | copy-start | bytes 786436
  288.4 82.7 %all-gather.20.cloned.1.call-start = ((), (), s32[]{:S(2)}) async-start(), calls=%async_computation.28 | async-start | bytes 1638400 | tf_op jit(solution)/shard_map/all_gather | solution.py:46
  332.6 34.5 %all-to-all-start.2 = ((bf16[4,256,1024]{1,2,0:T(8,128)(2,1)}), bf16[4,256,1024]{1,2,0:T(8,128)(2,1)}, u32[]{:S(2)}, u32[]{:S(2)}) async-start(bf16[4,256,1024]{1,2,0:T(8,128)(2,1)} %bitcast.255), calls=%async_computation.4 | async-start | bytes 4194304 | tf_op jit(solution)/shard_map/all_to_all | solution.py:130
  337.1 71.7 %reduce-scatter.17.cloned.1.call-start = ((), (), s32[]{:S(2)}) async-start(), calls=%async_computation.29 | async-start | bytes 1638400 | tf_op jit(solution)/shard_map/reduce_scatter | solution.py:42
  379.5 29.2 %copy-start.2 = (bf16[8,80,256]{2,1,0:T(8,128)(2,1)S(1)}, bf16[8,80,256]{2,1,0:T(8,128)(2,1)}, u32[]{:S(2)}) copy-start(bf16[8,80,256]{2,1,0:T(8,128)(2,1)} %all_to_all.56) | copy-start | bytes 983044
  382.1 28.4 %copy-start.36 = (bf16[2,256,256]{2,1,0:T(8,128)(2,1)S(1)}, bf16[2,256,256]{2,1,0:T(8,128)(2,1)}, u32[]{:S(2)}) copy-start(bf16[2,256,256]{2,1,0:T(8,128)(2,1)} %param.18) | copy-start | bytes 786436
  382.1 85.2 %all-gather.22.cloned.1.call-start = ((), (), s32[]{:S(2)}) async-start(), calls=%async_computation.30 | async-start | bytes 1638400 | tf_op jit(solution)/shard_map/all_gather | solution.py:46
  411.6 13.9 %all-to-all-start.5 = ((bf16[8,80,256]{2,1,0:T(8,128)(2,1)}), bf16[8,80,256]{2,1,0:T(8,128)(2,1)S(1)}, u32[]{:S(2)}, u32[]{:S(2)}) async-start(bf16[8,80,256]{2,1,0:T(8,128)(2,1)} %bitcast.35), calls=%async_computation.9 | async-start | bytes 655360 | tf_op jit(solution)/shard_map/all_to_all | solution.py:54
  426.2 37.2 %all-to-all-start.3 = ((bf16[4,256,1024]{1,2,0:T(8,128)(2,1)}), bf16[4,256,1024]{1,2,0:T(8,128)(2,1)}, u32[]{:S(2)}, u32[]{:S(2)}) async-start(bf16[4,256,1024]{1,2,0:T(8,128)(2,1)} %bitcast.256), calls=%async_computation.6 | async-start | bytes 4194304 | tf_op jit(solution)/shard_map/all_to_all | solution.py:130
  430.6 44.0 %all-gather.24.cloned.1.call-start = ((), (), s32[]{:S(2)}) async-start(), calls=%async_computation.32 | async-start | bytes 1638400 | tf_op jit(solution)/shard_map/all_gather | solution.py:46
  431.4 77.8 %reduce-scatter.21.cloned.1.call-start = ((), (), s32[]{:S(2)}) async-start(), calls=%async_computation.33 | async-start | bytes 1638400 | tf_op jit(solution)/shard_map/reduce_scatter | solution.py:42
  482.7 55.5 %reduce-scatter.19.cloned.1.call-start = ((), (), s32[]{:S(2)}) async-start(), calls=%async_computation.31 | async-start | bytes 1638400 | tf_op jit(solution)/shard_map/reduce_scatter | solution.py:42
  482.7 55.5 %copy-start.10 = (bf16[8,80,256]{2,1,0:T(8,128)(2,1)S(1)}, bf16[8,80,256]{2,1,0:T(8,128)(2,1)}, u32[]{:S(2)}) copy-start(bf16[8,80,256]{2,1,0:T(8,128)(2,1)} %copy-done.9) | copy-start | bytes 983044
  482.7 55.5 %copy-start.16 = (bf16[640,256]{1,0:T(8,128)(2,1)S(1)}, bf16[640,256]{1,0:T(8,128)(2,1)}, u32[]{:S(2)}) copy-start(bf16[640,256]{1,0:T(8,128)(2,1)} %fusion.84) | copy-start | bytes 983044
  486.8 73.2 %all-gather.26.cloned.1.call-start = ((), (), s32[]{:S(2)}) async-start(), calls=%async_computation.34 | async-start | bytes 1638400 | tf_op jit(solution)/shard_map/all_gather | solution.py:46
  541.5 53.9 %reduce-scatter.23.cloned.1.call-start = ((), (), s32[]{:S(2)}) async-start(), calls=%async_computation.35 | async-start | bytes 1638400 | tf_op jit(solution)/shard_map/reduce_scatter | solution.py:42
  565.1 30.3 %copy-start.15 = (bf16[640,256]{1,0:T(8,128)(2,1)S(1)}, bf16[640,256]{1,0:T(8,128)(2,1)}, u32[]{:S(2)}) copy-start(bf16[640,256]{1,0:T(8,128)(2,1)} %get-tuple-element.32) | copy-start | bytes 983044
  568.8 60.5 %all-gather.28.cloned.1.call-start = ((), (), s32[]{:S(2)}) async-start(), calls=%async_computation.36 | async-start | bytes 1310720 | tf_op jit(solution)/shard_map/all_gather | solution.py:46
  613.1 48.8 %reduce-scatter.25.cloned.1.call-start = ((), (), s32[]{:S(2)}) async-start(), calls=%async_computation.37 | async-start | bytes 1310720 | tf_op jit(solution)/shard_map/reduce_scatter | solution.py:42
  633.8 28.1 %copy-start.31 = (bf16[2,256,256]{2,1,0:T(8,128)(2,1)S(1)}, bf16[2,256,256]{2,1,0:T(8,128)(2,1)}, u32[]{:S(2)}) copy-start(bf16[2,256,256]{2,1,0:T(8,128)(2,1)} %convolution_convert_fusion.14) | copy-start | bytes 786436
  636.9 44.1 %copy-start.20 = (bf16[256,1024]{1,0:T(8,128)(2,1)S(1)}, bf16[256,1024]{1,0:T(8,128)(2,1)}, u32[]{:S(2)}) copy-start(bf16[256,1024]{1,0:T(8,128)(2,1)} %all_gather.49) | copy-start | bytes 1572868
  637.0 44.1 %all-gather.30.cloned.1.call-start = ((), (), s32[]{:S(2)}) async-start(), calls=%async_computation.38 | async-start | bytes 1310720 | tf_op jit(solution)/shard_map/all_gather | solution.py:46
  661.9 21.1 %copy-start.29 = (bf16[2,256,4,64]{1,3,2,0:T(8,128)(2,1)S(1)}, bf16[2,256,4,64]{1,3,2,0:T(8,128)(2,1)}, u32[]{:S(2)}) copy-start(bf16[2,256,4,64]{1,3,2,0:T(8,128)(2,1)} %copy-done.28) | copy-start | bytes 786436
  664.1 143.7 %reduce-scatter.27.cloned.1.call-start = ((), (), s32[]{:S(2)}) async-start(), calls=%async_computation.39 | async-start | bytes 1310720 | tf_op jit(solution)/shard_map/reduce_scatter | solution.py:42
  701.1 115.6 %reduce-scatter.31.cloned.1.call-start = ((), (), s32[]{:S(2)}) async-start(), calls=%async_computation.41 | async-start | bytes 2359296 | tf_op jit(solution)/shard_map/reduce_scatter | solution.py:251
  705.4 163.4 %reduce-scatter.29.cloned.1.call-start = ((), (), s32[]{:S(2)}) async-start(), calls=%async_computation.40 | async-start | bytes 1769472 | tf_op jit(solution)/shard_map/reduce_scatter | solution.py:251
  709.0 230.6 %reduce-scatter.35.cloned.1.call-start = ((), (), s32[]{:S(2)}) async-start(), calls=%async_computation.43 | async-start | bytes 2359296 | tf_op jit(solution)/shard_map/reduce_scatter | solution.py:259
  718.5 29.2 %all-to-all-start.10 = ((bf16[4,256,1024]{2,1,0:T(8,128)(2,1)}), bf16[4,256,1024]{2,1,0:T(8,128)(2,1)S(1)}, u32[]{:S(2)}, u32[]{:S(2)}) async-start(bf16[4,256,1024]{2,1,0:T(8,128)(2,1)} %bitcast.271), calls=%async_computation.22 | async-start | bytes 4194304 | tf_op jit(solution)/shard_map/all_to_all | solution.py:246
  747.8 23.3 %all-to-all-start.4 = ((bf16[8,80,256]{2,1,0:T(8,128)(2,1)}), bf16[8,80,256]{2,1,0:T(8,128)(2,1)S(1)}, u32[]{:S(2)}, u32[]{:S(2)}) async-start(bf16[8,80,256]{2,1,0:T(8,128)(2,1)} %bitcast.29), calls=%async_computation.8 | async-start | bytes 655360 | tf_op jit(solution)/shard_map/all_to_all | solution.py:54
  777.1 33.7 %all-to-all-start.9 = ((bf16[4,256,1024]{2,1,0:T(8,128)(2,1)}), bf16[4,256,1024]{2,1,0:T(8,128)(2,1)S(1)}, u32[]{:S(2)}, u32[]{:S(2)}) async-start(bf16[4,256,1024]{2,1,0:T(8,128)(2,1)} %bitcast.267), calls=%async_computation.21 | async-start | bytes 4194304 | tf_op jit(solution)/shard_map/all_to_all | solution.py:246
  780.7 224.9 %reduce-scatter.33.cloned.1.call-start = ((), (), s32[]{:S(2)}) async-start(), calls=%async_computation.42 | async-start | bytes 589824 | tf_op jit(solution)/shard_map/reduce_scatter | solution.py:258
  787.0 20.8 %copy-start.18 = (bf16[512,256]{1,0:T(8,128)(2,1)S(1)}, bf16[512,256]{1,0:T(8,128)(2,1)}, u32[]{:S(2)}) copy-start(bf16[512,256]{1,0:T(8,128)(2,1)} %get-tuple-element.40) | copy-start | bytes 786436
  810.8 59.8 %all-to-all-start.8 = ((f32[8,2,32]{2,1,0:T(2,128)}), f32[8,2,32]{2,1,0:T(2,128)S(1)}, u32[]{:S(2)}, u32[]{:S(2)}) async-start(f32[8,2,32]{2,1,0:T(2,128)} %pad_maximum_fusion.2), calls=%async_computation.19 | async-start | bytes 16384 | tf_op jit(solution)/shard_map/all_to_all | solution.py:261
  870.6 137.1 %all-to-all-start.7 = ((bf16[4,32,1792]{2,1,0:T(8,128)(2,1)}), bf16[4,32,1792]{2,1,0:T(8,128)(2,1)S(1)}, u32[]{:S(2)}, u32[]{:S(2)}) async-start(bf16[4,32,1792]{2,1,0:T(8,128)(2,1)} %pad_maximum_fusion.1), calls=%async_computation.17 | async-start | bytes 917504 | tf_op jit(solution)/shard_map/all_to_all | solution.py:254
  (38 other events, 138.6 us)
Sparse Core Ops, SparseCore 0:
  9.6 19.3 all-gather.13
  31.7 43.7 all-gather.31
  135.4 29.4 reduce-scatter.12
  167.5 48.1 all-gather.33
  217.7 16.2 all-gather.15
  235.9 48.2 all-gather.17
  288.5 24.1 reduce-scatter.14
  328.6 21.8 all-gather.19
  382.3 26.4 reduce-scatter.16
  410.7 18.3 all-gather.21
  433.6 26.7 all-gather.23
  482.8 26.3 reduce-scatter.20
  511.7 26.4 reduce-scatter.18
  541.6 18.3 all-gather.25
  568.9 26.4 reduce-scatter.22
  613.3 15.9 all-gather.27
  637.1 24.7 reduce-scatter.24
  664.2 16.8 all-gather.29
  701.3 24.7 reduce-scatter.26
  729.5 71.3 reduce-scatter.30
  804.2 64.4 reduce-scatter.28
  872.3 67.3 reduce-scatter.34
  943.6 61.9 reduce-scatter.32

commit v2 on v1

v2 whole, which is shorter than its diff:
```python
import functools

import jax
import jax.numpy as jnp
from jax import lax
from jax.experimental import pallas as pl
from jax.experimental.pallas import tpu as pltpu
from jax.sharding import PartitionSpec as P

HEAD_SIZE = 64
F32 = jnp.float32
BF16 = jnp.bfloat16

MESH = pl.DeviceIdType.MESH
ANY = pl.BlockSpec(memory_space=pl.ANY)
VM = pl.BlockSpec(memory_space=pltpu.VMEM)
DMA = pltpu.SemaphoreType.DMA
VMEM_BYTES = 60 * 1024 * 1024
QUARTER = 256


def section_places():
    me = lax.axis_index("section")
    return me, me + 1 - 2 * lax.rem(me, 2), me + 2 - 4 * lax.div(me, 2)


def greet(peers):
    barrier = pltpu.get_barrier_semaphore()
    for peer in peers:
        pl.semaphore_signal(barrier, inc=1, device_id=peer, device_id_type=MESH)
    pl.semaphore_wait(barrier, len(peers))


def push(src, dst, send, recv, peer):
    return pltpu.make_async_remote_copy(
        src_ref=src, dst_ref=dst, send_sem=send, recv_sem=recv, device_id=peer, device_id_type=MESH
    )


def columns(which):
    return pl.ds(pl.multiple_of(which * QUARTER, QUARTER), QUARTER)


def call(kernel, out_shape, in_specs, out_specs, scratch, collective_id, *operands):
    return pl.pallas_call(
        kernel,
        out_shape=out_shape,
        in_specs=in_specs,
        out_specs=out_specs,
        scratch_shapes=scratch,
        compiler_params=pltpu.CompilerParams(
            collective_id=collective_id, has_side_effects=True, vmem_limit_bytes=VMEM_BYTES
        ),
    )(*operands)


def reduce_kernel(chunks, with_stats, *refs):
    if with_stats:
        part, stats, out, stats_out = refs[:4]
        first_in, far, far_in, s1, r1, s2, r2, st_in, st_mid, st_far, st_s, st_r = refs[4:]
    else:
        part, out, first_in, far, far_in, s1, r1, s2, r2 = refs
    me, beside, across = section_places()
    core, side = lax.rem(me, 2), lax.div(me, 2)
    greet([{"section": beside}, {"section": across}])
    rows = part.shape[0] // chunks
    beside_core = 1 - core
    sends = []
    if with_stats:
        st = push(stats, st_in, st_s.at[0], st_r.at[0], {"section": beside})
        st.start()
    for k in range(chunks):
        for which, half in ((1, 1 - side), (0, side)):
            at = pl.ds(k * rows, rows)
            c = push(
                part.at[at, columns(2 * half + beside_core)],
                first_in.at[which, at],
                s1.at[which, k],
                r1.at[which, k],
                {"section": beside},
            )
            c.start()
            sends.append(c)
    if with_stats:
        st.wait()
        st_mid[...] = stats[...] + st_in[...]
        st2 = push(st_mid, st_far, st_s.at[1], st_r.at[1], {"section": across})
        st2.start()
    crossing = []
    for k in range(chunks):
        at = pl.ds(k * rows, rows)
        sends[2 * k].wait()
        far[at] = (part[at, columns(2 * (1 - side) + core)].astype(F32) + first_in[1, at].astype(F32)).astype(BF16)
        c = push(far.at[at], far_in.at[at], s2.at[k], r2.at[k], {"section": across})
        c.start()
        crossing.append(c)
    for k in range(chunks):
        at = pl.ds(k * rows, rows)
        sends[2 * k + 1].wait()
        near = part[at, columns(me)].astype(F32) + first_in[0, at].astype(F32)
        crossing[k].wait()
        out[at] = near + far_in[at].astype(F32)
    if with_stats:
        st2.wait()
        stats_out[...] = st_mid[...] + st_far[...]


def reduce_call(part, stats, collective_id, chunks=4):
    rows, _ = part.shape
    scratch = [
        pltpu.VMEM((2, rows, QUARTER), BF16),
        pltpu.VMEM((rows, QUARTER), BF16),
        pltpu.VMEM((rows, QUARTER), BF16),
        DMA((2, chunks)),
        DMA((2, chunks)),
        DMA((chunks,)),
        DMA((chunks,)),
    ]
    out = jax.ShapeDtypeStruct((rows, QUARTER), F32)
    if stats is None:
        return call(
            functools.partial(reduce_kernel, chunks, False), out, [VM], VM, scratch, collective_id, part
        )
    st = pltpu.VMEM(stats.shape, F32)
    return call(
        functools.partial(reduce_kernel, chunks, True),
        (out, jax.ShapeDtypeStruct(stats.shape, F32)),
        [VM, VM],
        (VM, VM),
        scratch + [st, st, st, DMA((2,)), DMA((2,))],
        collective_id,
        part,
        stats,
    )


def gather_kernel(chunks, q, out, s, r):
    me, beside, across = section_places()
    greet([{"section": beside}, {"section": across}])
    rows = q.shape[0] // chunks
    copies = []
    for k in range(chunks):
        at = pl.ds(k * rows, rows)
        for kind, to in ((0, across), (1, beside)):
            c = push(q.at[at], out.at[at, columns(me)], s.at[kind, k], r.at[kind, k], {"section": to})
            c.start()
            copies.append(c)
    out[:, columns(me)] = q[...]
    for k in range(chunks):
        at = pl.ds(k * rows, rows)
        copies[2 * k].wait()
        here = out.at[at, columns(across)]
        c = push(here, here, s.at[2, k], r.at[2, k], {"section": beside})
        c.start()
        copies.append(c)
    for k in range(chunks):
        copies[2 * k + 1].wait()
        copies[2 * chunks + k].wait()


def gather_call(q, collective_id, chunks=4):
    rows = q.shape[0]
    return call(
        functools.partial(gather_kernel, chunks),
        jax.ShapeDtypeStruct((rows, 4 * QUARTER), BF16),
        [VM],
        VM,
        [DMA((3, chunks)), DMA((3, chunks))],
        collective_id,
        q,
    )


def exchange_kernel(spread, src, out, s, r):
    me, beside, across = section_places()
    w = lax.axis_index("wide")
    count = src.shape[0]
    peers = [{"wide": lax.rem(w + j, count)} for j in range(1, count)]
    greet(peers + ([{"section": beside}, {"section": across}] if spread else []))

    def place(which, block):
        return out.at[block, :, columns(which)] if spread else out.at[block]

    def wide_copy(to):
        return push(src.at[to], place(me, w), s.at[0, to], r.at[0, w], {"wide": to})

    def arrival(frm):
        return push(src.at[frm], place(me, frm), s.at[0, frm], r.at[0, frm], {"wide": frm})

    def spread_copy(kind, block, to):
        here = place(across, block) if kind == 3 else place(me, block)
        return push(here, here, s.at[kind, block], r.at[kind, block], {"section": to})

    for j in range(1, count):
        wide_copy(lax.rem(w + j, count)).start()
    if spread:
        out[w, :, columns(me)] = src[w]
    else:
        out[w] = src[w]
    for j in range(count):
        block = lax.rem(w + j, count)
        if j:
            arrival(block).wait_recv()
        if spread:
            spread_copy(1, block, across).start()
            spread_copy(2, block, beside).start()
    if spread:
        for j in range(count):
            block = lax.rem(w + j, count)
            spread_copy(1, block, across).wait_recv()
            spread_copy(3, block, beside).start()
        for j in range(count):
            block = lax.rem(w + j, count)
            spread_copy(1, block, across).wait_send()
            spread_copy(2, block, beside).wait()
            spread_copy(3, block, beside).wait()
    for j in range(1, count):
        wide_copy(lax.rem(w + j, count)).wait_send()


def exchange_call(slots, spread, collective_id):
    count, n, quarter = slots.shape
    return call(
        functools.partial(exchange_kernel, spread),
        jax.ShapeDtypeStruct((count, n, 4 * quarter if spread else quarter), BF16),
        [VM],
        VM,
        [DMA((4, count)), DMA((4, count))],
        collective_id,
        slots,
    )


def weights_kernel(qkv, inn, vec, outw, backw, first, second, tok, *refs):
    o_qkv, o_in, o_vec, o_out, o_back, o_first, o_second, o_tok = refs[:8]
    st_qkv, st_in, st_vec, loc, cut_s, cut_r, tok_s, tok_r, line_s, line_r, exp_s, exp_r = refs[8:]
    me, beside, across = section_places()
    w = lax.axis_index("wide")
    length = lax.axis_size("wide") // 2
    a, b = lax.div(w, 2), lax.rem(w, 2)
    other = 1 - b
    diagonal = beside + across - me
    peers = [beside, across, diagonal]
    barrier = pltpu.get_barrier_semaphore()
    for p in peers:
        pl.semaphore_signal(barrier, inc=1, device_id={"section": p}, device_id_type=MESH)
    pl.semaphore_signal(barrier, inc=1, device_id={"wide": 2 * a + other}, device_id_type=MESH)

    @pl.when(a > 0)
    def _():
        pl.semaphore_signal(barrier, inc=1, device_id={"wide": w - 2}, device_id_type=MESH)

    @pl.when(a < length - 1)
    def _():
        pl.semaphore_signal(barrier, inc=1, device_id={"wide": w + 2}, device_id_type=MESH)

    pl.semaphore_wait(barrier, 4 + jnp.minimum(a, 1) + jnp.minimum(length - 1 - a, 1))

    cuts = ((qkv, st_qkv), (inn, st_in), (vec, st_vec))
    sent, locals_ = [], []
    for i, (src, stage) in enumerate(cuts):
        for k, p in enumerate(peers):
            c = push(src.at[p] if i < 2 else src, stage.at[me], cut_s.at[i, k], cut_r.at[i, k], {"section": p})
            c.start()
            sent.append(c)
        c = pltpu.make_async_copy(src.at[me] if i < 2 else src, stage.at[me], loc.at[i])
        c.start()
        locals_.append(c)
    tok_c = [
        push(tok, o_tok.at[:, columns(me)], tok_s.at[k], tok_r.at[k], {"section": p})
        for k, p in enumerate((across, beside))
    ]
    for c in tok_c:
        c.start()
    own_tok = pltpu.make_async_copy(tok, o_tok.at[:, columns(me)], loc.at[3])
    own_tok.start()
    late = [own_tok]
    for i, (src, dst) in enumerate(((first, o_first), (second, o_second))):
        c = pltpu.make_async_copy(src.at[me], dst.at[me], loc.at[4 + i])
        c.start()
        late.append(c)
    exp_c = []
    for i, (src, dst) in enumerate(((first, o_first), (second, o_second))):
        for k, p in enumerate((across, diagonal, beside)):
            c = push(src.at[p], dst.at[me], exp_s.at[i, k], exp_r.at[i, k], {"section": p})
            c.start()
            exp_c.append(c)

    lines = (
        (st_qkv, o_qkv, True),
        (outw, o_out, False),
        (st_in, o_in, True),
        (backw, o_back, False),
        (st_vec, o_vec, False),
    )
    staged = {0: 0, 2: 1, 4: 2}

    def item(i, which, kind, to, own=False):
        src, dst, _ = lines[i]
        return push(
            src if own else dst.at[which], dst.at[which], line_s.at[kind, i, which], line_r.at[i, which], {"wide": to}
        )

    up, down, pair = 0, 1, 2

    def along(i, which, kind, own, act):
        if kind == pair:
            act(item(i, which, pair, 2 * a + other, own))
            return

        @pl.when((a < length - 1) if kind == up else (a > 0))
        def _():
            act(item(i, which, kind, w + 2 if kind == up else w - 2, own))

    def start(c):
        c.start()

    def done(c):
        c.wait_send()

    for i, (src, dst, _) in enumerate(lines):
        if i in staged:
            j = staged[i]
            for k in range(3):
                sent[3 * j + k].wait_recv()
            locals_[j].wait()
        for kind in (up, down, pair):
            along(i, w, kind, True, start)
        c = pltpu.make_async_copy(src, dst.at[w], loc.at[6 + i])
        c.start()
        late.append(c)
    tok_c[0].wait_recv()
    spot = o_tok.at[:, columns(across)]
    tok_fwd = push(spot, spot, tok_s.at[2], tok_r.at[2], {"section": beside})
    tok_fwd.start()

    mate = 2 * a + other

    def arrived(i, which):
        item(i, which, pair, mate).wait_recv()

    for i in range(len(lines)):
        if not lines[i][2]:
            arrived(i, mate)
            for kind in (up, down):
                along(i, mate, kind, False, start)

    def step(t, carry):
        for i in range(len(lines)):
            for kind, there, ok in ((up, a - t, a - t >= 0), (down, a + t, a + t < length)):

                @pl.when(ok)
                def _():
                    arrived(i, 2 * there + b)
                    along(i, 2 * there + b, kind, False, start)
                    if lines[i][2]:
                        along(i, 2 * there + b, pair, False, start)
                    else:
                        arrived(i, 2 * there + other)
                        along(i, 2 * there + other, kind, False, start)

        return carry

    lax.fori_loop(1, length, step, 0)
    for i in range(len(lines)):
        if lines[i][2]:
            lax.fori_loop(0, length, lambda there, carry: (arrived(i, 2 * there + other), carry)[1], 0)
        for kind in (up, down, pair):
            along(i, w, kind, True, done)
        if not lines[i][2]:
            for kind in (up, down):
                along(i, mate, kind, False, done)

    def finish(t, carry):
        for i in range(len(lines)):
            for kind, there, ok in ((up, a - t, a - t >= 0), (down, a + t, a + t < length)):

                @pl.when(ok)
                def _():
                    along(i, 2 * there + b, kind, False, done)
                    if lines[i][2]:
                        along(i, 2 * there + b, pair, False, done)
                    else:
                        along(i, 2 * there + other, kind, False, done)

        return carry

    lax.fori_loop(1, length, finish, 0)
    for c in sent:
        c.wait_send()
    tok_c[0].wait_send()
    tok_c[1].wait()
    tok_fwd.wait()
    for c in exp_c:
        c.wait()
    for c in late:
        c.wait()


def weights_call(qkv, inn, vec, outw, backw, first, second, tok, wide, collective_id):
    outs = [
        ((wide, *qkv.shape), BF16),
        ((wide, *inn.shape), BF16),
        ((wide, 4, *vec.shape), F32),
        ((wide, *outw.shape), BF16),
        ((wide, *backw.shape), BF16),
        (first.shape, BF16),
        (second.shape, BF16),
        ((tok.shape[0], 4 * QUARTER), BF16),
    ]
    return call(
        weights_kernel,
        tuple(jax.ShapeDtypeStruct(*o) for o in outs),
        [ANY] * 8,
        tuple([ANY] * 8),
        [
            pltpu.VMEM(qkv.shape, BF16),
            pltpu.VMEM(inn.shape, BF16),
            pltpu.VMEM((4, *vec.shape), F32),
            DMA((11,)),
            DMA((3, 3)),
            DMA((3, 3)),
            DMA((3,)),
            DMA((3,)),
            DMA((3, 5, wide)),
            DMA((5, wide)),
            DMA((2, 3)),
            DMA((2, 3)),
        ],
        collective_id,
        qkv,
        inn,
        vec,
        outw,
        backw,
        first,
        second,
        tok,
    )


GROUP = 32


def add_rows(dst, left, right):
    rows = dst.shape[0]
    step = min(rows, GROUP)

    def one(j, carry):
        at = pl.ds(pl.multiple_of(j * step, step), step)
        dst[at] = (left[at].astype(F32) + right[at].astype(F32)).astype(dst.dtype)
        return carry

    lax.fori_loop(0, rows // step, one, 0)


def gradients_kernel(*refs):
    count = 5
    src = refs[:count]
    first, second = refs[count : count + 2]
    o_qkv, o_in, o_out, o_back, o_gain, o_first, o_second = refs[7:14]
    acc = refs[14:19]
    line_in = refs[19:24]
    pair_in = refs[24:29]
    (st_qkv, st_in, loc, exp_s, exp_r, cut_s, cut_r, pair_s, pair_r, line_s, line_r) = refs[29:]
    me, beside, across = section_places()
    diagonal = beside + across - me
    w = lax.axis_index("wide")
    length = lax.axis_size("wide") // 2
    a, b = lax.div(w, 2), lax.rem(w, 2)
    other = 1 - b
    mate = {"wide": 2 * a + other}
    peers = [beside, across, diagonal]
    barrier = pltpu.get_barrier_semaphore()
    for p in peers:
        pl.semaphore_signal(barrier, inc=1, device_id={"section": p}, device_id_type=MESH)
    pl.semaphore_signal(barrier, inc=1, device_id=mate, device_id_type=MESH)

    @pl.when(a > 0)
    def _():
        pl.semaphore_signal(barrier, inc=1, device_id={"wide": w - 2}, device_id_type=MESH)

    @pl.when(a < length - 1)
    def _():
        pl.semaphore_signal(barrier, inc=1, device_id={"wide": w + 2}, device_id_type=MESH)

    pl.semaphore_wait(barrier, 4 + jnp.minimum(a, 1) + jnp.minimum(length - 1 - a, 1))

    pair_first = (True, True, False, False, False)

    def pair_copy(i, there):
        return push(src[i].at[2 * there + other], pair_in[i].at[there], pair_s.at[i, there], pair_r.at[i, there], mate)

    for i in range(count):
        if pair_first[i]:
            lax.fori_loop(0, length, lambda t, c, i=i: (pair_copy(i, t).start(), c)[1], 0)

    late = []
    for i, (s, d) in enumerate(((first, o_first), (second, o_second))):
        c = pltpu.make_async_copy(s.at[me], d.at[me], loc.at[i])
        c.start()
        late.append(c)
        for k, p in enumerate((across, diagonal, beside)):
            c = push(s.at[p], d.at[me], exp_s.at[i, k], exp_r.at[i, k], {"section": p})
            c.start()
            late.append(c)

    def slots(i, there):
        if pair_first[i]:
            return [(there, 2 * there + b)]
        return [(2 * there, 2 * there), (2 * there + 1, 2 * there + 1)]

    def line_copy(i, block, to_block, to):
        return push(acc[i].at[block], line_in[i].at[to_block], line_s.at[i, block], line_r.at[i, to_block], {"wide": to})

    def wide_of(i):
        return 1 if pair_first[i] else 2

    def ready(i, there, block, own):
        if pair_first[i]:
            pair_copy(i, there).wait_recv()
            add_rows(acc[i].at[block], src[i].at[own], pair_in[i].at[there])
        else:
            acc[i][block] = src[i][own]

    def flow(i, there, from_edge, to):
        n = wide_of(i)
        for j, (block, own) in enumerate(slots(i, there)):
            ready(i, there, block, own)

            @pl.when(from_edge)
            def _():
                line_copy(i, block, block, w).wait_recv()
                add_rows(acc[i].at[block], acc[i].at[block], line_in[i].at[block])

            if to == "down":
                line_copy(i, block, block, w - 2).start()
            else:
                target = jnp.where(there == a + 1, n * length + j, block)
                line_copy(i, block, target, w + 2).start()

    def step(t, carry):
        high = length - 1 - t
        for i in range(count):

            @pl.when(t < a)
            def _():
                flow(i, t, a < length - 1, "down")

            @pl.when(high > a)
            def _():
                flow(i, high, a > 0, "up")

        return carry

    lax.fori_loop(0, length, step, 0)
    finals = []
    for i in range(count):
        n = wide_of(i)
        for j, (block, own) in enumerate(slots(i, a)):
            ready(i, a, block, own)

            @pl.when(a < length - 1)
            def _():
                line_copy(i, block, block, w).wait_recv()
                add_rows(acc[i].at[block], acc[i].at[block], line_in[i].at[block])

            @pl.when(a > 0)
            def _():
                line_copy(i, block, n * length + j, w).wait_recv()
                add_rows(acc[i].at[block], acc[i].at[block], line_in[i].at[n * length + j])

        if not pair_first[i]:
            c = push(acc[i].at[2 * a + other], pair_in[i].at[0], pair_s.at[i, 0], pair_r.at[i, 0], mate)
            c.start()
            finals.append(c)
        else:
            out, k0 = ((o_qkv, 0), (o_in, 1))[i]
            st = (st_qkv, st_in)[i]
            small = st.shape[1]
            for p in range(4):
                st[p] = acc[i][a, pl.ds(p * small, small)]
            for k, p in enumerate(peers):
                c = push(st.at[p], out.at[me], cut_s.at[i, k], cut_r.at[i, k], {"section": p})
                c.start()
                late.append(c)
            c = pltpu.make_async_copy(st.at[me], out.at[me], loc.at[2 + i])
            c.start()
            late.append(c)
    for i, out in ((2, o_out), (3, o_back), (4, o_gain)):
        finals[i - 2].wait_recv()
        add_rows(out, acc[i].at[2 * a + b], pair_in[i].at[0])
    for c in finals:
        c.wait_send()
    for c in late:
        c.wait()

    def finish(t, carry):
        for i in range(count):
            if pair_first[i]:
                pair_copy(i, t).wait_send()

            @pl.when(t != a)
            def _():
                for block, _ in slots(i, t):
                    line_copy(i, block, block, w).wait_send()

        return carry

    lax.fori_loop(0, length, finish, 0)


def gradients_call(dense, first, second, collective_id):
    wide = dense[0].shape[0]
    length = wide // 2
    shapes = [d.shape[1:] for d in dense]
    kinds = [d.dtype for d in dense]
    small = shapes[0][0] // 4
    first_count = [length, length, wide, wide, wide]
    in_count = [length + 1, length + 1, wide + 2, wide + 2, wide + 2]
    pair_count = [length, length, 1, 1, 1]
    outs = [((4, small, shapes[0][1]), BF16), ((4, small, shapes[1][1]), BF16)]
    outs += [(s, F32) for s in shapes[2:]] + [(first.shape, BF16), (second.shape, BF16)]
    scratch = [pltpu.VMEM((n, *s), k) for n, s, k in zip(first_count, shapes, kinds)]
    scratch += [pltpu.VMEM((n, *s), k) for n, s, k in zip(in_count, shapes, kinds)]
    scratch += [pltpu.VMEM((n, *s), k) for n, s, k in zip(pair_count, shapes, kinds)]
    scratch += [
        pltpu.VMEM((4, small, shapes[0][1]), BF16),
        pltpu.VMEM((4, small, shapes[1][1]), BF16),
        DMA((4,)),
        DMA((2, 3)),
        DMA((2, 3)),
        DMA((2, 3)),
        DMA((2, 3)),
        DMA((5, length)),
        DMA((5, length)),
        DMA((5, wide)),
        DMA((5, wide + 2)),
    ]
    return call(
        gradients_kernel,
        tuple(jax.ShapeDtypeStruct(*o) for o in outs),
        [VM] * 5 + [ANY, ANY],
        (ANY, ANY, VM, VM, VM, ANY, ANY),
        scratch,
        collective_id,
        *dense,
        first,
        second,
    )


def dot(left, right):
    return jnp.dot(left, right, preferred_element_type=F32)


def dot_nt(left, right):
    return lax.dot_general(left, right, (((1,), (1,)), ((), ())), preferred_element_type=F32)


def dot_tn(left, right):
    return lax.dot_general(left, right, (((0,), (0,)), ((), ())), preferred_element_type=F32)


def gelu_value(v):
    return 0.5 * v * (1.0 + lax.erf(v * 0.7071067811865476))


def gelu_slope(v):
    return (
        0.5 * (1.0 + lax.erf(v * 0.7071067811865476))
        + v * jnp.exp(-0.5 * v * v) * 0.3989422804014327
    )


def unit_norm(v):
    centred = v - jnp.mean(v, axis=-1, keepdims=True)
    scale = lax.rsqrt(jnp.mean(centred * centred, axis=-1, keepdims=True) + 1e-05)
    return centred * scale, scale


IDS = {}


def id_of(*key):
    return IDS.setdefault(key, len(IDS))


def reduce_quarters(part, stats=None):
    return reduce_call(part.astype(BF16), stats, id_of("reduce", part.shape, stats is None))


def gather_quarters(quarter):
    return gather_call(quarter, id_of("gather", quarter.shape))


def wide_exchange(slots, spread):
    return exchange_call(slots, spread, id_of("exchange", spread))


def attention_probs(queries, keys, lengths):
    rows = queries.shape[2]
    raw = jnp.einsum("mhqd,mhkd->mhqk", queries, keys, preferred_element_type=F32)
    pos = jnp.arange(rows, dtype=jnp.int32)
    same = pos[None, :, None] // lengths[:, None, None] == pos[None, None, :] // lengths[:, None, None]
    allowed = (pos[:, None] >= pos[None, :])[None] & same
    scores = jnp.where(allowed[:, None], raw * HEAD_SIZE ** (-0.5), -1e30)
    highest = jnp.max(scores, axis=-1, keepdims=True)
    expo = jnp.exp(scores - highest)
    return expo / jnp.sum(expo, axis=-1, keepdims=True)


def body(
    tokens_in,
    cotangent,
    routes,
    seq_lengths,
    qkv_weight,
    out_weight,
    attn_gain,
    ffn_in,
    ffn_back,
    ffn_gain,
    centroids,
    first_gain,
    first_in,
    first_back,
    second_gain,
    second_in,
    second_back,
):
    sections = lax.axis_size("section")
    wide = lax.axis_size("wide")
    section_id = lax.axis_index("section")
    wide_id = lax.axis_index("wide")
    micro, rows, quarter = tokens_in.shape
    width = quarter * sections
    cap = 5 * rows // (4 * wide)
    tok_rows = micro * rows
    hid = first_back.shape[1]
    small = qkv_weight.shape[0]
    qkv_cols = qkv_weight.shape[1] // sections

    qkv_cut = (
        qkv_weight.reshape(small, 3, sections, quarter).transpose(2, 0, 1, 3).reshape(sections, small, qkv_cols)
    )
    in_cut = ffn_in.reshape(small, sections, hid).transpose(1, 0, 2)
    vectors = jnp.concatenate([first_gain[0], second_gain[0], centroids[0], attn_gain, ffn_gain]).astype(F32)
    vectors = jnp.pad(vectors, (0, 1024 - vectors.shape[0])).reshape(8, 128)
    tokens_q = tokens_in.reshape(tok_rows, quarter)

    def slice_in(weight):
        return weight[0].reshape(quarter, sections, hid).transpose(1, 0, 2)

    qkv_w, in_w, vectors, out_w, back_w, first_w, second_w, tokens = weights_call(
        qkv_cut,
        in_cut,
        vectors,
        out_weight,
        ffn_back,
        slice_in(first_in),
        slice_in(second_in),
        tokens_q,
        wide,
        id_of("weights"),
    )
    qkv_w = qkv_w.transpose(1, 0, 2, 3).reshape(width, qkv_cols)
    in_w = in_w.transpose(1, 0, 2, 3).reshape(width, hid)
    out_w = out_w.reshape(quarter, width)
    back_w = back_w.reshape(hid, width)
    first_w = first_w.reshape(width, hid)
    second_w = second_w.reshape(width, hid)
    vectors = vectors.reshape(wide, sections, 1024).transpose(1, 0, 2)
    own = lax.dynamic_index_in_dim(vectors, wide_id, axis=1, keepdims=False)
    gain_first = own[:, :quarter].reshape(1, width)
    gain_second = own[:, quarter : 2 * quarter].reshape(1, width)
    centre = own[:, 2 * quarter : 3 * quarter].reshape(1, width)
    gain_attn = vectors[:, :, 3 * quarter : 3 * quarter + small].reshape(1, width)
    gain_ffn = vectors[:, :, 3 * quarter + small : 3 * quarter + 2 * small].reshape(1, width)
    own_quarter = lambda v: lax.dynamic_slice_in_dim(v, section_id * quarter, quarter, axis=1)
    first_b = first_back[0]
    second_b = second_back[0]

    experts = jnp.arange(wide, dtype=jnp.int32)
    choose = (routes == experts).astype(jnp.int32)
    upto = (jnp.arange(rows)[:, None] >= jnp.arange(rows)[None, :]).astype(BF16)
    ranking = jnp.einsum("rk,mke->mre", upto, choose.astype(BF16), preferred_element_type=F32).astype(jnp.int32) - 1
    slot_of = routes[:, :, 0] * cap + jnp.sum(ranking * choose, axis=2)
    onehot = (jnp.arange(wide * cap, dtype=jnp.int32)[None, :, None] == slot_of[:, None, :]).astype(BF16)

    def to_experts(rows_q):
        packed = jnp.einsum("msr,mrd->msd", onehot, rows_q.reshape(micro, rows, quarter), preferred_element_type=F32)
        packed = packed.astype(BF16).reshape(micro, wide, cap, quarter).transpose(1, 0, 2, 3)
        return wide_exchange(packed.reshape(wide, micro * cap, quarter), True).reshape(wide * micro * cap, width)

    def to_tokens(slots_q):
        back = wide_exchange(slots_q.reshape(wide, micro * cap, quarter), False)
        back = back.reshape(wide, micro, cap, quarter).transpose(1, 0, 2, 3).reshape(micro, wide * cap, quarter)
        got = jnp.einsum("msr,msd->mrd", onehot, back, preferred_element_type=F32)
        return got.astype(BF16).reshape(tok_rows, quarter)

    unit_a, scale_a = unit_norm(tokens.astype(F32))
    normed_a = (unit_a * gain_attn).astype(BF16)
    packed = dot(normed_a, qkv_w).astype(BF16)
    heads = quarter // HEAD_SIZE

    def by_head(v):
        return v.reshape(micro, rows, heads, HEAD_SIZE).transpose(0, 2, 1, 3)

    def from_head(v):
        return v.transpose(0, 2, 1, 3).reshape(tok_rows, quarter)

    queries, keys, values = (by_head(packed[:, i * quarter : (i + 1) * quarter]) for i in range(3))
    probs = attention_probs(queries, keys, seq_lengths)
    probs_b = probs.astype(BF16)
    mixed = from_head(
        jnp.einsum("mhqk,mhkd->mhqd", probs_b, values, preferred_element_type=F32).astype(BF16)
    )
    attended_q = (tokens_q.astype(F32) + reduce_quarters(dot(mixed, out_w))).astype(BF16)
    attended = gather_quarters(attended_q)

    def branch(v, w_in, w_back, gain):
        unit, scale = unit_norm(v.astype(F32))
        normed = (unit * gain).astype(BF16)
        pre = dot(normed, w_in)
        hidden = gelu_value(pre).astype(BF16)
        return (normed, unit, scale, pre, hidden), dot(hidden, w_back)

    def branch_back(grad, saved, w_in, w_back, gain, more=None):
        normed, unit, scale, pre, hidden = saved
        d_back = dot_tn(hidden, grad)
        d_pre = (dot_nt(grad, w_back) * gelu_slope(pre)).astype(BF16)
        d_in = dot_tn(normed, d_pre)
        return d_in, d_back, norm_back(dot_nt(d_pre, w_in), unit, scale, gain, more)

    def norm_back(d_part, unit, scale, gain, more=None):
        d_unit = d_part * gain
        sums = jnp.stack([jnp.sum(d_unit, axis=1), jnp.sum(d_unit * unit, axis=1)])
        if more is not None:
            sums = jnp.concatenate([sums, more])
        d_q, sums = reduce_quarters(d_part, jnp.pad(sums, ((0, 8 - sums.shape[0]), (0, 0))))
        extra, sums = sums[2], sums / width
        unit_q = own_quarter(unit)
        d_rows = scale * (d_q * own_quarter(gain) - sums[0][:, None] - unit_q * sums[1][:, None])
        return d_rows, jnp.sum(d_q * unit_q, axis=0), extra

    saved_d, part = branch(attended, in_w, back_w, gain_ffn)
    fed_q = (attended_q.astype(F32) + reduce_quarters(part)).astype(BF16)
    routed = to_experts(fed_q)
    routed_q = own_quarter(routed)
    d_mixed = to_experts(cotangent.reshape(tok_rows, quarter)).astype(F32)
    d_mixed_q = own_quarter(d_mixed)
    saved_1, part = branch(routed, first_w, first_b, gain_first)
    first_q = (routed_q.astype(F32) + reduce_quarters(part)).astype(BF16)
    first = gather_quarters(first_q)
    saved_2, part = branch(first, second_w, second_b, gain_second)
    gate = jax.nn.sigmoid(jnp.sum(routed.astype(F32) * centre, axis=-1, keepdims=True))
    second_q = first_q.astype(F32) + reduce_quarters(part)
    mixed_q = routed_q.astype(F32) + gate * second_q
    block_out = to_tokens(mixed_q.astype(BF16)).reshape(micro, rows, quarter)

    d_second = gate * d_mixed
    d_second_q = gate * d_mixed_q
    d_second_in, d_second_back, (norm_q, second_gain_grad, d_logit) = branch_back(
        d_second.astype(BF16), saved_2, second_w, second_b, gain_second, jnp.sum(d_mixed_q * second_q, axis=-1)[None]
    )
    d_logit = d_logit[:, None] * gate * (1.0 - gate)
    centroids_grad = jnp.sum(d_logit * routed_q.astype(F32), axis=0)[None]
    d_gated_q = (d_mixed_q + d_logit * own_quarter(centre)).astype(BF16)
    d_first_q = (d_second_q + norm_q).astype(BF16)
    d_first_in, d_first_back, (norm_q, first_gain_grad, _) = branch_back(
        gather_quarters(d_first_q), saved_1, first_w, first_b, gain_first
    )
    d_routed_q = (d_first_q.astype(F32) + norm_q + d_gated_q.astype(F32)).astype(BF16)
    d_fed_q = to_tokens(d_routed_q)
    d_in, d_back, (norm_q, d_gain_ffn, _) = branch_back(gather_quarters(d_fed_q), saved_d, in_w, back_w, gain_ffn)
    d_attended_q = (d_fed_q.astype(F32) + norm_q).astype(BF16)
    d_attended = gather_quarters(d_attended_q)
    d_out = dot_tn(mixed, d_attended)
    d_mix = by_head(dot_nt(d_attended, out_w).astype(BF16))
    d_probs = jnp.einsum("mhqd,mhkd->mhqk", d_mix, values, preferred_element_type=F32)
    delta = jnp.sum(probs * d_probs, axis=-1, keepdims=True)
    d_scores = (probs * (d_probs - delta) * HEAD_SIZE ** (-0.5)).astype(BF16)
    d_queries = jnp.einsum("mhqk,mhkd->mhqd", d_scores, keys, preferred_element_type=F32)
    d_keys = jnp.einsum("mhqk,mhqd->mhkd", d_scores, queries, preferred_element_type=F32)
    d_values = jnp.einsum("mhqk,mhqd->mhkd", probs_b, d_mix, preferred_element_type=F32)
    d_packed = jnp.concatenate([from_head(v) for v in (d_queries, d_keys, d_values)], axis=1).astype(BF16)
    d_qkv = dot_tn(normed_a, d_packed)
    norm_q, d_gain_attn, _ = norm_back(dot_nt(d_packed, qkv_w), unit_a, scale_a, gain_attn)
    tokens_grad = (d_attended_q.astype(F32) + norm_q).reshape(micro, rows, quarter)

    def by_wide(grad):
        pieces = grad.astype(BF16).reshape(sections, wide, small, grad.shape[1]).transpose(1, 0, 2, 3)
        return pieces.reshape(wide, sections * small, grad.shape[1])

    def own_in(pieces):
        return pieces.transpose(1, 0, 2).reshape(1, quarter, sections * hid).astype(F32)

    d_gains = jnp.stack([d_gain_attn.reshape(wide, small), d_gain_ffn.reshape(wide, small)], axis=1)
    d_gains = jnp.pad(d_gains, ((0, 0), (0, 6), (0, 128 - small)))
    qkv_grad, ffn_in_grad, out_grad, ffn_back_grad, d_gains, d_first_in, d_second_in = gradients_call(
        (
            by_wide(d_qkv),
            by_wide(d_in),
            d_out.astype(BF16).reshape(wide, small, width),
            d_back.astype(BF16).reshape(wide, hid // wide, width),
            d_gains,
        ),
        d_first_in.astype(BF16).reshape(sections, quarter, hid),
        d_second_in.astype(BF16).reshape(sections, quarter, hid),
        id_of("gradients"),
    )
    qkv_grad = qkv_grad.astype(F32).reshape(sections, small, 3, quarter).transpose(1, 2, 0, 3)
    qkv_grad = qkv_grad.reshape(small, 3 * width)
    ffn_in_grad = ffn_in_grad.astype(F32).transpose(1, 0, 2).reshape(small, sections * hid)
    return (
        block_out,
        tokens_grad,
        qkv_grad,
        out_grad,
        d_gains[0, :small],
        ffn_in_grad,
        ffn_back_grad,
        d_gains[1, :small],
        centroids_grad,
        first_gain_grad[None],
        own_in(d_first_in),
        d_first_back[None],
        second_gain_grad[None],
        own_in(d_second_in),
        d_second_back[None],
    )


def solution(mesh):
    dense = P(("section", "wide"), None)
    dense_gain = P(("section", "wide"))
    tokens = P(None, "wide", "section")
    gain = P("wide", "section")
    expert = P("wide", "section", None)
    in_specs = (
        (tokens, tokens, P(None, "wide", None), P(), dense, dense, dense_gain, dense, dense, dense_gain)
        + (gain, gain, expert, expert, gain, expert, expert)
    )
    out_specs = (
        (tokens, tokens, dense, dense, dense_gain, dense, dense, dense_gain)
        + (gain, gain, expert, expert, gain, expert, expert)
    )
    return jax.shard_map(body, mesh=mesh, in_specs=in_specs, out_specs=out_specs, check_vma=False)
```

time: 1030 us -> 665 us (0.65)
  waiting for transfers between devices: 584 us -> 0 us
  Pallas kernels: 0 us -> 436 us
  blocking collectives: 172 us -> 0 us
  starting transfers between devices: 39.9 us -> 0 us
  between operations: 15.7 us -> 2.23 us
  matrix products: 108 us -> 97.2 us
  other arithmetic: 34.2 us -> 44.6 us
    pallas_call x0 -> x19, Pallas kernels: none -> 436 us  [call(): pl.pallas_call(kernel, out_shape=out_shape, in_specs=in_specs, out_specs=...]
    reduce_scatter x12 -> x0, waiting for transfers between devices: 334 us -> none  [the longest x8 164 us: reduce_quarters(): lax.psum_scatter(part.astype(BF16), 'section', scatter_dimension=1, tiled...]
    all_gather x11 -> x0, waiting for transfers between devices: 157 us -> none  [the longest x8 65.9 us: gather_quarters(): return lax.all_gather(quarter, 'section', axis=1, tiled=True)]
    all_gather x2 -> x0, blocking collectives: 93.9 us -> none  [the longest x1 62 us: body(): lax.all_gather(vectors, ('section', 'wide'), axis=0, tiled=False)]
    all_to_all x8 -> x0, waiting for transfers between devices: 90.9 us -> none  [the longest x2 61.6 us: slice_in(): lax.all_to_all(pieces, 'section', split_axis=0, concat_axis=0, tiled=True)]
    all_to_all x3 -> x0, blocking collectives: 41.4 us -> none  [the longest x2 28.8 us: wide_exchange(): lax.all_to_all(slots, 'wide', split_axis=0, concat_axis=0, tiled=True)]
    all_to_all x8 -> x0, starting transfers between devices: 38.2 us -> none  [the longest x2 12.3 us: wide_exchange(): lax.all_to_all(slots, 'wide', split_axis=0, concat_axis=0, tiled=True)]
    psum x4 -> x0, blocking collectives: 36.4 us -> none  [section_sum(): return lax.psum(v, 'section')]
  transfers between devices with their start and end apart: 31 -> 0, of which waited for: 20 -> 0; matrix products, arithmetic and copies ran while one was open for 11% -> 0% of each run, Pallas kernels for 0% -> 0%
where the time goes in v2:
time: 665 us; the launch traced here: 653 us
  Pallas kernels  436 us (66%)
  matrix products  97.2 us (15%)
  local copies, waits for them, and re-layouts  72.5 us (11%)
  other arithmetic  44.6 us (7%)
    pallas_call x19, Pallas kernels, call(): pl.pallas_call(kernel, out_shape=out_shape, in_specs=in_specs, out_specs=...  436 us
    dot_general x8, matrix products, dot_nt(): lax.dot_general(left, right, (((1,), (1,)), ((), ())), preferred_element_...  27.4 us
    unnamed x138, local copies, waits for them, and re-layouts  26.1 us
    dot_general x8, matrix products, dot_tn(): lax.dot_general(left, right, (((0,), (0,)), ((), ())), preferred_element_...  25.9 us
    dot_general x8, matrix products, dot(): return jnp.dot(left, right, preferred_element_type=F32)  22.8 us

profile of v2, /device:TPU:12, one launch (start us, length us, event | category | flops | bytes accessed | tf_op | source)
XLA Modules:
  0.0 652.8 jit_solution(235646277506323600)
XLA Ops:
  8.7 4.1 copy.90
  12.7 3.9 copy.91
  16.7 4.1 copy.92
  20.7 3.9 copy.93
  24.7 82.7 %shard_map.280 = (bf16[8,4,32,768]{3,2,1,0:T(8,128)(2,1)}, bf16[8,4,32,1024]{3,2,1,0:T(8,128)(2,1)}, f32[8,4,8,128]{3,2,1,0:T(8,128)}, bf16[8,32,1024]{2,1,0:T(8...) custom-call(bf16[4,32,768]{2,1,0:T(8,128)(2,1)} %reshape.569.qkv, ...), custom_call_target="tpu_custom_call" | custom-call | tf_op jit(solution)/shard_map/pallas_call | solution.py:45
  108.3 3.2 copy.104
  111.8 2.8 copy.95
  120.1 3.3 fusion.139
  127.8 12.0 %shard_map.281 = f32[512,256]{1,0:T(8,128)} custom-call(bf16[512,1024]{1,0:T(8,128)(2,1)} %convolution_convert_fusion.6.refs_0_), custom_call_target="tpu_custom_call" | custom-call | tf_op jit(solution)/shard_map/pallas_call | solution.py:45
  141.6 11.0 %shard_map.282 = bf16[512,1024]{1,0:T(8,128)(2,1)} custom-call(bf16[512,256]{1,0:T(8,128)(2,1)} %add_convert_fusion.5.q), custom_call_target="tpu_custom_call" | custom-call | tf_op jit(solution)/shard_map/pallas_call | solution.py:45
  155.9 4.5 multiply_convert_fusion.7
  162.7 12.1 %shard_map.283 = f32[512,256]{1,0:T(8,128)} custom-call(bf16[512,1024]{1,0:T(8,128)(2,1)} %convolution_convert_fusion.5.refs_0_), custom_call_target="tpu_custom_call" | custom-call | tf_op jit(solution)/shard_map/pallas_call | solution.py:45
  177.1 23.0 %shard_map.284 = bf16[8,80,1024]{2,1,0:T(8,128)(2,1)} custom-call(bf16[8,80,256]{2,1,0:T(8,128)(2,1)} %bitcast.301), custom_call_target="tpu_custom_call" | custom-call | tf_op jit(solution)/shard_map/pallas_call | solution.py:45
  204.5 3.2 multiply_convert_fusion.5
  211.3 13.6 %shard_map.285 = f32[640,256]{1,0:T(8,128)} custom-call(bf16[640,1024]{1,0:T(8,128)(2,1)} %fusion.57.refs_0_), custom_call_target="tpu_custom_call" | custom-call | tf_op jit(solution)/shard_map/pallas_call | solution.py:45
  226.9 12.6 %shard_map.286 = bf16[640,1024]{1,0:T(8,128)(2,1)} custom-call(bf16[640,256]{1,0:T(8,128)(2,1)} %fusion.88.q), custom_call_target="tpu_custom_call" | custom-call | tf_op jit(solution)/shard_map/pallas_call | solution.py:45
  241.7 5.1 multiply_convert_fusion.3
  247.8 21.6 %shard_map.289 = bf16[8,80,1024]{2,1,0:T(8,128)(2,1)} custom-call(bf16[8,80,256]{2,1,0:T(8,128)(2,1)} %bitcast.302), custom_call_target="tpu_custom_call" | custom-call | tf_op jit(solution)/shard_map/pallas_call | solution.py:45
  274.0 3.7 multiply_reduce_fusion.3
  282.2 13.6 %shard_map.287 = f32[640,256]{1,0:T(8,128)} custom-call(bf16[640,1024]{1,0:T(8,128)(2,1)} %fusion.60.refs_0_), custom_call_target="tpu_custom_call" | custom-call | tf_op jit(solution)/shard_map/pallas_call | solution.py:45
  298.0 14.0 %shard_map.290 = (f32[640,256]{1,0:T(8,128)}, f32[8,640]{1,0:T(8,128)}) custom-call(bf16[640,1024]{1,0:T(8,128)(2,1)} %get-tuple-element.114.refs_0_, f32[8,640]{1,0:T(8,128)} %select_maximum_fusion.2.refs_1_), custom_call_target="tpu_custom_call" | custom-call | tf_op jit(solution)/shard_map/pallas_call | solution.py:45
  312.8 3.2 multiply_reduce_fusion.9
  316.0 12.6 %shard_map.291 = bf16[640,1024]{1,0:T(8,128)(2,1)} custom-call(bf16[640,256]{1,0:T(8,128)(2,1)} %get-tuple-element.106.q), custom_call_target="tpu_custom_call" | custom-call | tf_op jit(solution)/shard_map/pallas_call | solution.py:45
  328.6 5.1 fusion.22
  333.8 3.8 multiply_reduce_fusion.2
  338.2 14.0 %shard_map.292 = (f32[640,256]{1,0:T(8,128)}, f32[8,640]{1,0:T(8,128)}) custom-call(bf16[640,1024]{1,0:T(8,128)(2,1)} %get-tuple-element.113.refs_0_, f32[8,640]{1,0:T(8,128)} %select_maximum_fusion.1.refs_1_), custom_call_target="tpu_custom_call" | custom-call | tf_op jit(solution)/shard_map/pallas_call | solution.py:45
  353.7 3.4 multiply_reduce_fusion.10
  357.1 12.6 %shard_map.288 = bf16[8,80,256]{2,1,0:T(8,128)(2,1)} custom-call(bf16[8,80,256]{2,1,0:T(8,128)(2,1)} %bitcast.294), custom_call_target="tpu_custom_call" | custom-call | tf_op jit(solution)/shard_map/pallas_call | solution.py:45
  371.8 11.6 %shard_map.293 = bf16[8,80,256]{2,1,0:T(8,128)(2,1)} custom-call(bf16[8,80,256]{2,1,0:T(8,128)(2,1)} %bitcast.293), custom_call_target="tpu_custom_call" | custom-call | tf_op jit(solution)/shard_map/pallas_call | solution.py:45
  385.6 11.1 %shard_map.294 = bf16[512,1024]{1,0:T(8,128)(2,1)} custom-call(bf16[512,256]{1,0:T(8,128)(2,1)} %bitcast.308), custom_call_target="tpu_custom_call" | custom-call | tf_op jit(solution)/shard_map/pallas_call | solution.py:45
  396.7 4.6 fusion.34
  401.4 3.1 multiply_reduce_fusion.8
  405.1 12.3 %shard_map.295 = (f32[512,256]{1,0:T(8,128)}, f32[8,512]{1,0:T(8,128)}) custom-call(bf16[512,1024]{1,0:T(8,128)(2,1)} %get-tuple-element.116.refs_0_, f32[8,512]{1,0:T(8,128)} %select_maximum_fusion.5.refs_1_), custom_call_target="tpu_custom_call" | custom-call | tf_op jit(solution)/shard_map/pallas_call | solution.py:45
  420.5 11.1 %shard_map.296 = bf16[512,1024]{1,0:T(8,128)(2,1)} custom-call(bf16[512,256]{1,0:T(8,128)(2,1)} %get-tuple-element.112.q), custom_call_target="tpu_custom_call" | custom-call | tf_op jit(solution)/shard_map/pallas_call | solution.py:45
  435.4 4.4 fusion.74
  440.2 4.4 fusion.71
  447.6 3.0 multiply_reduce_fusion.7
  451.2 12.3 %shard_map.297 = (f32[512,256]{1,0:T(8,128)}, f32[8,512]{1,0:T(8,128)}) custom-call(bf16[512,1024]{1,0:T(8,128)(2,1)} %get-tuple-element.115.refs_0_, f32[8,512]{1,0:T(8,128)} %select_maximum_fusion.4.refs_1_), custom_call_target="tpu_custom_call" | custom-call | tf_op jit(solution)/shard_map/pallas_call | solution.py:45
  474.1 2.6 convolution_convert_fusion
  477.5 5.0 convolution_convert_fusion.3
  482.6 3.4 convolution_convert_fusion.2
  486.0 122.4 %shard_map.298 = (bf16[4,32,768]{2,1,0:T(8,128)(2,1)}, bf16[4,32,1024]{2,1,0:T(8,128)(2,1)}, f32[32,1024]{1,0:T(8,128)}, f32[128,1024]{1,0:T(8,128)}, f32[8,128]...) custom-call(bf16[8,128,768]{2,1,0:T(8,128)(2,1)} %bitcast.277, ...), custom_call_target="tpu_custom_call" | custom-call | tf_op jit(solution)/shard_map/pallas_call | solution.py:45
  615.6 5.4 copy.122
  621.0 5.7 copy.124
  626.7 5.3 convolution_bitcast_fusion.1
  634.5 5.3 copy.123
  639.8 5.7 copy.125
  645.6 5.4 convolution_bitcast_fusion
  (257 shorter events, 93.6 us)
Async XLA Ops:
  0.6 270.6 %copy-start = (bf16[1,1024,1024]{2,1,0:T(8,128)(2,1)S(1)}, bf16[1,1024,1024]{2,1,0:T(8,128)(2,1)}, u32[]{:S(2)}) copy-start(bf16[1,1024,1024]{2,1,0:T(8,128)(2,1)} %param.33) | copy-start | bytes 6291460
  111.5 3.1 copy-start.13
  117.7 5.6 copy-start.26
  119.5 3.8 copy-start.36
  120.1 5.2 copy-start.34
  123.3 3.0 copy-start.31
  125.6 14.2 %copy-start.29 = (bf16[2,256,256]{2,1,0:T(8,128)(2,1)S(1)}, bf16[2,256,256]{2,1,0:T(8,128)(2,1)}, u32[]{:S(2)}) copy-start(bf16[2,256,256]{2,1,0:T(8,128)(2,1)} %param.17) | copy-start | bytes 786436
  152.7 3.2 copy-start.8
  155.9 4.5 copy-start.44
  160.4 2.3 copy-start.56
  160.4 14.3 %copy-start.19 = (bf16[512,256]{1,0:T(8,128)(2,1)S(1)}, bf16[512,256]{1,0:T(8,128)(2,1)}, u32[]{:S(2)}) copy-start(bf16[512,256]{1,0:T(8,128)(2,1)} %add_convert_fusion.5.q) | copy-start | bytes 786436
  162.7 13.2 %copy-start.41 = (s32[2,256,1]{1,2,0:T(1,128)S(1)}, s32[2,256,1]{1,2,0:T(1,128)}, u32[]{:S(2)}) copy-start(s32[2,256,1]{1,2,0:T(1,128)} %param.19) | copy-start | bytes 6148
  204.5 4.3 copy-start.43
  241.7 5.1 copy-start.39
  269.4 2.1 copy-start.58
  271.6 2.4 copy-start.4
  271.6 2.5 copy-start.47
  274.0 3.7 copy-start.51
  274.0 3.7 copy-start.6
  282.2 13.6 %copy-start.11 = (bf16[640,256]{1,0:T(8,128)(2,1)S(1)}, bf16[640,256]{1,0:T(8,128)(2,1)}, u32[]{:S(2)}) copy-start(bf16[640,256]{1,0:T(8,128)(2,1)} %fusion.88.q) | copy-start | bytes 983044
  328.6 5.1 copy-start.46
  333.7 3.8 copy-start.53
  333.7 19.9 %copy-start.10 = (f32[640,256]{1,0:T(8,128)S(1)}, f32[640,256]{1,0:T(8,128)}, u32[]{:S(2)}) copy-start(f32[640,256]{1,0:T(8,128)} %shard_map.287) | copy-start | bytes 1966084
  333.7 19.9 %copy-start.15 = (bf16[640,256]{1,0:T(8,128)(2,1)S(1)}, bf16[640,256]{1,0:T(8,128)(2,1)}, u32[]{:S(2)}) copy-start(bf16[640,256]{1,0:T(8,128)(2,1)} %get-tuple-element.106.q) | copy-start | bytes 983044
  396.7 4.6 copy-start.9
  396.7 4.6 copy-start.22
  401.3 3.2 copy-start.49
  401.3 17.0 %copy-start.30 = (bf16[2,256,256]{2,1,0:T(8,128)(2,1)S(1)}, bf16[2,256,256]{2,1,0:T(8,128)(2,1)}, u32[]{:S(2)}) copy-start(bf16[2,256,256]{2,1,0:T(8,128)(2,1)} %convolution_convert_fusion.14) | copy-start | bytes 786436
  404.5 27.1 %copy-start.32 = (bf16[8,32,1024]{2,1,0:T(8,128)(2,1)S(1)}, bf16[8,32,1024]{2,1,0:T(8,128)(2,1)}, u32[]{:S(2)}) copy-start(bf16[8,32,1024]{2,1,0:T(8,128)(2,1)} %get-tuple-element.41) | copy-start | bytes 1572868
  420.5 13.1 %copy-start.27 = (bf16[2,256,4,64]{1,3,2,0:T(8,128)(2,1)S(1)}, bf16[2,256,4,64]{1,3,2,0:T(8,128)(2,1)}, u32[]{:S(2)}) copy-start(bf16[2,256,4,64]{1,3,2,0:T(8,128)(2,1)} %copy-done.26) | copy-start | bytes 786436
  433.4 2.1 copy-start.37
  435.4 4.8 copy-start.35
  445.0 2.6 copy-start.14
  445.0 2.6 copy-start.24
  447.6 16.7 %copy-start.18 = (bf16[512,256]{1,0:T(8,128)(2,1)S(1)}, bf16[512,256]{1,0:T(8,128)(2,1)}, u32[]{:S(2)}) copy-start(bf16[512,256]{1,0:T(8,128)(2,1)} %get-tuple-element.112.q) | copy-start | bytes 786436
  471.0 3.1 copy-start.28
  471.0 3.1 copy-start.57
  474.1 3.4 copy-start.54
  477.5 5.1 copy-start.5
  477.5 5.1 copy-start.52
  608.5 3.8 copy-start.38
  608.5 4.7 copy-start.21
  621.0 5.7 copy-start.25
  626.7 5.3 copy-start.20
  639.8 5.7 copy-start.7
  645.5 5.4 copy-start.40
  645.5 6.1 copy-start.33
  645.5 6.9 %copy-start.1 = (bf16[1,1024,1024]{2,1,0:T(8,128)(2,1)S(1)}, bf16[1,1024,1024]{2,1,0:T(8,128)(2,1)}, u32[]{:S(2)}) copy-start(bf16[1,1024,1024]{2,1,0:T(8,128)(2,1)} %param.33) | copy-start | bytes 6291460
  (11 other events, 16.0 us)

commit v3 on v2

--- a/solution.py
+++ b/solution.py
@@ -256,16 +256,29 @@
 
     pl.semaphore_wait(barrier, 4 + jnp.minimum(a, 1) + jnp.minimum(length - 1 - a, 1))
 
-    cuts = ((qkv, st_qkv), (inn, st_in), (vec, st_vec))
-    sent, locals_ = [], []
-    for i, (src, stage) in enumerate(cuts):
-        for k, p in enumerate(peers):
-            c = push(src.at[p] if i < 2 else src, stage.at[me], cut_s.at[i, k], cut_r.at[i, k], {"section": p})
+    hid = o_first.shape[2]
+    width = 4 * QUARTER
+    sent, local_cuts = [], []
+
+    def part_of(src, start, count):
+        return src.at[:, pl.ds(pl.multiple_of(start, 128), count)]
+
+    def cuts_for(p):
+        got = [
+            (0, part_of(qkv, j * width + p * QUARTER, QUARTER), st_qkv.at[me, :, pl.ds(j * QUARTER, QUARTER)])
+            for j in range(3)
+        ]
+        return got + [(1, part_of(inn, p * hid, hid), st_in.at[me]), (2, vec, st_vec.at[me])]
+
+    for k, p in enumerate(peers):
+        for n, (i, src, dst) in enumerate(cuts_for(p)):
+            c = push(src, dst, cut_s.at[n, k], cut_r.at[n, k], {"section": p})
             c.start()
-            sent.append(c)
-        c = pltpu.make_async_copy(src.at[me] if i < 2 else src, stage.at[me], loc.at[i])
+            sent.append((i, c))
+    for n, (i, src, dst) in enumerate(cuts_for(me)):
+        c = pltpu.make_async_copy(src, dst, loc.at[11 + n])
         c.start()
-        locals_.append(c)
+        local_cuts.append((i, c))
     tok_c = [
         push(tok, o_tok.at[:, columns(me)], tok_s.at[k], tok_r.at[k], {"section": p})
         for k, p in enumerate((across, beside))
@@ -276,13 +289,13 @@
     own_tok.start()
     late = [own_tok]
     for i, (src, dst) in enumerate(((first, o_first), (second, o_second))):
-        c = pltpu.make_async_copy(src.at[me], dst.at[me], loc.at[4 + i])
+        c = pltpu.make_async_copy(part_of(src, me * hid, hid), dst.at[me], loc.at[4 + i])
         c.start()
         late.append(c)
     exp_c = []
     for i, (src, dst) in enumerate(((first, o_first), (second, o_second))):
         for k, p in enumerate((across, diagonal, beside)):
-            c = push(src.at[p], dst.at[me], exp_s.at[i, k], exp_r.at[i, k], {"section": p})
+            c = push(part_of(src, p * hid, hid), dst.at[me], exp_s.at[i, k], exp_r.at[i, k], {"section": p})
             c.start()
             exp_c.append(c)
 
@@ -295,11 +308,14 @@
     )
     staged = {0: 0, 2: 1, 4: 2}
 
+    def place(i, which):
+        dst = lines[i][1]
+        return dst.at[:, which] if i in staged else dst.at[which]
+
     def item(i, which, kind, to, own=False):
-        src, dst, _ = lines[i]
-        return push(
-            src if own else dst.at[which], dst.at[which], line_s.at[kind, i, which], line_r.at[i, which], {"wide": to}
-        )
+        src, _, _ = lines[i]
+        spot = place(i, which)
+        return push(src if own else spot, spot, line_s.at[kind, i, which], line_r.at[i, which], {"wide": to})
 
     up, down, pair = 0, 1, 2
 
@@ -320,13 +336,15 @@
 
     for i, (src, dst, _) in enumerate(lines):
         if i in staged:
-            j = staged[i]
-            for k in range(3):
-                sent[3 * j + k].wait_recv()
-            locals_[j].wait()
+            for j, c in sent:
+                if j == staged[i]:
+                    c.wait_recv()
+            for j, c in local_cuts:
+                if j == staged[i]:
+                    c.wait()
         for kind in (up, down, pair):
             along(i, w, kind, True, start)
-        c = pltpu.make_async_copy(src, dst.at[w], loc.at[6 + i])
+        c = pltpu.make_async_copy(src, place(i, w), loc.at[6 + i])
         c.start()
         late.append(c)
     tok_c[0].wait_recv()
@@ -386,7 +404,7 @@
         return carry
 
     lax.fori_loop(1, length, finish, 0)
-    for c in sent:
+    for _, c in sent:
         c.wait_send()
     tok_c[0].wait_send()
     tok_c[1].wait()
@@ -398,14 +416,17 @@
 
 
 def weights_call(qkv, inn, vec, outw, backw, first, second, tok, wide, collective_id):
+    small = qkv.shape[0]
+    hid = inn.shape[1] // 4
+    cut = 3 * QUARTER
     outs = [
-        ((wide, *qkv.shape), BF16),
-        ((wide, *inn.shape), BF16),
-        ((wide, 4, *vec.shape), F32),
+        ((4, wide, small, cut), BF16),
+        ((4, wide, small, hid), BF16),
+        ((4, wide, *vec.shape), F32),
         ((wide, *outw.shape), BF16),
         ((wide, *backw.shape), BF16),
-        (first.shape, BF16),
-        (second.shape, BF16),
+        ((4, first.shape[0], hid), BF16),
+        ((4, first.shape[0], hid), BF16),
         ((tok.shape[0], 4 * QUARTER), BF16),
     ]
     return call(
@@ -414,12 +435,12 @@
         [ANY] * 8,
         tuple([ANY] * 8),
         [
-            pltpu.VMEM(qkv.shape, BF16),
-            pltpu.VMEM(inn.shape, BF16),
+            pltpu.VMEM((4, small, cut), BF16),
+            pltpu.VMEM((4, small, hid), BF16),
             pltpu.VMEM((4, *vec.shape), F32),
-            DMA((11,)),
-            DMA((3, 3)),
-            DMA((3, 3)),
+            DMA((16,)),
+            DMA((5, 3)),
+            DMA((5, 3)),
             DMA((3,)),
             DMA((3,)),
             DMA((3, 5, wide)),
@@ -443,6 +464,10 @@
 
 
 def add_rows(dst, left, right):
+    if len(dst.shape) == 3:
+        for j in range(dst.shape[0]):
+            add_rows(dst.at[j], left.at[j], right.at[j])
+        return
     rows = dst.shape[0]
     step = min(rows, GROUP)
 
@@ -454,56 +479,85 @@
     lax.fori_loop(0, rows // step, one, 0)
 
 
-def gradients_kernel(*refs):
-    count = 5
-    src = refs[:count]
-    first, second = refs[count : count + 2]
-    o_qkv, o_in, o_out, o_back, o_gain, o_first, o_second = refs[7:14]
-    acc = refs[14:19]
-    line_in = refs[19:24]
-    pair_in = refs[24:29]
-    (st_qkv, st_in, loc, exp_s, exp_r, cut_s, cut_r, pair_s, pair_r, line_s, line_r) = refs[29:]
+def attention_pair(pair, qkv, mask):
+    q2, k2, v2 = (qkv(j * QUARTER + pair * 128) for j in range(3))
+    got = []
+    for h in range(2):
+        q, k, v = (x[:, h * HEAD_SIZE : (h + 1) * HEAD_SIZE] for x in (q2, k2, v2))
+        scores = jnp.where(mask > 0.0, dot_nt(q, k) * HEAD_SIZE ** (-0.5), -1e30)
+        expo = jnp.exp(scores - jnp.max(scores, axis=-1, keepdims=True))
+        got.append((q, k, v, expo / jnp.sum(expo, axis=-1, keepdims=True)))
+    return got
+
+
+def row_norm(v):
+    centred = v - jnp.mean(v, axis=-1, keepdims=True)
+    scale = lax.rsqrt(jnp.mean(centred * centred, axis=-1, keepdims=True) + 1e-05)
+    return centred * scale, scale
+
+
+def line_of_wide():
+    w = lax.axis_index("wide")
+    length = lax.axis_size("wide") // 2
+    return w, length, lax.div(w, 2), lax.rem(w, 2)
+
+
+def greet_line(section_peers, all_wide):
+    w, length, a, b = line_of_wide()
+    barrier = pltpu.get_barrier_semaphore()
+    for p in section_peers:
+        pl.semaphore_signal(barrier, inc=1, device_id={"section": p}, device_id_type=MESH)
+    if all_wide:
+        for j in range(1, 2 * length):
+            pl.semaphore_signal(
+                barrier, inc=1, device_id={"wide": lax.rem(w + j, 2 * length)}, device_id_type=MESH
+            )
+        pl.semaphore_wait(barrier, len(section_peers) + 2 * length - 1)
+        return
+    pl.semaphore_signal(barrier, inc=1, device_id={"wide": 2 * a + 1 - b}, device_id_type=MESH)
+
+    @pl.when(a > 0)
+    def _():
+        pl.semaphore_signal(barrier, inc=1, device_id={"wide": w - 2}, device_id_type=MESH)
+
+    @pl.when(a < length - 1)
+    def _():
+        pl.semaphore_signal(barrier, inc=1, device_id={"wide": w + 2}, device_id_type=MESH)
+
+    pl.semaphore_wait(barrier, len(section_peers) + 1 + jnp.minimum(a, 1) + jnp.minimum(length - 1 - a, 1))
+
+
+def tail_kernel(*refs):
+    (g_in, g_back, first, second, d_att, tok, n1, qkv, mixed, w_qkv, w_out, mask, gain, gain_d) = refs[:14]
+    o_qkv, o_in, o_out, o_back, o_gain, o_first, o_second, o_tok = refs[14:22]
+    g_qkv, g_out = refs[22:24]
+    acc = refs[24:28]
+    line_in = refs[28:32]
+    pair_in = refs[32:36]
+    (d_mix, d_qkv, part, unit, scales, stats, stats_in, stats_mid, stats_far, near_in, far, far_in, gains, gains_in) = refs[36:50]
+    (loc, exp_s, exp_r, cut_s, cut_r, pair_s, pair_r, line_s, line_r, s1, r1, s2, r2, st_s, st_r, gn_s, gn_r) = refs[50:]
+    src = (g_qkv, g_in, g_out, g_back)
+    pair_first = (True, True, False, False)
     me, beside, across = section_places()
     diagonal = beside + across - me
-    w = lax.axis_index("wide")
-    length = lax.axis_size("wide") // 2
-    a, b = lax.div(w, 2), lax.rem(w, 2)
+    core, side = lax.rem(me, 2), lax.div(me, 2)
+    w, length, a, b = line_of_wide()
     other = 1 - b
     mate = {"wide": 2 * a + other}
     peers = [beside, across, diagonal]
-    barrier = pltpu.get_barrier_semaphore()
-    for p in peers:
-        pl.semaphore_signal(barrier, inc=1, device_id={"section": p}, device_id_type=MESH)
-    pl.semaphore_signal(barrier, inc=1, device_id=mate, device_id_type=MESH)
-
-    @pl.when(a > 0)
-    def _():
-        pl.semaphore_signal(barrier, inc=1, device_id={"wide": w - 2}, device_id_type=MESH)
-
-    @pl.when(a < length - 1)
-    def _():
-        pl.semaphore_signal(barrier, inc=1, device_id={"wide": w + 2}, device_id_type=MESH)
-
-    pl.semaphore_wait(barrier, 4 + jnp.minimum(a, 1) + jnp.minimum(length - 1 - a, 1))
-
-    pair_first = (True, True, False, False, False)
+    greet_line(peers, True)
+    hid = first.shape[2]
+    rows = mask.shape[1]
+    micro = mask.shape[0]
+    late = []
+
+    def spot(ref, which, count):
+        return ref.at[:, pl.ds(pl.multiple_of(which * count, count), count)]
 
     def pair_copy(i, there):
-        return push(src[i].at[2 * there + other], pair_in[i].at[there], pair_s.at[i, there], pair_r.at[i, there], mate)
-
-    for i in range(count):
-        if pair_first[i]:
-            lax.fori_loop(0, length, lambda t, c, i=i: (pair_copy(i, t).start(), c)[1], 0)
-
-    late = []
-    for i, (s, d) in enumerate(((first, o_first), (second, o_second))):
-        c = pltpu.make_async_copy(s.at[me], d.at[me], loc.at[i])
-        c.start()
-        late.append(c)
-        for k, p in enumerate((across, diagonal, beside)):
-            c = push(s.at[p], d.at[me], exp_s.at[i, k], exp_r.at[i, k], {"section": p})
-            c.start()
-            late.append(c)
+        return push(
+            src[i].at[:, 2 * there + other], pair_in[i].at[there], pair_s.at[i, there], pair_r.at[i, there], mate
+        )
 
     def slots(i, there):
         if pair_first[i]:
@@ -513,18 +567,15 @@
     def line_copy(i, block, to_block, to):
         return push(acc[i].at[block], line_in[i].at[to_block], line_s.at[i, block], line_r.at[i, to_block], {"wide": to})
 
-    def wide_of(i):
-        return 1 if pair_first[i] else 2
-
     def ready(i, there, block, own):
         if pair_first[i]:
             pair_copy(i, there).wait_recv()
-            add_rows(acc[i].at[block], src[i].at[own], pair_in[i].at[there])
+            add_rows(acc[i].at[block], src[i].at[:, own], pair_in[i].at[there])
         else:
             acc[i][block] = src[i][own]
 
     def flow(i, there, from_edge, to):
-        n = wide_of(i)
+        n = 1 if pair_first[i] else 2
         for j, (block, own) in enumerate(slots(i, there)):
             ready(i, there, block, own)
 
@@ -539,24 +590,30 @@
                 target = jnp.where(there == a + 1, n * length + j, block)
                 line_copy(i, block, target, w + 2).start()
 
-    def step(t, carry):
-        high = length - 1 - t
-        for i in range(count):
-
-            @pl.when(t < a)
-            def _():
-                flow(i, t, a < length - 1, "down")
-
-            @pl.when(high > a)
-            def _():
-                flow(i, high, a > 0, "up")
-
-        return carry
-
-    lax.fori_loop(0, length, step, 0)
-    finals = []
-    for i in range(count):
-        n = wide_of(i)
+    def pairs(i):
+        lax.fori_loop(0, length, lambda t, c: (pair_copy(i, t).start(), c)[1], 0)
+
+    def steps(group, start, stop):
+        def step(t, carry):
+            high = length - 1 - t
+            for i in group:
+
+                @pl.when(t < a)
+                def _():
+                    flow(i, t, a < length - 1, "down")
+
+                @pl.when(high > a)
+                def _():
+                    flow(i, high, a > 0, "up")
+
+            return carry
+
+        lax.fori_loop(start, stop, step, 0)
+
+    finals = {}
+
+    def own_block(i):
+        n = 1 if pair_first[i] else 2
         for j, (block, own) in enumerate(slots(i, a)):
             ready(i, a, block, own)
 
@@ -573,30 +630,167 @@
         if not pair_first[i]:
             c = push(acc[i].at[2 * a + other], pair_in[i].at[0], pair_s.at[i, 0], pair_r.at[i, 0], mate)
             c.start()
-            finals.append(c)
-        else:
-            out, k0 = ((o_qkv, 0), (o_in, 1))[i]
-            st = (st_qkv, st_in)[i]
-            small = st.shape[1]
-            for p in range(4):
-                st[p] = acc[i][a, pl.ds(p * small, small)]
-            for k, p in enumerate(peers):
-                c = push(st.at[p], out.at[me], cut_s.at[i, k], cut_r.at[i, k], {"section": p})
+            finals[i] = c
+            return
+        block = acc[i].at[a]
+
+        def cut(p):
+            if i == 1:
+                return [(block.at[p], spot(o_in, me, hid))]
+            third = [pl.ds(j * QUARTER, QUARTER) for j in range(3)]
+            return [(block.at[p, :, third[j]], spot(o_qkv, 4 * j + me, QUARTER)) for j in range(3)]
+
+        for k, p in enumerate(peers):
+            for j, (here, there) in enumerate(cut(p)):
+                n = 3 * i + j
+                c = push(here, there, cut_s.at[n, k], cut_r.at[n, k], {"section": p})
                 c.start()
                 late.append(c)
-            c = pltpu.make_async_copy(st.at[me], out.at[me], loc.at[2 + i])
+        for j, (here, there) in enumerate(cut(me)):
+            c = pltpu.make_async_copy(here, there, loc.at[2 + 3 * i + j])
             c.start()
             late.append(c)
-    for i, out in ((2, o_out), (3, o_back), (4, o_gain)):
-        finals[i - 2].wait_recv()
+
+    pairs(1)
+    for i, (s, d) in enumerate(((first, o_first), (second, o_second))):
+        c = pltpu.make_async_copy(s.at[me], spot(d, me, hid), loc.at[i])
+        c.start()
+        late.append(c)
+        for k, p in enumerate((across, diagonal, beside)):
+            c = push(s.at[p], spot(d, me, hid), exp_s.at[i, k], exp_r.at[i, k], {"section": p})
+            c.start()
+            late.append(c)
+    group = (3, 1)
+    cuts = [k * length // 4 for k in range(5)]
+    small = g_out.shape[1]
+    wide = 2 * length
+
+    def store_blocks(ref, index, value):
+        for j in range(wide):
+            piece = value[j * small : (j + 1) * small].astype(BF16)
+            if index is None:
+                ref[j] = piece
+            else:
+                ref[index, j] = piece
+
+    for m in range(micro):
+        at = pl.ds(m * rows, rows)
+        d_mix[at] = dot_nt(d_att[at], w_out[...]).astype(BF16)
+    store_blocks(g_out, None, dot_tn(mixed[...], d_att[...]))
+    steps(group, cuts[0], cuts[1])
+
+    def micro_back(m, carry):
+        at = pl.ds(pl.multiple_of(m * rows, rows), rows)
+        for pair in range(2):
+            heads = attention_pair(pair, lambda c: qkv[at, pl.ds(c, 128)], mask[m])
+            d_pair = d_mix[at, pl.ds(pair * 128, 128)]
+            grads = []
+            for h, (q, k, v, probs) in enumerate(heads):
+                d_out = d_pair[:, h * HEAD_SIZE : (h + 1) * HEAD_SIZE]
+                d_probs = dot_nt(d_out, v)
+                delta = jnp.sum(probs * d_probs, axis=-1, keepdims=True)
+                d_scores = (probs * (d_probs - delta) * HEAD_SIZE ** (-0.5)).astype(BF16)
+                grads.append((dot(d_scores, k), dot_tn(d_scores, q), dot_tn(probs.astype(BF16), d_out)))
+            for j in range(3):
+                both = jnp.concatenate([grads[0][j], grads[1][j]], axis=1).astype(BF16)
+                d_qkv[at, pl.ds(j * QUARTER + pair * 128, 128)] = both
+        return carry
+
+    for m in range(micro):
+        micro_back(m, 0)
+        steps(group, cuts[1 + m], cuts[2 + m])
+    for p in range(4):
+        store_blocks(g_qkv, p, dot_tn(n1[:, pl.ds(p * QUARTER, QUARTER)], d_qkv[...]))
+    pairs(0)
+    steps((2,), 0, length)
+
+    count = d_att.shape[0]
+    chunk = 128
+    chunks = count // chunk
+    lane = lax.broadcasted_iota(jnp.int32, (chunk, 128), 1)
+    beside_core = 1 - core
+    sends = []
+    for k in range(chunks):
+        at = pl.ds(k * chunk, chunk)
+        u, scale = row_norm(tok[at].astype(F32))
+        unit[at] = u
+        scales[at] = jnp.broadcast_to(scale, (chunk, 128))
+        d_normed = dot_nt(d_qkv[at], w_qkv[...])
+        part[at] = d_normed.astype(BF16)
+        d_unit = d_normed * gain[...]
+        sum_a = jnp.sum(d_unit, axis=-1, keepdims=True)
+        sum_b = jnp.sum(d_unit * u, axis=-1, keepdims=True)
+        both = jnp.where(lane == 0, sum_a, jnp.where(lane == 1, sum_b, 0.0))
+        stats[:, at] = both.T[:8]
+        for which, half in ((1, 1 - side), (0, side)):
+            c = push(
+                part.at[at, columns(2 * half + beside_core)],
+                near_in.at[which, at],
+                s1.at[which, k],
+                r1.at[which, k],
+                {"section": beside},
+            )
+            c.start()
+            sends.append(c)
+    st1 = push(stats, stats_in, st_s.at[0], st_r.at[0], {"section": beside})
+    st1.start()
+    crossing = []
+    for k in range(chunks):
+        at = pl.ds(k * chunk, chunk)
+        sends[2 * k].wait()
+        far[at] = (part[at, columns(2 * (1 - side) + core)].astype(F32) + near_in[1, at].astype(F32)).astype(BF16)
+        c = push(far.at[at], far_in.at[at], s2.at[k], r2.at[k], {"section": across})
+        c.start()
+        crossing.append(c)
+    st1.wait()
+    stats_mid[...] = stats[...] + stats_in[...]
+    st2 = push(stats_mid, stats_far, st_s.at[1], st_r.at[1], {"section": across})
+    st2.start()
+    steps(group, cuts[3], cuts[4])
+    steps((0,), 0, length)
+    st2.wait()
+    stats[...] = (stats_mid[...] + stats_far[...]) * (1.0 / gain.shape[1])
+    total = jnp.zeros((1, QUARTER), F32)
+    gain_q = gain[:, columns(me)]
+    for k in range(chunks):
+        at = pl.ds(k * chunk, chunk)
+        sends[2 * k + 1].wait()
+        near = part[at, columns(me)].astype(F32) + near_in[0, at].astype(F32)
+        crossing[k].wait()
+        d_q = near + far_in[at].astype(F32)
+        u = unit[at, columns(me)]
+        sums = jnp.concatenate([stats[:, at], jnp.zeros((chunk - 8, chunk), F32)], axis=0).T
+        norm = scales[at, pl.ds(0, 1)] * (d_q * gain_q - sums[:, 0:1] - u * sums[:, 1:2])
+        o_tok[at] = d_att[at, columns(me)].astype(F32) + norm
+        total = total + jnp.sum(d_q * u, axis=0, keepdims=True)
+    row = lax.broadcasted_iota(jnp.int32, (8, QUARTER), 0)
+    gains[...] = jnp.where(row == 0, total, jnp.where(row == 1, gain_d[...], 0.0))
+
+    def gain_copy(to, frm):
+        return push(gains, gains_in.at[frm], gn_s.at[to], gn_r.at[frm], {"wide": to})
+
+    for j in range(1, wide):
+        gain_copy(lax.rem(w + j, wide), w).start()
+    for i in (3, 1, 2, 0):
+        own_block(i)
+    gathered = gains[...]
+    for j in range(1, wide):
+        frm = lax.rem(w + j, wide)
+        gain_copy(frm, frm).wait_recv()
+        gathered = gathered + gains_in[frm]
+    o_gain[...] = gathered
+    for i, out in ((3, o_back), (2, o_out)):
+        finals[i].wait_recv()
         add_rows(out, acc[i].at[2 * a + b], pair_in[i].at[0])
-    for c in finals:
+    for c in finals.values():
         c.wait_send()
     for c in late:
         c.wait()
+    for j in range(1, wide):
+        gain_copy(lax.rem(w + j, wide), w).wait_send()
 
     def finish(t, carry):
-        for i in range(count):
+        for i in range(4):
             if pair_first[i]:
                 pair_copy(i, t).wait_send()
 
@@ -610,43 +804,73 @@
     lax.fori_loop(0, length, finish, 0)
 
 
-def gradients_call(dense, first, second, collective_id):
-    wide = dense[0].shape[0]
+def tail_call(g_in, g_back, first, second, d_att, tok, n1, qkv, mixed, w_qkv, w_out, mask, gain, gain_d, collective_id):
+    wide = g_back.shape[0]
     length = wide // 2
-    shapes = [d.shape[1:] for d in dense]
-    kinds = [d.dtype for d in dense]
-    small = shapes[0][0] // 4
-    first_count = [length, length, wide, wide, wide]
-    in_count = [length + 1, length + 1, wide + 2, wide + 2, wide + 2]
-    pair_count = [length, length, 1, 1, 1]
-    outs = [((4, small, shapes[0][1]), BF16), ((4, small, shapes[1][1]), BF16)]
-    outs += [(s, F32) for s in shapes[2:]] + [(first.shape, BF16), (second.shape, BF16)]
-    scratch = [pltpu.VMEM((n, *s), k) for n, s, k in zip(first_count, shapes, kinds)]
-    scratch += [pltpu.VMEM((n, *s), k) for n, s, k in zip(in_count, shapes, kinds)]
-    scratch += [pltpu.VMEM((n, *s), k) for n, s, k in zip(pair_count, shapes, kinds)]
+    small = g_in.shape[2]
+    hid = first.shape[2]
+    count, width = d_att.shape
+    chunks = count // 128
+    shapes = [(4, small, 3 * QUARTER), (4, small, hid), (small, width), g_back.shape[1:]]
+    expert = ((first.shape[1], 4 * hid), BF16)
+    outs = [
+        ((small, 3 * width), BF16),
+        ((small, 4 * hid), BF16),
+        (shapes[2], F32),
+        (shapes[3], F32),
+        ((8, QUARTER), F32),
+        expert,
+        expert,
+        ((count, QUARTER), F32),
+    ]
+    scratch = [pltpu.VMEM((4, wide, small, 3 * QUARTER), BF16), pltpu.VMEM((wide, small, width), BF16)]
+    for counts in (
+        [length, length, wide, wide],
+        [length + 1, length + 1, wide + 2, wide + 2],
+        [length, length, 1, 1],
+    ):
+        scratch += [pltpu.VMEM((n, *s), BF16) for n, s in zip(counts, shapes)]
     scratch += [
-        pltpu.VMEM((4, small, shapes[0][1]), BF16),
-        pltpu.VMEM((4, small, shapes[1][1]), BF16),
-        DMA((4,)),
+        pltpu.VMEM((count, QUARTER), BF16),
+        pltpu.VMEM((count, 3 * QUARTER), BF16),
+        pltpu.VMEM((count, width), BF16),
+        pltpu.VMEM((count, width), F32),
+        pltpu.VMEM((count, 128), F32),
+        pltpu.VMEM((8, count), F32),
+        pltpu.VMEM((8, count), F32),
+        pltpu.VMEM((8, count), F32),
+        pltpu.VMEM((8, count), F32),
+        pltpu.VMEM((2, count, QUARTER), BF16),
+        pltpu.VMEM((count, QUARTER), BF16),
+        pltpu.VMEM((count, QUARTER), BF16),
+        pltpu.VMEM((8, QUARTER), F32),
+        pltpu.VMEM((wide, 8, QUARTER), F32),
+        DMA((8,)),
         DMA((2, 3)),
         DMA((2, 3)),
-        DMA((2, 3)),
-        DMA((2, 3)),
-        DMA((5, length)),
-        DMA((5, length)),
-        DMA((5, wide)),
-        DMA((5, wide + 2)),
+        DMA((4, 3)),
+        DMA((4, 3)),
+        DMA((4, length)),
+        DMA((4, length)),
+        DMA((4, wide)),
+        DMA((4, wide + 2)),
+        DMA((2, chunks)),
+        DMA((2, chunks)),
+        DMA((chunks,)),
+        DMA((chunks,)),
+        DMA((2,)),
+        DMA((2,)),
+        DMA((wide,)),
+        DMA((wide,)),
     ]
     return call(
-        gradients_kernel,
+        tail_kernel,
         tuple(jax.ShapeDtypeStruct(*o) for o in outs),
-        [VM] * 5 + [ANY, ANY],
-        (ANY, ANY, VM, VM, VM, ANY, ANY),
+        [VM, VM, ANY, ANY] + [VM] * 10,
+        (ANY, ANY, VM, VM, VM, ANY, ANY, VM),
         scratch,
         collective_id,
-        *dense,
-        first,
-        second,
+        *(g_in, g_back, first, second, d_att, tok, n1, qkv, mixed, w_qkv, w_out, mask, gain, gain_d),
     )
 
 
@@ -696,6 +920,12 @@
 
 def wide_exchange(slots, spread):
     return exchange_call(slots, spread, id_of("exchange", spread))
+
+
+def allowed_of(lengths, rows):
+    pos = jnp.arange(rows, dtype=jnp.int32)
+    group = pos[None] // lengths[:, None]
+    return ((pos[:, None] >= pos[None, :])[None] & (group[:, :, None] == group[:, None, :])).astype(F32)
 
 
 def attention_probs(queries, keys, lengths):
@@ -741,36 +971,29 @@
     small = qkv_weight.shape[0]
     qkv_cols = qkv_weight.shape[1] // sections
 
-    qkv_cut = (
-        qkv_weight.reshape(small, 3, sections, quarter).transpose(2, 0, 1, 3).reshape(sections, small, qkv_cols)
-    )
-    in_cut = ffn_in.reshape(small, sections, hid).transpose(1, 0, 2)
     vectors = jnp.concatenate([first_gain[0], second_gain[0], centroids[0], attn_gain, ffn_gain]).astype(F32)
     vectors = jnp.pad(vectors, (0, 1024 - vectors.shape[0])).reshape(8, 128)
     tokens_q = tokens_in.reshape(tok_rows, quarter)
 
-    def slice_in(weight):
-        return weight[0].reshape(quarter, sections, hid).transpose(1, 0, 2)
-
     qkv_w, in_w, vectors, out_w, back_w, first_w, second_w, tokens = weights_call(
-        qkv_cut,
-        in_cut,
+        qkv_weight,
+        ffn_in,
         vectors,
         out_weight,
         ffn_back,
-        slice_in(first_in),
-        slice_in(second_in),
+        first_in[0],
+        second_in[0],
         tokens_q,
         wide,
         id_of("weights"),
     )
-    qkv_w = qkv_w.transpose(1, 0, 2, 3).reshape(width, qkv_cols)
-    in_w = in_w.transpose(1, 0, 2, 3).reshape(width, hid)
+    qkv_w = qkv_w.reshape(width, qkv_cols)
+    in_w = in_w.reshape(width, hid)
     out_w = out_w.reshape(quarter, width)
     back_w = back_w.reshape(hid, width)
     first_w = first_w.reshape(width, hid)
     second_w = second_w.reshape(width, hid)
-    vectors = vectors.reshape(wide, sections, 1024).transpose(1, 0, 2)
+    vectors = vectors.reshape(sections, wide, 1024)
     own = lax.dynamic_index_in_dim(vectors, wide_id, axis=1, keepdims=False)
     gain_first = own[:, :quarter].reshape(1, width)
     gain_second = own[:, quarter : 2 * quarter].reshape(1, width)
@@ -876,58 +1099,43 @@
     d_in, d_back, (norm_q, d_gain_ffn, _) = branch_back(gather_quarters(d_fed_q), saved_d, in_w, back_w, gain_ffn)
     d_attended_q = (d_fed_q.astype(F32) + norm_q).astype(BF16)
     d_attended = gather_quarters(d_attended_q)
-    d_out = dot_tn(mixed, d_attended)
-    d_mix = by_head(dot_nt(d_attended, out_w).astype(BF16))
-    d_probs = jnp.einsum("mhqd,mhkd->mhqk", d_mix, values, preferred_element_type=F32)
-    delta = jnp.sum(probs * d_probs, axis=-1, keepdims=True)
-    d_scores = (probs * (d_probs - delta) * HEAD_SIZE ** (-0.5)).astype(BF16)
-    d_queries = jnp.einsum("mhqk,mhkd->mhqd", d_scores, keys, preferred_element_type=F32)
-    d_keys = jnp.einsum("mhqk,mhqd->mhkd", d_scores, queries, preferred_element_type=F32)
-    d_values = jnp.einsum("mhqk,mhqd->mhkd", probs_b, d_mix, preferred_element_type=F32)
-    d_packed = jnp.concatenate([from_head(v) for v in (d_queries, d_keys, d_values)], axis=1).astype(BF16)
-    d_qkv = dot_tn(normed_a, d_packed)
-    norm_q, d_gain_attn, _ = norm_back(dot_nt(d_packed, qkv_w), unit_a, scale_a, gain_attn)
-    tokens_grad = (d_attended_q.astype(F32) + norm_q).reshape(micro, rows, quarter)
-
-    def by_wide(grad):
-        pieces = grad.astype(BF16).reshape(sections, wide, small, grad.shape[1]).transpose(1, 0, 2, 3)
-        return pieces.reshape(wide, sections * small, grad.shape[1])
-
-    def own_in(pieces):
-        return pieces.transpose(1, 0, 2).reshape(1, quarter, sections * hid).astype(F32)
-
-    d_gains = jnp.stack([d_gain_attn.reshape(wide, small), d_gain_ffn.reshape(wide, small)], axis=1)
-    d_gains = jnp.pad(d_gains, ((0, 0), (0, 6), (0, 128 - small)))
-    qkv_grad, ffn_in_grad, out_grad, ffn_back_grad, d_gains, d_first_in, d_second_in = gradients_call(
-        (
-            by_wide(d_qkv),
-            by_wide(d_in),
-            d_out.astype(BF16).reshape(wide, small, width),
-            d_back.astype(BF16).reshape(wide, hid // wide, width),
-            d_gains,
-        ),
+    def by_row(grad):
+        return grad.astype(BF16).reshape(sections, wide, small, grad.shape[1])
+
+    qkv_grad, ffn_in_grad, out_grad, ffn_back_grad, d_gains, d_first_in, d_second_in, tokens_grad = tail_call(
+        by_row(d_in),
+        d_back.astype(BF16).reshape(wide, hid // wide, width),
         d_first_in.astype(BF16).reshape(sections, quarter, hid),
         d_second_in.astype(BF16).reshape(sections, quarter, hid),
-        id_of("gradients"),
-    )
-    qkv_grad = qkv_grad.astype(F32).reshape(sections, small, 3, quarter).transpose(1, 2, 0, 3)
-    qkv_grad = qkv_grad.reshape(small, 3 * width)
-    ffn_in_grad = ffn_in_grad.astype(F32).transpose(1, 0, 2).reshape(small, sections * hid)
+        d_attended,
+        tokens,
+        normed_a,
+        packed,
+        mixed,
+        qkv_w,
+        out_w,
+        allowed_of(seq_lengths, rows),
+        gain_attn,
+        d_gain_ffn[None],
+        id_of("tail"),
+    )
+    d_gains = lax.dynamic_slice_in_dim(d_gains, wide_id * small, small, axis=1)
+    tokens_grad = tokens_grad.reshape(micro, rows, quarter)
     return (
         block_out,
         tokens_grad,
-        qkv_grad,
+        qkv_grad.astype(F32),
         out_grad,
-        d_gains[0, :small],
-        ffn_in_grad,
+        d_gains[0],
+        ffn_in_grad.astype(F32),
         ffn_back_grad,
-        d_gains[1, :small],
+        d_gains[1],
         centroids_grad,
         first_gain_grad[None],
-        own_in(d_first_in),
+        d_first_in[None].astype(F32),
         d_first_back[None],
         second_gain_grad[None],
-        own_in(d_second_in),
+        d_second_in[None].astype(F32),
         d_second_back[None],
     )
 

time: 665 us -> 565 us (0.85)
  local copies, waits for them, and re-layouts: 72.5 us -> 19.7 us
  Pallas kernels: 436 us -> 412 us
  matrix products: 97.2 us -> 73.3 us
    pallas_call x19 -> x18, Pallas kernels: 436 us -> 412 us  [call(): pl.pallas_call(kernel, out_shape=out_shape, in_specs=in_specs, out_specs=...]
    unnamed x138 -> x113, local copies, waits for them, and re-layouts: 26.1 us -> 6.99 us
    dot_general x4 -> x0, matrix products: 12.8 us -> none  [the longest x1 4.43 us: body(): jnp.einsum('mhqk,mhqd->mhkd', d_scores, queries, preferred_element_type=F32)]
    convert_element_type x3 -> x0, local copies, waits for them, and re-layouts: 10.9 us -> none  [the longest x2 10.7 us: own_in(): pieces.transpose(1, 0, 2).reshape(1, quarter, sections * hid).astype(F32)]
    reshape x12 -> x2, local copies, waits for them, and re-layouts: 11 us -> 1.86 us  [the longest x1 1.02 us: body(): vectors = vectors.reshape(sections, wide, 1024)]
    another operation x4 -> x0, local copies, waits for them, and re-layouts: 8.04 us -> none  [the longest x2 7.87 us: slice_in(): return weight[0].reshape(quarter, sections, hid).transpose(1, 0, 2)]
    transpose x5 -> x0, local copies, waits for them, and re-layouts: 6.83 us -> none  [the longest x1 3.19 us: body(): in_w = in_w.transpose(1, 0, 2, 3).reshape(width, hid)]
    dot_general x8 -> x6, matrix products: 25.9 us -> 19.9 us  [dot_tn(): lax.dot_general(left, right, (((0,), (0,)), ((), ())), preferred_element_...]
where the time goes in v3:
time: 565 us; the launch traced here: 554 us
  Pallas kernels  412 us (73%)
  matrix products  73.3 us (13%)
  other arithmetic  46.9 us (8%)
  local copies, waits for them, and re-layouts  19.7 us (3%)
    pallas_call x18, Pallas kernels, call(): pl.pallas_call(kernel, out_shape=out_shape, in_specs=in_specs, out_specs=...  412 us
    dot_general x6, matrix products, dot_nt(): lax.dot_general(left, right, (((1,), (1,)), ((), ())), preferred_element_...  22.7 us
    dot_general x8, matrix products, dot(): return jnp.dot(left, right, preferred_element_type=F32)  22.7 us
    dot_general x6, matrix products, dot_tn(): lax.dot_general(left, right, (((0,), (0,)), ((), ())), preferred_element_...  19.9 us

profile of v3, /device:TPU:12, one launch (start us, length us, event | category | flops | bytes accessed | tf_op | source)
XLA Modules:
  0.0 554.2 jit_solution(14316758814069886009)
XLA Ops:
  4.9 81.9 %shard_map.280 = (bf16[4,8,32,768]{3,2,1,0:T(8,128)(2,1)}, bf16[4,8,32,1024]{3,2,1,0:T(8,128)(2,1)}, f32[4,8,8,128]{3,2,1,0:T(8,128)}, bf16[8,32,1024]{2,1,0:T(8...) custom-call(bf16[32,3072]{1,0:T(8,128)(2,1)} %qkv.1, ...), custom_call_target="tpu_custom_call" | custom-call | tf_op jit(solution)/shard_map/pallas_call | solution.py:45
  94.5 3.1 fusion.102
  98.1 2.0 fusion.57
  102.6 12.8 %shard_map.281 = f32[512,256]{1,0:T(8,128)} custom-call(bf16[512,1024]{1,0:T(8,128)(2,1)} %convolution_convert_fusion.5.refs_0_), custom_call_target="tpu_custom_call" | custom-call | tf_op jit(solution)/shard_map/pallas_call | solution.py:45
  115.4 1.8 add_convert_fusion.5.q
  117.2 11.7 %shard_map.282 = bf16[512,1024]{1,0:T(8,128)(2,1)} custom-call(bf16[512,256]{1,0:T(8,128)(2,1)} %add_convert_fusion.5.q), custom_call_target="tpu_custom_call" | custom-call | tf_op jit(solution)/shard_map/pallas_call | solution.py:45
  132.1 4.5 multiply_convert_fusion.6
  136.6 2.3 convolution_convert_fusion.4.refs_0_
  138.8 12.0 %shard_map.283 = f32[512,256]{1,0:T(8,128)} custom-call(bf16[512,1024]{1,0:T(8,128)(2,1)} %convolution_convert_fusion.4.refs_0_), custom_call_target="tpu_custom_call" | custom-call | tf_op jit(solution)/shard_map/pallas_call | solution.py:45
  153.2 23.1 %shard_map.284 = bf16[8,80,1024]{2,1,0:T(8,128)(2,1)} custom-call(bf16[8,80,256]{2,1,0:T(8,128)(2,1)} %bitcast.221), custom_call_target="tpu_custom_call" | custom-call | tf_op jit(solution)/shard_map/pallas_call | solution.py:45
  176.4 2.0 fusion.9
  180.7 3.2 multiply_convert_fusion.5
  185.0 2.6 fusion.49.refs_0_
  187.6 13.6 %shard_map.285 = f32[640,256]{1,0:T(8,128)} custom-call(bf16[640,1024]{1,0:T(8,128)(2,1)} %fusion.49.refs_0_), custom_call_target="tpu_custom_call" | custom-call | tf_op jit(solution)/shard_map/pallas_call | solution.py:45
  201.2 1.9 fusion.65.q
  203.1 12.6 %shard_map.286 = bf16[640,1024]{1,0:T(8,128)(2,1)} custom-call(bf16[640,256]{1,0:T(8,128)(2,1)} %fusion.65.q), custom_call_target="tpu_custom_call" | custom-call | tf_op jit(solution)/shard_map/pallas_call | solution.py:45
  217.9 5.1 multiply_convert_fusion.3
  224.0 21.7 %shard_map.289 = bf16[8,80,1024]{2,1,0:T(8,128)(2,1)} custom-call(bf16[8,80,256]{2,1,0:T(8,128)(2,1)} %bitcast.222), custom_call_target="tpu_custom_call" | custom-call | tf_op jit(solution)/shard_map/pallas_call | solution.py:45
  247.9 2.4 fusion.15
  250.3 3.7 multiply_reduce_fusion.3
  254.1 1.8 convert.12
  255.9 2.6 fusion.52.refs_0_
  258.5 13.6 %shard_map.287 = f32[640,256]{1,0:T(8,128)} custom-call(bf16[640,1024]{1,0:T(8,128)(2,1)} %fusion.52.refs_0_), custom_call_target="tpu_custom_call" | custom-call | tf_op jit(solution)/shard_map/pallas_call | solution.py:45
  274.3 14.0 %shard_map.290 = (f32[640,256]{1,0:T(8,128)}, f32[8,640]{1,0:T(8,128)}) custom-call(bf16[640,1024]{1,0:T(8,128)(2,1)} %get-tuple-element.78.refs_0_, f32[8,640]{1,0:T(8,128)} %select_maximum_fusion.1.refs_1_), custom_call_target="tpu_custom_call" | custom-call | tf_op jit(solution)/shard_map/pallas_call | solution.py:45
  289.2 3.2 multiply_reduce_fusion.6
  292.3 12.6 %shard_map.291 = bf16[640,1024]{1,0:T(8,128)(2,1)} custom-call(bf16[640,256]{1,0:T(8,128)(2,1)} %get-tuple-element.72.q), custom_call_target="tpu_custom_call" | custom-call | tf_op jit(solution)/shard_map/pallas_call | solution.py:45
  304.9 5.1 fusion.21
  310.0 3.8 multiply_reduce_fusion.2
  314.4 14.0 %shard_map.292 = (f32[640,256]{1,0:T(8,128)}, f32[8,640]{1,0:T(8,128)}) custom-call(bf16[640,1024]{1,0:T(8,128)(2,1)} %get-tuple-element.77.refs_0_, f32[8,640]{1,0:T(8,128)} %select_maximum_fusion.refs_1_), custom_call_target="tpu_custom_call" | custom-call | tf_op jit(solution)/shard_map/pallas_call | solution.py:45
  330.1 3.4 multiply_reduce_fusion.7
  333.5 12.6 %shard_map.288 = bf16[8,80,256]{2,1,0:T(8,128)(2,1)} custom-call(bf16[8,80,256]{2,1,0:T(8,128)(2,1)} %bitcast.214), custom_call_target="tpu_custom_call" | custom-call | tf_op jit(solution)/shard_map/pallas_call | solution.py:45
  348.2 11.6 %shard_map.293 = bf16[8,80,256]{2,1,0:T(8,128)(2,1)} custom-call(bf16[8,80,256]{2,1,0:T(8,128)(2,1)} %bitcast.213), custom_call_target="tpu_custom_call" | custom-call | tf_op jit(solution)/shard_map/pallas_call | solution.py:45
  362.0 11.0 %shard_map.294 = bf16[512,1024]{1,0:T(8,128)(2,1)} custom-call(bf16[512,256]{1,0:T(8,128)(2,1)} %bitcast.224), custom_call_target="tpu_custom_call" | custom-call | tf_op jit(solution)/shard_map/pallas_call | solution.py:45
  373.1 4.5 fusion.35
  377.6 2.8 convolution_convert_fusion.1
  380.5 2.6 convolution_convert_fusion
  383.1 3.2 convolution_convert_fusion.3
  386.3 3.5 convolution_convert_fusion.2
  389.8 3.2 multiply_reduce_fusion.5
  393.6 12.3 %shard_map.295 = (f32[512,256]{1,0:T(8,128)}, f32[8,512]{1,0:T(8,128)}) custom-call(bf16[512,1024]{1,0:T(8,128)(2,1)} %get-tuple-element.79.refs_0_, f32[8,512]{1,0:T(8,128)} %select_maximum_fusion.3.refs_1_), custom_call_target="tpu_custom_call" | custom-call | tf_op jit(solution)/shard_map/pallas_call | solution.py:45
  406.6 2.7 multiply_reduce_fusion.9
  409.4 11.0 %shard_map.296.refs_4_ = bf16[512,1024]{1,0:T(8,128)(2,1)} custom-call(bf16[512,256]{1,0:T(8,128)(2,1)} %get-tuple-element.76.q), custom_call_target="tpu_custom_call" | custom-call | tf_op jit(solution)/shard_map/pallas_call | solution.py:45
  421.9 110.2 %shard_map.297 = (bf16[32,3072]{1,0:T(8,128)(2,1)}, bf16[32,4096]{1,0:T(8,128)(2,1)}, f32[32,1024]{1,0:T(8,128)}, f32[128,1024]{1,0:T(8,128)}, f32[8,256]{1,0:T(...) custom-call(bf16[4,8,32,1024]{3,2,1,0:T(8,128)(2,1)} %bitcast.207, ...), custom_call_target="tpu_custom_call" | custom-call | tf_op jit(solution)/shard_map/pallas_call | solution.py:45
  535.1 1.8 convert_element_type.279
  536.9 4.2 bitcast_convert_fusion.1
  541.1 3.9 convolution_bitcast_fusion.1
  545.0 2.5 bitcast_convert_fusion
  547.5 3.9 convolution_bitcast_fusion
  (196 shorter events, 46.6 us)
Async XLA Ops:
  0.6 246.8 %copy-start = (bf16[1,1024,1024]{2,1,0:T(8,128)(2,1)S(1)}, bf16[1,1024,1024]{2,1,0:T(8,128)(2,1)}, u32[]{:S(2)}) copy-start(bf16[1,1024,1024]{2,1,0:T(8,128)(2,1)} %param.33) | copy-start | bytes 6291460
  4.9 83.1 %copy-start.32 = (s32[2]{0:T(128)S(1)}, s32[2]{0:T(128)}, u32[]{:S(2)}) copy-start(s32[2]{0:T(128)} %param.20) | copy-start | bytes 28
  86.8 3.4 copy-start.3
  90.2 1.4 copy-start.21
  91.3 1.4 copy-start.13
  98.1 3.0 copy-start.20
  100.4 15.0 %copy-start.24 = (bf16[2,256,256]{2,1,0:T(8,128)(2,1)S(1)}, bf16[2,256,256]{2,1,0:T(8,128)(2,1)}, u32[]{:S(2)}) copy-start(bf16[2,256,256]{2,1,0:T(8,128)(2,1)} %param.17) | copy-start | bytes 786436
  128.8 3.2 copy-start.9
  132.0 4.5 copy-start.35
  136.6 2.3 copy-start.47
  136.6 14.3 %copy-start.18 = (bf16[512,256]{1,0:T(8,128)(2,1)S(1)}, bf16[512,256]{1,0:T(8,128)(2,1)}, u32[]{:S(2)}) copy-start(bf16[512,256]{1,0:T(8,128)(2,1)} %add_convert_fusion.5.q) | copy-start | bytes 786436
  138.8 13.2 %copy-start.31 = (s32[2,256,1]{1,2,0:T(1,128)S(1)}, s32[2,256,1]{1,2,0:T(1,128)}, u32[]{:S(2)}) copy-start(s32[2,256,1]{1,2,0:T(1,128)} %param.19) | copy-start | bytes 6148
  176.4 2.0 copy-start.2
  179.1 1.6 copy-start.36
  180.7 4.3 copy-start.33
  183.9 1.1 copy-start.39
  215.7 1.7 copy-start.4
  217.9 5.1 copy-start.28
  245.7 2.1 copy-start.49
  247.9 2.4 copy-start.5
  247.9 2.5 copy-start.38
  250.3 3.7 copy-start.41
  250.3 3.7 copy-start.7
  254.1 1.8 copy-start.45
  258.5 13.6 %copy-start.12 = (bf16[640,256]{1,0:T(8,128)(2,1)S(1)}, bf16[640,256]{1,0:T(8,128)(2,1)}, u32[]{:S(2)}) copy-start(bf16[640,256]{1,0:T(8,128)(2,1)} %fusion.65.q) | copy-start | bytes 983044
  304.9 5.1 copy-start.37
  310.0 3.8 copy-start.43
  310.0 20.0 %copy-start.11 = (f32[640,256]{1,0:T(8,128)S(1)}, f32[640,256]{1,0:T(8,128)}, u32[]{:S(2)}) copy-start(f32[640,256]{1,0:T(8,128)} %shard_map.287) | copy-start | bytes 1966084
  310.0 20.0 %copy-start.15 = (bf16[640,256]{1,0:T(8,128)(2,1)S(1)}, bf16[640,256]{1,0:T(8,128)(2,1)}, u32[]{:S(2)}) copy-start(bf16[640,256]{1,0:T(8,128)(2,1)} %get-tuple-element.72.q) | copy-start | bytes 983044
  373.0 4.6 copy-start.10
  377.6 2.8 copy-start.23
  377.6 2.8 copy-start.48
  380.5 2.6 copy-start.29
  380.5 2.6 copy-start.44
  383.1 3.2 copy-start.6
  383.1 3.2 copy-start.42
  386.3 3.5 copy-start.34
  389.7 16.9 %copy-start.25 = (bf16[2,256,256]{2,1,0:T(8,128)(2,1)S(1)}, bf16[2,256,256]{2,1,0:T(8,128)(2,1)}, u32[]{:S(2)}) copy-start(bf16[2,256,256]{2,1,0:T(8,128)(2,1)} %convolution_convert_fusion.10) | copy-start | bytes 786436
  392.9 27.5 %copy-start.17 = (bf16[32,8,2,256]{3,1,2,0:T(8,128)(2,1)S(1)}, bf16[32,8,2,256]{3,1,2,0:T(8,128)(2,1)}, u32[]{:S(2)}) copy-start(bf16[32,8,2,256]{3,1,2,0:T(8,128)(2,1)} %copy-done.16) | copy-start | bytes 786436
  536.9 4.3 copy-start.22
  536.9 4.3 copy-start.40
  541.1 3.9 copy-start.19
  545.0 2.5 copy-start.8
  545.0 2.5 copy-start.46
  547.5 4.0 copy-start.27
  547.5 4.8 copy-start.30
  547.5 5.4 copy-start.26
  547.5 6.2 %copy-start.1 = (bf16[1,1024,1024]{2,1,0:T(8,128)(2,1)S(1)}, bf16[1,1024,1024]{2,1,0:T(8,128)(2,1)}, u32[]{:S(2)}) copy-start(bf16[1,1024,1024]{2,1,0:T(8,128)(2,1)} %param.33) | copy-start | bytes 6291460
  (2 other events, 1.6 us)

commit v4 on v3

--- a/solution.py
+++ b/solution.py
@@ -228,235 +228,6 @@
         [DMA((4, count)), DMA((4, count))],
         collective_id,
         slots,
-    )
-
-
-def weights_kernel(qkv, inn, vec, outw, backw, first, second, tok, *refs):
-    o_qkv, o_in, o_vec, o_out, o_back, o_first, o_second, o_tok = refs[:8]
-    st_qkv, st_in, st_vec, loc, cut_s, cut_r, tok_s, tok_r, line_s, line_r, exp_s, exp_r = refs[8:]
-    me, beside, across = section_places()
-    w = lax.axis_index("wide")
-    length = lax.axis_size("wide") // 2
-    a, b = lax.div(w, 2), lax.rem(w, 2)
-    other = 1 - b
-    diagonal = beside + across - me
-    peers = [beside, across, diagonal]
-    barrier = pltpu.get_barrier_semaphore()
-    for p in peers:
-        pl.semaphore_signal(barrier, inc=1, device_id={"section": p}, device_id_type=MESH)
-    pl.semaphore_signal(barrier, inc=1, device_id={"wide": 2 * a + other}, device_id_type=MESH)
-
-    @pl.when(a > 0)
-    def _():
-        pl.semaphore_signal(barrier, inc=1, device_id={"wide": w - 2}, device_id_type=MESH)
-
-    @pl.when(a < length - 1)
-    def _():
-        pl.semaphore_signal(barrier, inc=1, device_id={"wide": w + 2}, device_id_type=MESH)
-
-    pl.semaphore_wait(barrier, 4 + jnp.minimum(a, 1) + jnp.minimum(length - 1 - a, 1))
-
-    hid = o_first.shape[2]
-    width = 4 * QUARTER
-    sent, local_cuts = [], []
-
-    def part_of(src, start, count):
-        return src.at[:, pl.ds(pl.multiple_of(start, 128), count)]
-
-    def cuts_for(p):
-        got = [
-            (0, part_of(qkv, j * width + p * QUARTER, QUARTER), st_qkv.at[me, :, pl.ds(j * QUARTER, QUARTER)])
-            for j in range(3)
-        ]
-        return got + [(1, part_of(inn, p * hid, hid), st_in.at[me]), (2, vec, st_vec.at[me])]
-
-    for k, p in enumerate(peers):
-        for n, (i, src, dst) in enumerate(cuts_for(p)):
-            c = push(src, dst, cut_s.at[n, k], cut_r.at[n, k], {"section": p})
-            c.start()
-            sent.append((i, c))
-    for n, (i, src, dst) in enumerate(cuts_for(me)):
-        c = pltpu.make_async_copy(src, dst, loc.at[11 + n])
-        c.start()
-        local_cuts.append((i, c))
-    tok_c = [
-        push(tok, o_tok.at[:, columns(me)], tok_s.at[k], tok_r.at[k], {"section": p})
-        for k, p in enumerate((across, beside))
-    ]
-    for c in tok_c:
-        c.start()
-    own_tok = pltpu.make_async_copy(tok, o_tok.at[:, columns(me)], loc.at[3])
-    own_tok.start()
-    late = [own_tok]
-    for i, (src, dst) in enumerate(((first, o_first), (second, o_second))):
-        c = pltpu.make_async_copy(part_of(src, me * hid, hid), dst.at[me], loc.at[4 + i])
-        c.start()
-        late.append(c)
-    exp_c = []
-    for i, (src, dst) in enumerate(((first, o_first), (second, o_second))):
-        for k, p in enumerate((across, diagonal, beside)):
-            c = push(part_of(src, p * hid, hid), dst.at[me], exp_s.at[i, k], exp_r.at[i, k], {"section": p})
-            c.start()
-            exp_c.append(c)
-
-    lines = (
-        (st_qkv, o_qkv, True),
-        (outw, o_out, False),
-        (st_in, o_in, True),
-        (backw, o_back, False),
-        (st_vec, o_vec, False),
-    )
-    staged = {0: 0, 2: 1, 4: 2}
-
-    def place(i, which):
-        dst = lines[i][1]
-        return dst.at[:, which] if i in staged else dst.at[which]
-
-    def item(i, which, kind, to, own=False):
-        src, _, _ = lines[i]
-        spot = place(i, which)
-        return push(src if own else spot, spot, line_s.at[kind, i, which], line_r.at[i, which], {"wide": to})
-
-    up, down, pair = 0, 1, 2
-
-    def along(i, which, kind, own, act):
-        if kind == pair:
-            act(item(i, which, pair, 2 * a + other, own))
-            return
-
-        @pl.when((a < length - 1) if kind == up else (a > 0))
-        def _():
-            act(item(i, which, kind, w + 2 if kind == up else w - 2, own))
-
-    def start(c):
-        c.start()
-
-    def done(c):
-        c.wait_send()
-
-    for i, (src, dst, _) in enumerate(lines):
-        if i in staged:
-            for j, c in sent:
-                if j == staged[i]:
-                    c.wait_recv()
-            for j, c in local_cuts:
-                if j == staged[i]:
-                    c.wait()
-        for kind in (up, down, pair):
-            along(i, w, kind, True, start)
-        c = pltpu.make_async_copy(src, place(i, w), loc.at[6 + i])
-        c.start()
-        late.append(c)
-    tok_c[0].wait_recv()
-    spot = o_tok.at[:, columns(across)]
-    tok_fwd = push(spot, spot, tok_s.at[2], tok_r.at[2], {"section": beside})
-    tok_fwd.start()
-
-    mate = 2 * a + other
-
-    def arrived(i, which):
-        item(i, which, pair, mate).wait_recv()
-
-    for i in range(len(lines)):
-        if not lines[i][2]:
-            arrived(i, mate)
-            for kind in (up, down):
-                along(i, mate, kind, False, start)
-
-    def step(t, carry):
-        for i in range(len(lines)):
-            for kind, there, ok in ((up, a - t, a - t >= 0), (down, a + t, a + t < length)):
-
-                @pl.when(ok)
-                def _():
-                    arrived(i, 2 * there + b)
-                    along(i, 2 * there + b, kind, False, start)
-                    if lines[i][2]:
-                        along(i, 2 * there + b, pair, False, start)
-                    else:
-                        arrived(i, 2 * there + other)
-                        along(i, 2 * there + other, kind, False, start)
-
-        return carry
-
-    lax.fori_loop(1, length, step, 0)
-    for i in range(len(lines)):
-        if lines[i][2]:
-            lax.fori_loop(0, length, lambda there, carry: (arrived(i, 2 * there + other), carry)[1], 0)
-        for kind in (up, down, pair):
-            along(i, w, kind, True, done)
-        if not lines[i][2]:
-            for kind in (up, down):
-                along(i, mate, kind, False, done)
-
-    def finish(t, carry):
-        for i in range(len(lines)):
-            for kind, there, ok in ((up, a - t, a - t >= 0), (down, a + t, a + t < length)):
-
-                @pl.when(ok)
-                def _():
-                    along(i, 2 * there + b, kind, False, done)
-                    if lines[i][2]:
-                        along(i, 2 * there + b, pair, False, done)
-                    else:
-                        along(i, 2 * there + other, kind, False, done)
-
-        return carry
-
-    lax.fori_loop(1, length, finish, 0)
-    for _, c in sent:
-        c.wait_send()
-    tok_c[0].wait_send()
-    tok_c[1].wait()
-    tok_fwd.wait()
-    for c in exp_c:
-        c.wait()
-    for c in late:
-        c.wait()
-
-
-def weights_call(qkv, inn, vec, outw, backw, first, second, tok, wide, collective_id):
-    small = qkv.shape[0]
-    hid = inn.shape[1] // 4
-    cut = 3 * QUARTER
-    outs = [
-        ((4, wide, small, cut), BF16),
-        ((4, wide, small, hid), BF16),
-        ((4, wide, *vec.shape), F32),
-        ((wide, *outw.shape), BF16),
-        ((wide, *backw.shape), BF16),
-        ((4, first.shape[0], hid), BF16),
-        ((4, first.shape[0], hid), BF16),
-        ((tok.shape[0], 4 * QUARTER), BF16),
-    ]
-    return call(
-        weights_kernel,
-        tuple(jax.ShapeDtypeStruct(*o) for o in outs),
-        [ANY] * 8,
-        tuple([ANY] * 8),
-        [
-            pltpu.VMEM((4, small, cut), BF16),
-            pltpu.VMEM((4, small, hid), BF16),
-            pltpu.VMEM((4, *vec.shape), F32),
-            DMA((16,)),
-            DMA((5, 3)),
-            DMA((5, 3)),
-            DMA((3,)),
-            DMA((3,)),
-            DMA((3, 5, wide)),
-            DMA((5, wide)),
-            DMA((2, 3)),
-            DMA((2, 3)),
-        ],
-        collective_id,
-        qkv,
-        inn,
-        vec,
-        outw,
-        backw,
-        first,
-        second,
-        tok,
     )
 
 
@@ -874,6 +645,331 @@
     )
 
 
+def head_kernel(*refs):
+    qkv, inn, vec, outw, backw, first, second, tok, mask = refs[:9]
+    o_qkv, o_in, o_vec, o_out, o_back, o_first, o_second, o_tok, o_n1, o_act, o_mixed, o_att = refs[9:21]
+    st_qkv, st_in, st_vec, gain, part, near_in, far, far_in = refs[21:29]
+    loc, cut_s, cut_r, tok_s, tok_r, line_s, line_r, exp_s, exp_r, s1, r1, s2, r2, g_s, g_r = refs[29:]
+    me, beside, across = section_places()
+    core, side = lax.rem(me, 2), lax.div(me, 2)
+    w, length, a, b = line_of_wide()
+    other = 1 - b
+    mate = 2 * a + other
+    diagonal = beside + across - me
+    peers = [beside, across, diagonal]
+    greet_line(peers, False)
+    hid = o_first.shape[2]
+    width = 4 * QUARTER
+    sent, local_cuts = [], []
+
+    def part_of(src, start, count):
+        return src.at[:, pl.ds(pl.multiple_of(start, 128), count)]
+
+    def cuts_for(p):
+        got = [
+            (0, part_of(qkv, j * width + p * QUARTER, QUARTER), st_qkv.at[me, :, pl.ds(j * QUARTER, QUARTER)])
+            for j in range(3)
+        ]
+        return got + [(1, part_of(inn, p * hid, hid), st_in.at[me]), (2, vec, st_vec.at[me])]
+
+    for k, p in enumerate(peers):
+        for n, (i, src, dst) in enumerate(cuts_for(p)):
+            c = push(src, dst, cut_s.at[n, k], cut_r.at[n, k], {"section": p})
+            c.start()
+            sent.append((i, c))
+    for n, (i, src, dst) in enumerate(cuts_for(me)):
+        c = pltpu.make_async_copy(src, dst, loc.at[11 + n])
+        c.start()
+        local_cuts.append((i, c))
+    tok_c = [
+        push(tok, o_tok.at[:, columns(me)], tok_s.at[k], tok_r.at[k], {"section": p})
+        for k, p in enumerate((across, beside))
+    ]
+    for c in tok_c:
+        c.start()
+    own_tok = pltpu.make_async_copy(tok, o_tok.at[:, columns(me)], loc.at[3])
+    own_tok.start()
+    late = []
+    exp_c = []
+    for i, (src, dst) in enumerate(((first, o_first), (second, o_second))):
+        c = pltpu.make_async_copy(part_of(src, me * hid, hid), dst.at[me], loc.at[4 + i])
+        c.start()
+        late.append(c)
+        for k, p in enumerate((across, diagonal, beside)):
+            c = push(part_of(src, p * hid, hid), dst.at[me], exp_s.at[i, k], exp_r.at[i, k], {"section": p})
+            c.start()
+            exp_c.append(c)
+
+    lines = (
+        (st_qkv, o_qkv, True),
+        (outw, o_out, False),
+        (st_in, o_in, True),
+        (backw, o_back, False),
+        (st_vec, o_vec, False),
+    )
+    staged = {0: 0, 2: 1, 4: 2}
+    up, down, pair = 0, 1, 2
+
+    def place(i, which):
+        dst = lines[i][1]
+        return dst.at[:, which] if i in staged else dst.at[which]
+
+    def item(i, which, kind, to, own=False):
+        spot = place(i, which)
+        return push(lines[i][0] if own else spot, spot, line_s.at[kind, i, which], line_r.at[i, which], {"wide": to})
+
+    def along(i, which, kind, own, act):
+        if kind == pair:
+            act(item(i, which, pair, mate, own))
+            return
+
+        @pl.when((a < length - 1) if kind == up else (a > 0))
+        def _():
+            act(item(i, which, kind, w + 2 if kind == up else w - 2, own))
+
+    def start(c):
+        c.start()
+
+    def done(c):
+        c.wait_send()
+
+    def arrived(i, which):
+        item(i, which, pair, mate).wait_recv()
+
+    def own_item(i):
+        if i in staged:
+            for j, c in sent:
+                if j == staged[i]:
+                    c.wait_recv()
+            for j, c in local_cuts:
+                if j == staged[i]:
+                    c.wait()
+        for kind in (up, down, pair):
+            along(i, w, kind, True, start)
+        c = pltpu.make_async_copy(lines[i][0], place(i, w), loc.at[6 + i])
+        c.start()
+        return c
+
+    def mate_item(i):
+        if not lines[i][2]:
+            arrived(i, mate)
+            for kind in (up, down):
+                along(i, mate, kind, False, start)
+
+    def both_ways(t, what):
+        for kind, there, ok in ((up, a - t, a - t >= 0), (down, a + t, a + t < length)):
+
+            @pl.when(ok)
+            def _():
+                what(kind, there)
+
+    def steps(group, begin, end):
+        def step(t, carry):
+            for i in group:
+
+                def pass_on(kind, there):
+                    arrived(i, 2 * there + b)
+                    along(i, 2 * there + b, kind, False, start)
+                    if lines[i][2]:
+                        along(i, 2 * there + b, pair, False, start)
+                    else:
+                        arrived(i, 2 * there + other)
+                        along(i, 2 * there + other, kind, False, start)
+
+                both_ways(t, pass_on)
+            return carry
+
+        lax.fori_loop(begin, end, step, 0)
+
+    def pair_items(i):
+        if lines[i][2]:
+            lax.fori_loop(0, length, lambda there, carry: (arrived(i, 2 * there + other), carry)[1], 0)
+
+    def all_sent(i):
+        for kind in (up, down, pair):
+            along(i, w, kind, True, done)
+        if not lines[i][2]:
+            for kind in (up, down):
+                along(i, mate, kind, False, done)
+
+        def finish(t, carry):
+            def one(kind, there):
+                along(i, 2 * there + b, kind, False, done)
+                if lines[i][2]:
+                    along(i, 2 * there + b, pair, False, done)
+                else:
+                    along(i, 2 * there + other, kind, False, done)
+
+            both_ways(t, one)
+            return carry
+
+        lax.fori_loop(1, length, finish, 0)
+
+    early, later = (4, 0, 1), (2, 3)
+    soon = [own_item(i) for i in early]
+    tok_c[0].wait_recv()
+    spot = o_tok.at[:, columns(across)]
+    tok_fwd = push(spot, spot, tok_s.at[2], tok_r.at[2], {"section": beside})
+    tok_fwd.start()
+    for i in early:
+        mate_item(i)
+    steps(early, 1, 2)
+    late += [own_item(i) for i in later]
+    steps(early, 2, length)
+    for i in later:
+        mate_item(i)
+    for i in early:
+        pair_items(i)
+    for c in soon:
+        c.wait()
+    own_tok.wait()
+    tok_c[1].wait_recv()
+    tok_fwd.wait_recv()
+
+    wide = 2 * length
+    small = qkv.shape[0]
+    per = 128 // small
+    for p in range(4):
+        for g in range(wide // per):
+            total = o_vec[p, g * per, 6:7]
+            for j in range(1, per):
+                total = total + o_vec[p, g * per + j, 6:7]
+            gain[:, pl.ds((p * (wide // per) + g) * 128, 128)] = total
+    micro, rows = mask.shape[:2]
+    count = micro * rows
+    chunk = 128
+    chunks = count // chunk
+
+    def project(k, carry):
+        at = pl.ds(pl.multiple_of(k * chunk, chunk), chunk)
+        unit, _ = row_norm(o_tok[at].astype(F32))
+        o_n1[at] = (unit * gain[...]).astype(BF16)
+        total = jnp.zeros((chunk, 3 * QUARTER), F32)
+        for p in range(4):
+            total = total + dot(o_n1[at, pl.ds(p * QUARTER, QUARTER)], o_qkv[p].reshape(QUARTER, 3 * QUARTER))
+        o_act[at] = total.astype(BF16)
+        return carry
+
+    lax.fori_loop(0, chunks, project, 0)
+    cuts = [1 + k * (length - 1) // 3 for k in range(4)]
+    beside_core = 1 - core
+    sends, crossing, spread = [], [], []
+    for m in range(micro):
+        at = pl.ds(m * rows, rows)
+        for n in range(2):
+            heads = attention_pair(n, lambda c: o_act[at, pl.ds(c, 128)], mask[m])
+            got = [dot(probs.astype(BF16), v) for _, _, v, probs in heads]
+            o_mixed[at, pl.ds(n * 128, 128)] = jnp.concatenate(got, axis=1).astype(BF16)
+        for k in range(m * rows // chunk, (m + 1) * rows // chunk):
+            at = pl.ds(k * chunk, chunk)
+            part[at] = dot(o_mixed[at], o_out[...].reshape(QUARTER, width)).astype(BF16)
+            for which, half in ((1, 1 - side), (0, side)):
+                c = push(
+                    part.at[at, columns(2 * half + beside_core)],
+                    near_in.at[which, at],
+                    s1.at[which, k],
+                    r1.at[which, k],
+                    {"section": beside},
+                )
+                c.start()
+                sends.append(c)
+        steps(later, cuts[m], cuts[m + 1])
+    for k in range(chunks):
+        at = pl.ds(k * chunk, chunk)
+        sends[2 * k].wait()
+        far[at] = (part[at, columns(2 * (1 - side) + core)].astype(F32) + near_in[1, at].astype(F32)).astype(BF16)
+        c = push(far.at[at], far_in.at[at], s2.at[k], r2.at[k], {"section": across})
+        c.start()
+        crossing.append(c)
+    for k in range(chunks):
+        at = pl.ds(k * chunk, chunk)
+        sends[2 * k + 1].wait()
+        near = part[at, columns(me)].astype(F32) + near_in[0, at].astype(F32)
+        crossing[k].wait()
+        o_att[at, columns(me)] = (o_tok[at, columns(me)].astype(F32) + (near + far_in[at].astype(F32))).astype(BF16)
+        here = o_att.at[at, columns(me)]
+        for kind, to in ((0, across), (1, beside)):
+            c = push(here, here, g_s.at[kind, k], g_r.at[kind, k], {"section": to})
+            c.start()
+            spread.append(c)
+    steps(later, cuts[micro], cuts[3])
+    for k in range(chunks):
+        spread[2 * k].wait()
+        here = o_att.at[pl.ds(k * chunk, chunk), columns(across)]
+        c = push(here, here, g_s.at[2, k], g_r.at[2, k], {"section": beside})
+        c.start()
+        spread.append(c)
+    for i in later:
+        pair_items(i)
+    for k in range(chunks):
+        spread[2 * k + 1].wait()
+        spread[2 * chunks + k].wait()
+    for i in early + later:
+        all_sent(i)
+    for _, c in sent:
+        c.wait_send()
+    for c in tok_c + [tok_fwd]:
+        c.wait_send()
+    for c in exp_c + late:
+        c.wait()
+
+
+def head_call(qkv, inn, vec, outw, backw, first, second, tok, mask, wide, collective_id):
+    small = qkv.shape[0]
+    hid = inn.shape[1] // 4
+    cut = 3 * QUARTER
+    count = tok.shape[0]
+    width = 4 * QUARTER
+    chunks = count // 128
+    outs = [
+        ((4, wide, small, cut), BF16),
+        ((4, wide, small, hid), BF16),
+        ((4, wide, *vec.shape), F32),
+        ((wide, *outw.shape), BF16),
+        ((wide, *backw.shape), BF16),
+        ((4, first.shape[0], hid), BF16),
+        ((4, first.shape[0], hid), BF16),
+        ((count, width), BF16),
+        ((count, width), BF16),
+        ((count, cut), BF16),
+        ((count, QUARTER), BF16),
+        ((count, width), BF16),
+    ]
+    return call(
+        head_kernel,
+        tuple(jax.ShapeDtypeStruct(*o) for o in outs),
+        [ANY] * 8 + [VM],
+        (VM, ANY, VM, VM, ANY, ANY, ANY, VM, VM, VM, VM, VM),
+        [
+            pltpu.VMEM((4, small, cut), BF16),
+            pltpu.VMEM((4, small, hid), BF16),
+            pltpu.VMEM((4, *vec.shape), F32),
+            pltpu.VMEM((1, width), F32),
+            pltpu.VMEM((count, width), BF16),
+            pltpu.VMEM((2, count, QUARTER), BF16),
+            pltpu.VMEM((count, QUARTER), BF16),
+            pltpu.VMEM((count, QUARTER), BF16),
+            DMA((16,)),
+            DMA((5, 3)),
+            DMA((5, 3)),
+            DMA((3,)),
+            DMA((3,)),
+            DMA((3, 5, wide)),
+            DMA((5, wide)),
+            DMA((2, 3)),
+            DMA((2, 3)),
+            DMA((2, chunks)),
+            DMA((2, chunks)),
+            DMA((chunks,)),
+            DMA((chunks,)),
+            DMA((3, chunks)),
+            DMA((3, chunks)),
+        ],
+        collective_id,
+        *(qkv, inn, vec, outw, backw, first, second, tok, mask),
+    )
+
+
 def dot(left, right):
     return jnp.dot(left, right, preferred_element_type=F32)
 
@@ -926,18 +1022,6 @@
     pos = jnp.arange(rows, dtype=jnp.int32)
     group = pos[None] // lengths[:, None]
     return ((pos[:, None] >= pos[None, :])[None] & (group[:, :, None] == group[:, None, :])).astype(F32)
-
-
-def attention_probs(queries, keys, lengths):
-    rows = queries.shape[2]
-    raw = jnp.einsum("mhqd,mhkd->mhqk", queries, keys, preferred_element_type=F32)
-    pos = jnp.arange(rows, dtype=jnp.int32)
-    same = pos[None, :, None] // lengths[:, None, None] == pos[None, None, :] // lengths[:, None, None]
-    allowed = (pos[:, None] >= pos[None, :])[None] & same
-    scores = jnp.where(allowed[:, None], raw * HEAD_SIZE ** (-0.5), -1e30)
-    highest = jnp.max(scores, axis=-1, keepdims=True)
-    expo = jnp.exp(scores - highest)
-    return expo / jnp.sum(expo, axis=-1, keepdims=True)
 
 
 def body(
@@ -971,11 +1055,16 @@
     small = qkv_weight.shape[0]
     qkv_cols = qkv_weight.shape[1] // sections
 
-    vectors = jnp.concatenate([first_gain[0], second_gain[0], centroids[0], attn_gain, ffn_gain]).astype(F32)
-    vectors = jnp.pad(vectors, (0, 1024 - vectors.shape[0])).reshape(8, 128)
+    per = 128 // small
+    spread = lambda v: lax.dynamic_update_slice_in_dim(
+        jnp.zeros((1, 128), F32), v.astype(F32)[None], lax.rem(wide_id, per) * small, 1
+    )
+    vectors = [v.astype(F32).reshape(2, 128) for v in (first_gain, second_gain, centroids)]
+    vectors = jnp.concatenate(vectors + [spread(attn_gain), spread(ffn_gain)], axis=0)
+    allowed = allowed_of(seq_lengths, rows)
     tokens_q = tokens_in.reshape(tok_rows, quarter)
 
-    qkv_w, in_w, vectors, out_w, back_w, first_w, second_w, tokens = weights_call(
+    (qkv_w, in_w, vectors, out_w, back_w, first_w, second_w, tokens, normed_a, packed, mixed, attended) = head_call(
         qkv_weight,
         ffn_in,
         vectors,
@@ -984,8 +1073,9 @@
         first_in[0],
         second_in[0],
         tokens_q,
+        allowed,
         wide,
-        id_of("weights"),
+        id_of("head"),
     )
     qkv_w = qkv_w.reshape(width, qkv_cols)
     in_w = in_w.reshape(width, hid)
@@ -993,13 +1083,11 @@
     back_w = back_w.reshape(hid, width)
     first_w = first_w.reshape(width, hid)
     second_w = second_w.reshape(width, hid)
-    vectors = vectors.reshape(sections, wide, 1024)
     own = lax.dynamic_index_in_dim(vectors, wide_id, axis=1, keepdims=False)
-    gain_first = own[:, :quarter].reshape(1, width)
-    gain_second = own[:, quarter : 2 * quarter].reshape(1, width)
-    centre = own[:, 2 * quarter : 3 * quarter].reshape(1, width)
-    gain_attn = vectors[:, :, 3 * quarter : 3 * quarter + small].reshape(1, width)
-    gain_ffn = vectors[:, :, 3 * quarter + small : 3 * quarter + 2 * small].reshape(1, width)
+    gain_first, gain_second, centre = (own[:, 2 * j : 2 * j + 2].reshape(1, width) for j in range(3))
+    gain_attn, gain_ffn = (
+        jnp.sum(vectors[:, :, j].reshape(sections, wide // per, per, 128), axis=2).reshape(1, width) for j in (6, 7)
+    )
     own_quarter = lambda v: lax.dynamic_slice_in_dim(v, section_id * quarter, quarter, axis=1)
     first_b = first_back[0]
     second_b = second_back[0]
@@ -1022,25 +1110,7 @@
         got = jnp.einsum("msr,msd->mrd", onehot, back, preferred_element_type=F32)
         return got.astype(BF16).reshape(tok_rows, quarter)
 
-    unit_a, scale_a = unit_norm(tokens.astype(F32))
-    normed_a = (unit_a * gain_attn).astype(BF16)
-    packed = dot(normed_a, qkv_w).astype(BF16)
-    heads = quarter // HEAD_SIZE
-
-    def by_head(v):
-        return v.reshape(micro, rows, heads, HEAD_SIZE).transpose(0, 2, 1, 3)
-
-    def from_head(v):
-        return v.transpose(0, 2, 1, 3).reshape(tok_rows, quarter)
-
-    queries, keys, values = (by_head(packed[:, i * quarter : (i + 1) * quarter]) for i in range(3))
-    probs = attention_probs(queries, keys, seq_lengths)
-    probs_b = probs.astype(BF16)
-    mixed = from_head(
-        jnp.einsum("mhqk,mhkd->mhqd", probs_b, values, preferred_element_type=F32).astype(BF16)
-    )
-    attended_q = (tokens_q.astype(F32) + reduce_quarters(dot(mixed, out_w))).astype(BF16)
-    attended = gather_quarters(attended_q)
+    attended_q = own_quarter(attended)
 
     def branch(v, w_in, w_back, gain):
         unit, scale = unit_norm(v.astype(F32))
@@ -1114,7 +1184,7 @@
         mixed,
         qkv_w,
         out_w,
-        allowed_of(seq_lengths, rows),
+        allowed,
         gain_attn,
         d_gain_ffn[None],
         id_of("tail"),

time: 565 us -> 532 us (0.942)
  Pallas kernels: 412 us -> 398 us
  matrix products: 73.3 us -> 65.7 us
    pallas_call x18 -> x16, Pallas kernels: 412 us -> 398 us  [call(): pl.pallas_call(kernel, out_shape=out_shape, in_specs=in_specs, out_specs=...]
    dot_general x8 -> x6, matrix products: 22.7 us -> 19.9 us  [dot(): return jnp.dot(left, right, preferred_element_type=F32)]
where the time goes in v4:
time: 532 us; the launch traced here: 526 us
  Pallas kernels  398 us (75%)
  matrix products  65.7 us (12%)
  other arithmetic  46.6 us (9%)
  local copies, waits for them, and re-layouts  14.6 us (3%)
    pallas_call x16, Pallas kernels, call(): pl.pallas_call(kernel, out_shape=out_shape, in_specs=in_specs, out_specs=...  398 us
    dot_general x6, matrix products, dot_nt(): lax.dot_general(left, right, (((1,), (1,)), ((), ())), preferred_element_...  23 us
    dot_general x6, matrix products, dot(): return jnp.dot(left, right, preferred_element_type=F32)  19.9 us
    dot_general x6, matrix products, dot_tn(): lax.dot_general(left, right, (((0,), (0,)), ((), ())), preferred_element_...  19.8 us

profile of v4, /device:TPU:12, one launch (start us, length us, event | category | flops | bytes accessed | tf_op | source)
XLA Modules:
  0.0 526.0 jit_solution(7102610958596717684)
XLA Ops:
  7.7 90.1 %shard_map.280 = (bf16[4,8,32,768]{3,2,1,0:T(8,128)(2,1)}, bf16[4,8,32,1024]{3,2,1,0:T(8,128)(2,1)}, f32[4,8,8,128]{3,2,1,0:T(8,128)}, bf16[8,32,1024]{2,1,0:T(8...) custom-call(bf16[32,3072]{1,0:T(8,128)(2,1)} %refs_0_.1, ...), custom_call_target="tpu_custom_call" | custom-call | tf_op jit(solution)/shard_map/pallas_call | solution.py:45
  101.1 1.6 fusion.23
  102.7 4.5 multiply_convert_fusion.6
  108.2 2.2 convolution_convert_fusion.4.refs_0_
  110.4 12.0 %shard_map.281 = f32[512,256]{1,0:T(8,128)} custom-call(bf16[512,1024]{1,0:T(8,128)(2,1)} %convolution_convert_fusion.4.refs_0_), custom_call_target="tpu_custom_call" | custom-call | tf_op jit(solution)/shard_map/pallas_call | solution.py:45
  124.9 24.6 %shard_map.282 = bf16[8,80,1024]{2,1,0:T(8,128)(2,1)} custom-call(bf16[8,80,256]{2,1,0:T(8,128)(2,1)} %bitcast.172), custom_call_target="tpu_custom_call" | custom-call | tf_op jit(solution)/shard_map/pallas_call | solution.py:45
  149.4 2.0 fusion.8
  153.8 2.9 multiply_convert_fusion.5
  157.7 2.6 fusion.42.refs_0_
  160.3 13.6 %shard_map.283 = f32[640,256]{1,0:T(8,128)} custom-call(bf16[640,1024]{1,0:T(8,128)(2,1)} %fusion.42.refs_0_), custom_call_target="tpu_custom_call" | custom-call | tf_op jit(solution)/shard_map/pallas_call | solution.py:45
  173.8 1.9 fusion.54.q
  175.8 12.6 %shard_map.284 = bf16[640,1024]{1,0:T(8,128)(2,1)} custom-call(bf16[640,256]{1,0:T(8,128)(2,1)} %fusion.54.q), custom_call_target="tpu_custom_call" | custom-call | tf_op jit(solution)/shard_map/pallas_call | solution.py:45
  188.4 1.7 convert_reduce_fusion.1
  190.6 5.1 multiply_convert_fusion.3
  196.7 21.7 %shard_map.287 = bf16[8,80,1024]{2,1,0:T(8,128)(2,1)} custom-call(bf16[8,80,256]{2,1,0:T(8,128)(2,1)} %bitcast.173), custom_call_target="tpu_custom_call" | custom-call | tf_op jit(solution)/shard_map/pallas_call | solution.py:45
  218.3 1.7 multiply_convert_fusion.2
  220.5 2.8 fusion.14
  223.4 3.7 multiply_reduce_fusion.3
  227.1 1.8 convert.16
  228.9 2.6 fusion.45.refs_0_
  231.5 13.6 %shard_map.285 = f32[640,256]{1,0:T(8,128)} custom-call(bf16[640,1024]{1,0:T(8,128)(2,1)} %fusion.45.refs_0_), custom_call_target="tpu_custom_call" | custom-call | tf_op jit(solution)/shard_map/pallas_call | solution.py:45
  245.2 1.5 multiply_reduce_fusion.8
  247.3 14.0 %shard_map.288 = (f32[640,256]{1,0:T(8,128)}, f32[8,640]{1,0:T(8,128)}) custom-call(bf16[640,1024]{1,0:T(8,128)(2,1)} %get-tuple-element.86.refs_0_, f32[8,640]{1,0:T(8,128)} %select_maximum_fusion.1.refs_1_), custom_call_target="tpu_custom_call" | custom-call | tf_op jit(solution)/shard_map/pallas_call | solution.py:45
  262.2 3.2 multiply_reduce_fusion.6
  265.4 12.5 %shard_map.289 = bf16[640,1024]{1,0:T(8,128)(2,1)} custom-call(bf16[640,256]{1,0:T(8,128)(2,1)} %get-tuple-element.80.q), custom_call_target="tpu_custom_call" | custom-call | tf_op jit(solution)/shard_map/pallas_call | solution.py:45
  277.9 5.1 fusion.20
  283.0 3.8 multiply_reduce_fusion.2
  287.4 14.0 %shard_map.290 = (f32[640,256]{1,0:T(8,128)}, f32[8,640]{1,0:T(8,128)}) custom-call(bf16[640,1024]{1,0:T(8,128)(2,1)} %get-tuple-element.85.refs_0_, f32[8,640]{1,0:T(8,128)} %select_maximum_fusion.refs_1_), custom_call_target="tpu_custom_call" | custom-call | tf_op jit(solution)/shard_map/pallas_call | solution.py:45
  303.0 3.4 multiply_reduce_fusion.7
  306.4 12.6 %shard_map.286 = bf16[8,80,256]{2,1,0:T(8,128)(2,1)} custom-call(bf16[8,80,256]{2,1,0:T(8,128)(2,1)} %bitcast.165), custom_call_target="tpu_custom_call" | custom-call | tf_op jit(solution)/shard_map/pallas_call | solution.py:45
  321.2 11.7 %shard_map.291 = bf16[8,80,256]{2,1,0:T(8,128)(2,1)} custom-call(bf16[8,80,256]{2,1,0:T(8,128)(2,1)} %bitcast.164), custom_call_target="tpu_custom_call" | custom-call | tf_op jit(solution)/shard_map/pallas_call | solution.py:45
  335.0 11.1 %shard_map.292 = bf16[512,1024]{1,0:T(8,128)(2,1)} custom-call(bf16[512,256]{1,0:T(8,128)(2,1)} %bitcast.174), custom_call_target="tpu_custom_call" | custom-call | tf_op jit(solution)/shard_map/pallas_call | solution.py:45
  346.1 4.5 fusion.29
  350.6 2.8 convolution_convert_fusion.1
  353.5 2.6 convolution_convert_fusion
  356.1 3.2 convolution_convert_fusion.3
  359.3 3.4 convolution_convert_fusion.2
  362.7 3.1 multiply_reduce_fusion.5
  366.4 12.3 %shard_map.293 = (f32[512,256]{1,0:T(8,128)}, f32[8,512]{1,0:T(8,128)}) custom-call(bf16[512,1024]{1,0:T(8,128)(2,1)} %get-tuple-element.87.refs_0_, f32[8,512]{1,0:T(8,128)} %select_maximum_fusion.3.refs_1_), custom_call_target="tpu_custom_call" | custom-call | tf_op jit(solution)/shard_map/pallas_call | solution.py:45
  379.5 2.7 multiply_reduce_fusion.9
  382.2 11.0 %shard_map.294.refs_4_ = bf16[512,1024]{1,0:T(8,128)(2,1)} custom-call(bf16[512,256]{1,0:T(8,128)(2,1)} %get-tuple-element.84.q), custom_call_target="tpu_custom_call" | custom-call | tf_op jit(solution)/shard_map/pallas_call | solution.py:45
  393.9 110.2 %shard_map.295 = (bf16[32,3072]{1,0:T(8,128)(2,1)}, bf16[32,4096]{1,0:T(8,128)(2,1)}, f32[32,1024]{1,0:T(8,128)}, f32[128,1024]{1,0:T(8,128)}, f32[8,256]{1,0:T(...) custom-call(bf16[4,8,32,1024]{3,2,1,0:T(8,128)(2,1)} %bitcast.159, ...), custom_call_target="tpu_custom_call" | custom-call | tf_op jit(solution)/shard_map/pallas_call | solution.py:45
  504.1 1.7 convert_element_type.243
  507.1 1.8 convert_element_type.244
  508.8 4.2 bitcast_convert_fusion.1
  513.1 3.9 convolution_bitcast_fusion.1
  517.0 2.5 bitcast_convert_fusion
  519.5 3.9 convolution_bitcast_fusion
  (148 shorter events, 32.4 us)
Async XLA Ops:
  0.6 219.4 %copy-start = (bf16[1,1024,1024]{2,1,0:T(8,128)(2,1)S(1)}, bf16[1,1024,1024]{2,1,0:T(8,128)(2,1)}, u32[]{:S(2)}) copy-start(bf16[1,1024,1024]{2,1,0:T(8,128)(2,1)} %param.33) | copy-start | bytes 6291460
  97.7 5.0 copy-start.9
  102.7 5.5 %copy-start.25 = (bf16[8,128,1024]{2,1,0:T(8,128)(2,1)S(1)}, bf16[8,128,1024]{2,1,0:T(8,128)(2,1)}, u32[]{:S(2)}) copy-start(bf16[8,128,1024]{2,1,0:T(8,128)(2,1)} %get-tuple-element.44) | copy-start | bytes 6291460
  107.2 1.0 copy-start.37
  110.4 13.2 %copy-start.22 = (s32[2,256,1]{1,2,0:T(1,128)S(1)}, s32[2,256,1]{1,2,0:T(1,128)}, u32[]{:S(2)}) copy-start(s32[2,256,1]{1,2,0:T(1,128)} %param.19) | copy-start | bytes 6148
  149.4 2.0 copy-start.2
  152.1 1.6 copy-start.26
  153.7 3.9 copy-start.23
  156.6 1.1 copy-start.29
  188.3 1.7 copy-start.3
  190.5 5.1 copy-start.19
  218.3 2.1 copy-start.39
  220.5 2.9 copy-start.4
  220.5 2.9 copy-start.28
  223.3 3.7 copy-start.31
  223.3 3.7 copy-start.6
  227.1 1.8 copy-start.35
  231.5 13.6 %copy-start.11 = (bf16[640,256]{1,0:T(8,128)(2,1)S(1)}, bf16[640,256]{1,0:T(8,128)(2,1)}, u32[]{:S(2)}) copy-start(bf16[640,256]{1,0:T(8,128)(2,1)} %fusion.54.q) | copy-start | bytes 983044
  277.9 5.1 copy-start.27
  283.0 3.8 copy-start.33
  283.0 20.0 %copy-start.8 = (f32[640,256]{1,0:T(8,128)S(1)}, f32[640,256]{1,0:T(8,128)}, u32[]{:S(2)}) copy-start(f32[640,256]{1,0:T(8,128)} %shard_map.285) | copy-start | bytes 1966084
  283.0 20.0 %copy-start.12 = (bf16[640,256]{1,0:T(8,128)(2,1)S(1)}, bf16[640,256]{1,0:T(8,128)(2,1)}, u32[]{:S(2)}) copy-start(bf16[640,256]{1,0:T(8,128)(2,1)} %get-tuple-element.80.q) | copy-start | bytes 983044
  346.1 4.6 copy-start.10
  350.6 2.8 copy-start.15
  350.6 2.8 copy-start.38
  353.5 2.6 copy-start.20
  353.5 2.6 copy-start.34
  356.1 3.2 copy-start.5
  356.1 3.2 copy-start.32
  359.3 3.4 copy-start.24
  362.7 16.8 %copy-start.16 = (bf16[2,256,256]{2,1,0:T(8,128)(2,1)S(1)}, bf16[2,256,256]{2,1,0:T(8,128)(2,1)}, u32[]{:S(2)}) copy-start(bf16[2,256,256]{2,1,0:T(8,128)(2,1)} %convolution_convert_fusion.7) | copy-start | bytes 786436
  508.8 4.3 copy-start.14
  508.8 4.3 copy-start.30
  513.1 3.9 copy-start.13
  517.0 2.5 copy-start.7
  517.0 2.5 copy-start.36
  519.5 4.0 copy-start.18
  519.5 4.8 copy-start.21
  519.5 5.4 %copy-start.17 = (f32[128,1024]{1,0:T(8,128)S(1)}, f32[128,1024]{1,0:T(8,128)}, u32[]{:S(2)}) copy-start(f32[128,1024]{1,0:T(8,128)} %get-tuple-element.140) | copy-start | bytes 1572868
  519.5 6.2 %copy-start.1 = (bf16[1,1024,1024]{2,1,0:T(8,128)(2,1)S(1)}, bf16[1,1024,1024]{2,1,0:T(8,128)(2,1)}, u32[]{:S(2)}) copy-start(bf16[1,1024,1024]{2,1,0:T(8,128)(2,1)} %param.33) | copy-start | bytes 6291460

commit v5 on v4

--- a/solution.py
+++ b/solution.py
@@ -299,14 +299,14 @@
 
 
 def tail_kernel(*refs):
-    (g_in, g_back, first, second, d_att, tok, n1, qkv, mixed, w_qkv, w_out, mask, gain, gain_d) = refs[:14]
-    o_qkv, o_in, o_out, o_back, o_gain, o_first, o_second, o_tok = refs[14:22]
-    g_qkv, g_out = refs[22:24]
-    acc = refs[24:28]
-    line_in = refs[28:32]
-    pair_in = refs[32:36]
-    (d_mix, d_qkv, part, unit, scales, stats, stats_in, stats_mid, stats_far, near_in, far, far_in, gains, gains_in) = refs[36:50]
-    (loc, exp_s, exp_r, cut_s, cut_r, pair_s, pair_r, line_s, line_r, s1, r1, s2, r2, st_s, st_r, gn_s, gn_r) = refs[50:]
+    (g_in, g_back, first, second, d_att, tok, n1, qkv, mixed, w_qkv, w_out, mask, gain, gain_d, res) = refs[:15]
+    o_qkv, o_in, o_out, o_back, o_gain, o_first, o_second, o_tok, o_res = refs[15:24]
+    g_qkv, g_out = refs[24:26]
+    acc = refs[26:30]
+    line_in = refs[30:34]
+    pair_in = refs[34:38]
+    (d_mix, d_qkv, part, unit, scales, stats, stats_in, stats_mid, stats_far, near_in, far, far_in, gains, gains_in) = refs[38:52]
+    (loc, exp_s, exp_r, cut_s, cut_r, pair_s, pair_r, line_s, line_r, s1, r1, s2, r2, st_s, st_r, gn_s, gn_r, o_s, o_r) = refs[52:]
     src = (g_qkv, g_in, g_out, g_back)
     pair_first = (True, True, False, False)
     me, beside, across = section_places()
@@ -431,6 +431,12 @@
             c = push(s.at[p], spot(d, me, hid), exp_s.at[i, k], exp_r.at[i, k], {"section": p})
             c.start()
             late.append(c)
+    def res_copy(to, frm):
+        return push(res.at[to], o_res.at[frm], o_s.at[to], o_r.at[frm], {"wide": to})
+
+    for j in range(1, 2 * length):
+        res_copy(lax.rem(w + j, 2 * length), w).start()
+    o_res[w] = res[w]
     group = (3, 1)
     cuts = [k * length // 4 for k in range(5)]
     small = g_out.shape[1]
@@ -558,7 +564,10 @@
     for c in late:
         c.wait()
     for j in range(1, wide):
-        gain_copy(lax.rem(w + j, wide), w).wait_send()
+        to = lax.rem(w + j, wide)
+        gain_copy(to, w).wait_send()
+        res_copy(to, w).wait_send()
+        res_copy(to, to).wait_recv()
 
     def finish(t, carry):
         for i in range(4):
@@ -575,7 +584,7 @@
     lax.fori_loop(0, length, finish, 0)
 
 
-def tail_call(g_in, g_back, first, second, d_att, tok, n1, qkv, mixed, w_qkv, w_out, mask, gain, gain_d, collective_id):
+def tail_call(g_in, g_back, first, second, d_att, tok, n1, qkv, mixed, w_qkv, w_out, mask, gain, gain_d, res, collective_id):
     wide = g_back.shape[0]
     length = wide // 2
     small = g_in.shape[2]
@@ -593,6 +602,7 @@
         expert,
         expert,
         ((count, QUARTER), F32),
+        (res.shape, BF16),
     ]
     scratch = [pltpu.VMEM((4, wide, small, 3 * QUARTER), BF16), pltpu.VMEM((wide, small, width), BF16)]
     for counts in (
@@ -633,23 +643,25 @@
         DMA((2,)),
         DMA((wide,)),
         DMA((wide,)),
+        DMA((wide,)),
+        DMA((wide,)),
     ]
     return call(
         tail_kernel,
         tuple(jax.ShapeDtypeStruct(*o) for o in outs),
-        [VM, VM, ANY, ANY] + [VM] * 10,
-        (ANY, ANY, VM, VM, VM, ANY, ANY, VM),
+        [VM, VM, ANY, ANY] + [VM] * 11,
+        (ANY, ANY, VM, VM, VM, ANY, ANY, VM, VM),
         scratch,
         collective_id,
-        *(g_in, g_back, first, second, d_att, tok, n1, qkv, mixed, w_qkv, w_out, mask, gain, gain_d),
+        *(g_in, g_back, first, second, d_att, tok, n1, qkv, mixed, w_qkv, w_out, mask, gain, gain_d, res),
     )
 
 
 def head_kernel(*refs):
-    qkv, inn, vec, outw, backw, first, second, tok, mask = refs[:9]
-    o_qkv, o_in, o_vec, o_out, o_back, o_first, o_second, o_tok, o_n1, o_act, o_mixed, o_att = refs[9:21]
-    st_qkv, st_in, st_vec, gain, part, near_in, far, far_in = refs[21:29]
-    loc, cut_s, cut_r, tok_s, tok_r, line_s, line_r, exp_s, exp_r, s1, r1, s2, r2, g_s, g_r = refs[29:]
+    qkv, inn, vec, outw, backw, first, second, tok, mask, cot = refs[:10]
+    o_qkv, o_in, o_vec, o_out, o_back, o_first, o_second, o_tok, o_n1, o_act, o_mixed, o_att, o_cot = refs[10:23]
+    st_qkv, st_in, st_vec, gain, part, near_in, far, far_in = refs[23:31]
+    loc, cut_s, cut_r, tok_s, tok_r, line_s, line_r, exp_s, exp_r, s1, r1, s2, r2, g_s, g_r, c_s, c_r = refs[31:]
     me, beside, across = section_places()
     core, side = lax.rem(me, 2), lax.div(me, 2)
     w, length, a, b = line_of_wide()
@@ -657,7 +669,7 @@
     mate = 2 * a + other
     diagonal = beside + across - me
     peers = [beside, across, diagonal]
-    greet_line(peers, False)
+    greet_line(peers, True)
     hid = o_first.shape[2]
     width = 4 * QUARTER
     sent, local_cuts = [], []
@@ -816,6 +828,20 @@
     steps(early, 1, 2)
     late += [own_item(i) for i in later]
     steps(early, 2, length)
+
+    def cot_place(which, block):
+        return o_cot.at[block, :, columns(which)]
+
+    def cot_wide(to, frm):
+        return push(cot.at[to], cot_place(me, frm), c_s.at[0, to], c_r.at[0, frm], {"wide": to})
+
+    def cot_spread(kind, block, to):
+        here = cot_place(across if kind == 3 else me, block)
+        return push(here, here, c_s.at[kind, block], c_r.at[kind, block], {"section": to})
+
+    for j in range(1, 2 * length):
+        cot_wide(lax.rem(w + j, 2 * length), w).start()
+    o_cot[w, :, columns(me)] = cot[w]
     for i in later:
         mate_item(i)
     for i in early:
@@ -893,14 +919,31 @@
             c.start()
             spread.append(c)
     steps(later, cuts[micro], cuts[3])
+    for j in range(wide):
+        block = lax.rem(w + j, wide)
+        if j:
+            cot_wide(block, block).wait_recv()
+        cot_spread(1, block, across).start()
+        cot_spread(2, block, beside).start()
     for k in range(chunks):
         spread[2 * k].wait()
         here = o_att.at[pl.ds(k * chunk, chunk), columns(across)]
         c = push(here, here, g_s.at[2, k], g_r.at[2, k], {"section": beside})
         c.start()
         spread.append(c)
+    for j in range(wide):
+        block = lax.rem(w + j, wide)
+        cot_spread(1, block, across).wait_recv()
+        cot_spread(3, block, beside).start()
     for i in later:
         pair_items(i)
+    for j in range(wide):
+        block = lax.rem(w + j, wide)
+        cot_spread(1, block, across).wait_send()
+        cot_spread(2, block, beside).wait()
+        cot_spread(3, block, beside).wait()
+        if j:
+            cot_wide(block, w).wait_send()
     for k in range(chunks):
         spread[2 * k + 1].wait()
         spread[2 * chunks + k].wait()
@@ -914,7 +957,8 @@
         c.wait()
 
 
-def head_call(qkv, inn, vec, outw, backw, first, second, tok, mask, wide, collective_id):
+def head_call(qkv, inn, vec, outw, backw, first, second, tok, mask, cot, collective_id):
+    wide = cot.shape[0]
     small = qkv.shape[0]
     hid = inn.shape[1] // 4
     cut = 3 * QUARTER
@@ -934,12 +978,13 @@
         ((count, cut), BF16),
         ((count, QUARTER), BF16),
         ((count, width), BF16),
+        ((*cot.shape[:2], width), BF16),
     ]
     return call(
         head_kernel,
         tuple(jax.ShapeDtypeStruct(*o) for o in outs),
-        [ANY] * 8 + [VM],
-        (VM, ANY, VM, VM, ANY, ANY, ANY, VM, VM, VM, VM, VM),
+        [ANY] * 8 + [VM, VM],
+        (VM, ANY, VM, VM, ANY, ANY, ANY, VM, VM, VM, VM, VM, VM),
         [
             pltpu.VMEM((4, small, cut), BF16),
             pltpu.VMEM((4, small, hid), BF16),
@@ -964,9 +1009,11 @@
             DMA((chunks,)),
             DMA((3, chunks)),
             DMA((3, chunks)),
+            DMA((4, wide)),
+            DMA((4, wide)),
         ],
         collective_id,
-        *(qkv, inn, vec, outw, backw, first, second, tok, mask),
+        *(qkv, inn, vec, outw, backw, first, second, tok, mask, cot),
     )
 
 
@@ -1055,6 +1102,29 @@
     small = qkv_weight.shape[0]
     qkv_cols = qkv_weight.shape[1] // sections
 
+    experts = jnp.arange(wide, dtype=jnp.int32)
+    choose = (routes == experts).astype(jnp.int32)
+    upto = (jnp.arange(rows)[:, None] >= jnp.arange(rows)[None, :]).astype(BF16)
+    ranking = jnp.einsum("rk,mke->mre", upto, choose.astype(BF16), preferred_element_type=F32).astype(jnp.int32) - 1
+    slot_of = routes[:, :, 0] * cap + jnp.sum(ranking * choose, axis=2)
+    onehot = (jnp.arange(wide * cap, dtype=jnp.int32)[None, :, None] == slot_of[:, None, :]).astype(BF16)
+
+    def to_slots(rows_q):
+        packed = jnp.einsum("msr,mrd->msd", onehot, rows_q.reshape(micro, rows, quarter), preferred_element_type=F32)
+        packed = packed.astype(BF16).reshape(micro, wide, cap, quarter).transpose(1, 0, 2, 3)
+        return packed.reshape(wide, micro * cap, quarter)
+
+    def to_experts(rows_q):
+        return wide_exchange(to_slots(rows_q), True).reshape(wide * micro * cap, width)
+
+    def from_slots(back):
+        back = back.reshape(wide, micro, cap, quarter).transpose(1, 0, 2, 3).reshape(micro, wide * cap, quarter)
+        got = jnp.einsum("msr,msd->mrd", onehot, back, preferred_element_type=F32)
+        return got.astype(BF16).reshape(tok_rows, quarter)
+
+    def to_tokens(slots_q):
+        return from_slots(wide_exchange(slots_q.reshape(wide, micro * cap, quarter), False))
+
     per = 128 // small
     spread = lambda v: lax.dynamic_update_slice_in_dim(
         jnp.zeros((1, 128), F32), v.astype(F32)[None], lax.rem(wide_id, per) * small, 1
@@ -1064,7 +1134,7 @@
     allowed = allowed_of(seq_lengths, rows)
     tokens_q = tokens_in.reshape(tok_rows, quarter)
 
-    (qkv_w, in_w, vectors, out_w, back_w, first_w, second_w, tokens, normed_a, packed, mixed, attended) = head_call(
+    (qkv_w, in_w, vectors, out_w, back_w, first_w, second_w, tokens, normed_a, packed, mixed, attended, d_mixed) = head_call(
         qkv_weight,
         ffn_in,
         vectors,
@@ -1074,7 +1144,7 @@
         second_in[0],
         tokens_q,
         allowed,
-        wide,
+        to_slots(cotangent.reshape(tok_rows, quarter)),
         id_of("head"),
     )
     qkv_w = qkv_w.reshape(width, qkv_cols)
@@ -1092,24 +1162,6 @@
     first_b = first_back[0]
     second_b = second_back[0]
 
-    experts = jnp.arange(wide, dtype=jnp.int32)
-    choose = (routes == experts).astype(jnp.int32)
-    upto = (jnp.arange(rows)[:, None] >= jnp.arange(rows)[None, :]).astype(BF16)
-    ranking = jnp.einsum("rk,mke->mre", upto, choose.astype(BF16), preferred_element_type=F32).astype(jnp.int32) - 1
-    slot_of = routes[:, :, 0] * cap + jnp.sum(ranking * choose, axis=2)
-    onehot = (jnp.arange(wide * cap, dtype=jnp.int32)[None, :, None] == slot_of[:, None, :]).astype(BF16)
-
-    def to_experts(rows_q):
-        packed = jnp.einsum("msr,mrd->msd", onehot, rows_q.reshape(micro, rows, quarter), preferred_element_type=F32)
-        packed = packed.astype(BF16).reshape(micro, wide, cap, quarter).transpose(1, 0, 2, 3)
-        return wide_exchange(packed.reshape(wide, micro * cap, quarter), True).reshape(wide * micro * cap, width)
-
-    def to_tokens(slots_q):
-        back = wide_exchange(slots_q.reshape(wide, micro * cap, quarter), False)
-        back = back.reshape(wide, micro, cap, quarter).transpose(1, 0, 2, 3).reshape(micro, wide * cap, quarter)
-        got = jnp.einsum("msr,msd->mrd", onehot, back, preferred_element_type=F32)
-        return got.astype(BF16).reshape(tok_rows, quarter)
-
     attended_q = own_quarter(attended)
 
     def branch(v, w_in, w_back, gain):
@@ -1141,7 +1193,7 @@
     fed_q = (attended_q.astype(F32) + reduce_quarters(part)).astype(BF16)
     routed = to_experts(fed_q)
     routed_q = own_quarter(routed)
-    d_mixed = to_experts(cotangent.reshape(tok_rows, quarter)).astype(F32)
+    d_mixed = d_mixed.reshape(wide * micro * cap, width).astype(F32)
     d_mixed_q = own_quarter(d_mixed)
     saved_1, part = branch(routed, first_w, first_b, gain_first)
     first_q = (routed_q.astype(F32) + reduce_quarters(part)).astype(BF16)
@@ -1150,7 +1202,6 @@
     gate = jax.nn.sigmoid(jnp.sum(routed.astype(F32) * centre, axis=-1, keepdims=True))
     second_q = first_q.astype(F32) + reduce_quarters(part)
     mixed_q = routed_q.astype(F32) + gate * second_q
-    block_out = to_tokens(mixed_q.astype(BF16)).reshape(micro, rows, quarter)
 
     d_second = gate * d_mixed
     d_second_q = gate * d_mixed_q
@@ -1172,7 +1223,7 @@
     def by_row(grad):
         return grad.astype(BF16).reshape(sections, wide, small, grad.shape[1])
 
-    qkv_grad, ffn_in_grad, out_grad, ffn_back_grad, d_gains, d_first_in, d_second_in, tokens_grad = tail_call(
+    qkv_grad, ffn_in_grad, out_grad, ffn_back_grad, d_gains, d_first_in, d_second_in, tokens_grad, result = tail_call(
         by_row(d_in),
         d_back.astype(BF16).reshape(wide, hid // wide, width),
         d_first_in.astype(BF16).reshape(sections, quarter, hid),
@@ -1187,8 +1238,10 @@
         allowed,
         gain_attn,
         d_gain_ffn[None],
+        mixed_q.astype(BF16).reshape(wide, micro * cap, quarter),
         id_of("tail"),
     )
+    block_out = from_slots(result).reshape(micro, rows, quarter)
     d_gains = lax.dynamic_slice_in_dim(d_gains, wide_id * small, small, axis=1)
     tokens_grad = tokens_grad.reshape(micro, rows, quarter)
     return (

time: 532 us -> 515 us (0.968)
  Pallas kernels: 398 us -> 381 us
    pallas_call x16 -> x14, Pallas kernels: 398 us -> 381 us  [call(): pl.pallas_call(kernel, out_shape=out_shape, in_specs=in_specs, out_specs=...]
where the time goes in v5:
time: 515 us; the launch traced here: 508 us
  Pallas kernels  381 us (74%)
  matrix products  67.1 us (13%)
  other arithmetic  44.1 us (9%)
  local copies, waits for them, and re-layouts  14.1 us (3%)
    pallas_call x14, Pallas kernels, call(): pl.pallas_call(kernel, out_shape=out_shape, in_specs=in_specs, out_specs=...  381 us
    dot_general x6, matrix products, dot_nt(): lax.dot_general(left, right, (((1,), (1,)), ((), ())), preferred_element_...  23.1 us
    dot_general x6, matrix products, dot(): return jnp.dot(left, right, preferred_element_type=F32)  20.2 us
    dot_general x6, matrix products, dot_tn(): lax.dot_general(left, right, (((0,), (0,)), ((), ())), preferred_element_...  19.8 us

profile of v5, /device:TPU:12, one launch (start us, length us, event | category | flops | bytes accessed | tf_op | source)
XLA Modules:
  0.0 508.0 jit_solution(17069893989101700956)
XLA Ops:
  9.2 1.2 convolution_convert_fusion.6
  11.2 97.8 %shard_map.280 = (bf16[4,8,32,768]{3,2,1,0:T(8,128)(2,1)}, bf16[4,8,32,1024]{3,2,1,0:T(8,128)(2,1)}, f32[4,8,8,128]{3,2,1,0:T(8,128)}, bf16[8,32,1024]{2,1,0:T(8...) custom-call(bf16[32,3072]{1,0:T(8,128)(2,1)} %refs_0_.1, ...), custom_call_target="tpu_custom_call" | custom-call | tf_op jit(solution)/shard_map/pallas_call | solution.py:45
  110.2 1.4 convert_reduce_fusion.2
  111.6 1.6 fusion.23
  113.3 4.5 multiply_convert_fusion.6
  118.5 4.1 convolution_convert_fusion.4.refs_0_
  122.7 12.0 %shard_map.281 = f32[512,256]{1,0:T(8,128)} custom-call(bf16[512,1024]{1,0:T(8,128)(2,1)} %convolution_convert_fusion.4.refs_0_), custom_call_target="tpu_custom_call" | custom-call | tf_op jit(solution)/shard_map/pallas_call | solution.py:45
  136.8 31.1 %shard_map.282 = bf16[8,80,1024]{2,1,0:T(8,128)(2,1)} custom-call(bf16[8,80,256]{2,1,0:T(8,128)(2,1)} %bitcast.170), custom_call_target="tpu_custom_call" | custom-call | tf_op jit(solution)/shard_map/pallas_call | solution.py:45
  168.0 2.0 fusion.8
  172.3 2.9 multiply_convert_fusion.5
  176.2 2.6 fusion.42.refs_0_
  178.8 13.6 %shard_map.283 = f32[640,256]{1,0:T(8,128)} custom-call(bf16[640,1024]{1,0:T(8,128)(2,1)} %fusion.42.refs_0_), custom_call_target="tpu_custom_call" | custom-call | tf_op jit(solution)/shard_map/pallas_call | solution.py:45
  192.4 1.9 fusion.54.q
  194.3 13.1 %shard_map.284 = bf16[640,1024]{1,0:T(8,128)(2,1)} custom-call(bf16[640,256]{1,0:T(8,128)(2,1)} %fusion.54.q), custom_call_target="tpu_custom_call" | custom-call | tf_op jit(solution)/shard_map/pallas_call | solution.py:45
  207.4 1.7 convert_reduce_fusion.1
  209.6 3.5 multiply_convert_fusion.2
  213.4 2.9 fusion.14
  216.3 3.7 multiply_reduce_fusion.3
  220.0 1.8 convert.16
  221.8 2.6 fusion.45.refs_0_
  224.5 13.6 %shard_map.285 = f32[640,256]{1,0:T(8,128)} custom-call(bf16[640,1024]{1,0:T(8,128)(2,1)} %fusion.45.refs_0_), custom_call_target="tpu_custom_call" | custom-call | tf_op jit(solution)/shard_map/pallas_call | solution.py:45
  238.1 1.5 multiply_reduce_fusion.8
  240.2 14.0 %shard_map.286 = (f32[640,256]{1,0:T(8,128)}, f32[8,640]{1,0:T(8,128)}) custom-call(bf16[640,1024]{1,0:T(8,128)(2,1)} %get-tuple-element.90.refs_0_, f32[8,640]{1,0:T(8,128)} %select_maximum_fusion.1.refs_1_), custom_call_target="tpu_custom_call" | custom-call | tf_op jit(solution)/shard_map/pallas_call | solution.py:45
  255.1 3.2 multiply_reduce_fusion.6
  258.3 12.6 %shard_map.287 = bf16[640,1024]{1,0:T(8,128)(2,1)} custom-call(bf16[640,256]{1,0:T(8,128)(2,1)} %get-tuple-element.84.q), custom_call_target="tpu_custom_call" | custom-call | tf_op jit(solution)/shard_map/pallas_call | solution.py:45
  270.9 5.1 fusion.20
  276.0 3.8 multiply_reduce_fusion.2
  280.4 14.0 %shard_map.288 = (f32[640,256]{1,0:T(8,128)}, f32[8,640]{1,0:T(8,128)}) custom-call(bf16[640,1024]{1,0:T(8,128)(2,1)} %get-tuple-element.89.refs_0_, f32[8,640]{1,0:T(8,128)} %select_maximum_fusion.refs_1_), custom_call_target="tpu_custom_call" | custom-call | tf_op jit(solution)/shard_map/pallas_call | solution.py:45
  295.9 3.4 multiply_reduce_fusion.7
  299.3 12.6 %shard_map.289 = bf16[8,80,256]{2,1,0:T(8,128)(2,1)} custom-call(bf16[8,80,256]{2,1,0:T(8,128)(2,1)} %bitcast.164), custom_call_target="tpu_custom_call" | custom-call | tf_op jit(solution)/shard_map/pallas_call | solution.py:45
  313.0 1.1 convolution_convert_fusion.8
  314.1 11.1 %shard_map.290 = bf16[512,1024]{1,0:T(8,128)(2,1)} custom-call(bf16[512,256]{1,0:T(8,128)(2,1)} %bitcast.173), custom_call_target="tpu_custom_call" | custom-call | tf_op jit(solution)/shard_map/pallas_call | solution.py:45
  325.2 4.5 fusion.29
  329.8 2.8 convolution_convert_fusion.1
  332.6 2.6 convolution_convert_fusion
  335.2 3.2 convolution_convert_fusion.3
  338.4 3.5 convolution_convert_fusion.2
  341.9 3.2 multiply_reduce_fusion.5
  345.6 12.3 %shard_map.291 = (f32[512,256]{1,0:T(8,128)}, f32[8,512]{1,0:T(8,128)}) custom-call(bf16[512,1024]{1,0:T(8,128)(2,1)} %get-tuple-element.91.refs_0_, f32[8,512]{1,0:T(8,128)} %select_maximum_fusion.3.refs_1_), custom_call_target="tpu_custom_call" | custom-call | tf_op jit(solution)/shard_map/pallas_call | solution.py:45
  358.7 2.7 multiply_reduce_fusion.9
  361.4 11.0 %shard_map.292.refs_4_ = bf16[512,1024]{1,0:T(8,128)(2,1)} custom-call(bf16[512,256]{1,0:T(8,128)(2,1)} %get-tuple-element.88.q), custom_call_target="tpu_custom_call" | custom-call | tf_op jit(solution)/shard_map/pallas_call | solution.py:45
  373.1 112.5 %shard_map.293 = (bf16[32,3072]{1,0:T(8,128)(2,1)}, bf16[32,4096]{1,0:T(8,128)(2,1)}, f32[32,1024]{1,0:T(8,128)}, f32[128,1024]{1,0:T(8,128)}, f32[8,256]{1,0:T(...) custom-call(bf16[4,8,32,1024]{3,2,1,0:T(8,128)(2,1)} %bitcast.157, ...), custom_call_target="tpu_custom_call" | custom-call | tf_op jit(solution)/shard_map/pallas_call | solution.py:45
  487.9 1.7 convert_element_type.243
  490.9 1.8 convert_element_type.244
  492.6 2.5 bitcast_convert_fusion.1
  495.2 3.9 convolution_bitcast_fusion.1
  499.0 2.5 bitcast_convert_fusion
  501.6 3.9 convolution_bitcast_fusion
  (136 shorter events, 29.9 us)
Async XLA Ops:
  0.6 212.7 %copy-start = (bf16[1,1024,1024]{2,1,0:T(8,128)(2,1)S(1)}, bf16[1,1024,1024]{2,1,0:T(8,128)(2,1)}, u32[]{:S(2)}) copy-start(bf16[1,1024,1024]{2,1,0:T(8,128)(2,1)} %param.33) | copy-start | bytes 6291460
  109.1 4.2 copy-start.6
  168.0 2.0 copy-start.2
  170.7 1.6 copy-start.23
  172.3 3.9 copy-start.21
  175.1 1.1 copy-start.26
  207.4 1.7 copy-start.3
  209.6 3.5 copy-start.9
  213.1 8.7 %copy-start.32 = (bf16[640,1024]{1,0:T(8,128)(2,1)}, bf16[640,1024]{1,0:T(8,128)(2,1)S(1)}, u32[]{:S(2)}) copy-start(bf16[640,1024]{1,0:T(8,128)(2,1)S(1)} %get-tuple-element.113) | copy-start | bytes 3932164
  213.4 2.9 copy-start.25
  216.3 3.7 copy-start.28
  224.5 13.6 %copy-start.8 = (bf16[640,256]{1,0:T(8,128)(2,1)S(1)}, bf16[640,256]{1,0:T(8,128)(2,1)}, u32[]{:S(2)}) copy-start(bf16[640,256]{1,0:T(8,128)(2,1)} %fusion.54.q) | copy-start | bytes 983044
  270.8 5.1 %copy-start.24 = (bf16[4,256,1024]{2,1,0:T(8,128)(2,1)S(1)}, bf16[4,256,1024]{2,1,0:T(8,128)(2,1)}, u32[]{:S(2)}) copy-start(bf16[4,256,1024]{2,1,0:T(8,128)(2,1)} %get-tuple-element.48) | copy-start | bytes 6291460
  275.9 3.8 copy-start.30
  275.9 20.0 %copy-start.5 = (f32[640,256]{1,0:T(8,128)S(1)}, f32[640,256]{1,0:T(8,128)}, u32[]{:S(2)}) copy-start(f32[640,256]{1,0:T(8,128)} %shard_map.285) | copy-start | bytes 1966084
  276.0 20.0 %copy-start.11 = (bf16[640,256]{1,0:T(8,128)(2,1)S(1)}, bf16[640,256]{1,0:T(8,128)(2,1)}, u32[]{:S(2)}) copy-start(bf16[640,256]{1,0:T(8,128)(2,1)} %get-tuple-element.84.q) | copy-start | bytes 983044
  325.2 4.6 copy-start.7
  329.8 2.8 copy-start.15
  329.8 2.8 copy-start.34
  332.6 2.6 copy-start.19
  332.6 2.6 copy-start.31
  335.2 3.2 copy-start.4
  335.2 3.2 copy-start.29
  338.4 3.5 copy-start.22
  341.9 16.8 %copy-start.16 = (bf16[2,256,256]{2,1,0:T(8,128)(2,1)S(1)}, bf16[2,256,256]{2,1,0:T(8,128)(2,1)}, u32[]{:S(2)}) copy-start(bf16[2,256,256]{2,1,0:T(8,128)(2,1)} %convolution_convert_fusion.8) | copy-start | bytes 786436
  485.6 7.1 %copy-start.13 = (bf16[256,4096]{1,0:T(8,128)(2,1)S(1)}, bf16[256,4096]{1,0:T(8,128)(2,1)}, u32[]{:S(2)}) copy-start(bf16[256,4096]{1,0:T(8,128)(2,1)} %get-tuple-element.69) | copy-start | bytes 6291460
  492.6 2.5 copy-start.14
  492.6 2.5 copy-start.27
  495.2 3.9 copy-start.12
  499.0 2.5 copy-start.10
  499.0 2.5 copy-start.33
  501.6 4.0 copy-start.18
  501.6 4.8 copy-start.20
  501.6 5.4 %copy-start.17 = (f32[128,1024]{1,0:T(8,128)S(1)}, f32[128,1024]{1,0:T(8,128)}, u32[]{:S(2)}) copy-start(f32[128,1024]{1,0:T(8,128)} %get-tuple-element.144) | copy-start | bytes 1572868
  501.6 6.2 %copy-start.1 = (bf16[1,1024,1024]{2,1,0:T(8,128)(2,1)S(1)}, bf16[1,1024,1024]{2,1,0:T(8,128)(2,1)}, u32[]{:S(2)}) copy-start(bf16[1,1024,1024]{2,1,0:T(8,128)(2,1)} %param.33) | copy-start | bytes 6291460

commit v6 on v5

--- a/solution.py
+++ b/solution.py
@@ -716,7 +716,7 @@
         (st_qkv, o_qkv, True),
         (outw, o_out, False),
         (st_in, o_in, True),
-        (backw, o_back, False),
+        (backw, o_back, True),
         (st_vec, o_vec, False),
     )
     staged = {0: 0, 2: 1, 4: 2}

time: 515 us -> 504 us (0.979)
  Pallas kernels: 381 us -> 371 us
    pallas_call x14, Pallas kernels: 381 us -> 371 us  [call(): pl.pallas_call(kernel, out_shape=out_shape, in_specs=in_specs, out_specs=...]
where the time goes in v6:
time: 504 us; the launch traced here: 497 us
  Pallas kernels  371 us (74%)
  matrix products  67.1 us (13%)
  other arithmetic  44.1 us (9%)
  local copies, waits for them, and re-layouts  14.1 us (3%)
    pallas_call x14, Pallas kernels, call(): pl.pallas_call(kernel, out_shape=out_shape, in_specs=in_specs, out_specs=...  371 us
    dot_general x6, matrix products, dot_nt(): lax.dot_general(left, right, (((1,), (1,)), ((), ())), preferred_element_...  23.1 us
    dot_general x6, matrix products, dot(): return jnp.dot(left, right, preferred_element_type=F32)  20.2 us
    dot_general x6, matrix products, dot_tn(): lax.dot_general(left, right, (((0,), (0,)), ((), ())), preferred_element_...  19.8 us

profile of v6, /device:TPU:12, one launch (start us, length us, event | category | flops | bytes accessed | tf_op | source)
XLA Modules:
  0.0 497.4 jit_solution(11653851777949147748)
XLA Ops:
  9.2 1.2 convolution_convert_fusion.6
  11.2 91.3 %shard_map.280 = (bf16[4,8,32,768]{3,2,1,0:T(8,128)(2,1)}, bf16[4,8,32,1024]{3,2,1,0:T(8,128)(2,1)}, f32[4,8,8,128]{3,2,1,0:T(8,128)}, bf16[8,32,1024]{2,1,0:T(8...) custom-call(bf16[32,3072]{1,0:T(8,128)(2,1)} %refs_0_.1, ...), custom_call_target="tpu_custom_call" | custom-call | tf_op jit(solution)/shard_map/pallas_call | solution.py:45
  103.7 1.4 convert_reduce_fusion.2
  105.1 1.6 fusion.23
  106.8 4.5 multiply_convert_fusion.6
  112.0 4.1 convolution_convert_fusion.4.refs_0_
  116.2 12.0 %shard_map.281 = f32[512,256]{1,0:T(8,128)} custom-call(bf16[512,1024]{1,0:T(8,128)(2,1)} %convolution_convert_fusion.4.refs_0_), custom_call_target="tpu_custom_call" | custom-call | tf_op jit(solution)/shard_map/pallas_call | solution.py:45
  130.3 27.4 %shard_map.282 = bf16[8,80,1024]{2,1,0:T(8,128)(2,1)} custom-call(bf16[8,80,256]{2,1,0:T(8,128)(2,1)} %bitcast.170), custom_call_target="tpu_custom_call" | custom-call | tf_op jit(solution)/shard_map/pallas_call | solution.py:45
  157.8 2.0 fusion.8
  162.1 2.9 multiply_convert_fusion.5
  166.0 2.6 fusion.42.refs_0_
  168.6 13.6 %shard_map.283 = f32[640,256]{1,0:T(8,128)} custom-call(bf16[640,1024]{1,0:T(8,128)(2,1)} %fusion.42.refs_0_), custom_call_target="tpu_custom_call" | custom-call | tf_op jit(solution)/shard_map/pallas_call | solution.py:45
  182.1 1.9 fusion.54.q
  184.1 12.6 %shard_map.284 = bf16[640,1024]{1,0:T(8,128)(2,1)} custom-call(bf16[640,256]{1,0:T(8,128)(2,1)} %fusion.54.q), custom_call_target="tpu_custom_call" | custom-call | tf_op jit(solution)/shard_map/pallas_call | solution.py:45
  196.7 1.7 convert_reduce_fusion.1
  198.9 3.5 multiply_convert_fusion.2
  202.6 2.9 fusion.14
  205.5 3.7 multiply_reduce_fusion.3
  209.2 1.8 convert.16
  211.1 2.6 fusion.45.refs_0_
  213.7 13.6 %shard_map.285 = f32[640,256]{1,0:T(8,128)} custom-call(bf16[640,1024]{1,0:T(8,128)(2,1)} %fusion.45.refs_0_), custom_call_target="tpu_custom_call" | custom-call | tf_op jit(solution)/shard_map/pallas_call | solution.py:45
  227.4 1.5 multiply_reduce_fusion.8
  229.5 14.0 %shard_map.286 = (f32[640,256]{1,0:T(8,128)}, f32[8,640]{1,0:T(8,128)}) custom-call(bf16[640,1024]{1,0:T(8,128)(2,1)} %get-tuple-element.90.refs_0_, f32[8,640]{1,0:T(8,128)} %select_maximum_fusion.1.refs_1_), custom_call_target="tpu_custom_call" | custom-call | tf_op jit(solution)/shard_map/pallas_call | solution.py:45
  244.3 3.2 multiply_reduce_fusion.6
  247.5 12.6 %shard_map.287 = bf16[640,1024]{1,0:T(8,128)(2,1)} custom-call(bf16[640,256]{1,0:T(8,128)(2,1)} %get-tuple-element.84.q), custom_call_target="tpu_custom_call" | custom-call | tf_op jit(solution)/shard_map/pallas_call | solution.py:45
  260.1 5.1 %fusion.20 = bf16[640,1024]{1,0:T(8,128)(2,1)S(1)} fusion(f32[640,1024]{1,0:T(8,128)} %get-tuple-element.111, bf16[640,1024]{1,0:T(8,128)(2,1)} %shard_map.287, bf16[1,1024,1024]{2,1,0:T(8,128)(2,1)} %param.30), kind=kOutput, calls=%fused_computation.30 | convolution fusion | flops 1348730880 | bytes 7340032 | tf_op jit(solution)/shard_map/dot_general | solution.py:1025
  265.2 3.8 multiply_reduce_fusion.2
  269.6 14.0 %shard_map.288 = (f32[640,256]{1,0:T(8,128)}, f32[8,640]{1,0:T(8,128)}) custom-call(bf16[640,1024]{1,0:T(8,128)(2,1)} %get-tuple-element.89.refs_0_, f32[8,640]{1,0:T(8,128)} %select_maximum_fusion.refs_1_), custom_call_target="tpu_custom_call" | custom-call | tf_op jit(solution)/shard_map/pallas_call | solution.py:45
  285.2 3.4 multiply_reduce_fusion.7
  288.6 12.6 %shard_map.289 = bf16[8,80,256]{2,1,0:T(8,128)(2,1)} custom-call(bf16[8,80,256]{2,1,0:T(8,128)(2,1)} %bitcast.164), custom_call_target="tpu_custom_call" | custom-call | tf_op jit(solution)/shard_map/pallas_call | solution.py:45
  302.2 1.1 convolution_convert_fusion.8
  303.3 11.1 %shard_map.290 = bf16[512,1024]{1,0:T(8,128)(2,1)} custom-call(bf16[512,256]{1,0:T(8,128)(2,1)} %bitcast.173), custom_call_target="tpu_custom_call" | custom-call | tf_op jit(solution)/shard_map/pallas_call | solution.py:45
  314.4 4.5 fusion.29
  319.0 2.8 convolution_convert_fusion.1
  321.8 2.6 convolution_convert_fusion
  324.4 3.2 convolution_convert_fusion.3
  327.6 3.5 convolution_convert_fusion.2
  331.1 3.2 multiply_reduce_fusion.5
  334.9 12.3 %shard_map.291 = (f32[512,256]{1,0:T(8,128)}, f32[8,512]{1,0:T(8,128)}) custom-call(bf16[512,1024]{1,0:T(8,128)(2,1)} %get-tuple-element.91.refs_0_, f32[8,512]{1,0:T(8,128)} %select_maximum_fusion.3.refs_1_), custom_call_target="tpu_custom_call" | custom-call | tf_op jit(solution)/shard_map/pallas_call | solution.py:45
  347.9 2.7 multiply_reduce_fusion.9
  350.7 11.0 %shard_map.292.refs_4_ = bf16[512,1024]{1,0:T(8,128)(2,1)} custom-call(bf16[512,256]{1,0:T(8,128)(2,1)} %get-tuple-element.88.q), custom_call_target="tpu_custom_call" | custom-call | tf_op jit(solution)/shard_map/pallas_call | solution.py:45
  362.3 112.6 %shard_map.293 = (bf16[32,3072]{1,0:T(8,128)(2,1)}, bf16[32,4096]{1,0:T(8,128)(2,1)}, f32[32,1024]{1,0:T(8,128)}, f32[128,1024]{1,0:T(8,128)}, f32[8,256]{1,0:T(...) custom-call(bf16[4,8,32,1024]{3,2,1,0:T(8,128)(2,1)} %bitcast.157, ...), custom_call_target="tpu_custom_call" | custom-call | tf_op jit(solution)/shard_map/pallas_call | solution.py:45
  477.2 1.7 convert_element_type.243
  480.2 1.8 convert_element_type.244
  482.0 2.5 bitcast_convert_fusion.1
  484.5 3.9 convolution_bitcast_fusion.1
  488.4 2.5 bitcast_convert_fusion
  490.9 3.9 convolution_bitcast_fusion
  (136 shorter events, 29.9 us)
Async XLA Ops:
  0.6 202.0 %copy-start = (bf16[1,1024,1024]{2,1,0:T(8,128)(2,1)S(1)}, bf16[1,1024,1024]{2,1,0:T(8,128)(2,1)}, u32[]{:S(2)}) copy-start(bf16[1,1024,1024]{2,1,0:T(8,128)(2,1)} %param.33) | copy-start | bytes 6291460
  102.6 4.2 copy-start.6
  157.7 2.0 copy-start.2
  160.5 1.6 copy-start.23
  162.1 3.9 copy-start.21
  164.9 1.1 copy-start.26
  196.6 1.7 copy-start.3
  198.8 3.5 copy-start.9
  202.3 8.8 %copy-start.32 = (bf16[640,1024]{1,0:T(8,128)(2,1)}, bf16[640,1024]{1,0:T(8,128)(2,1)S(1)}, u32[]{:S(2)}) copy-start(bf16[640,1024]{1,0:T(8,128)(2,1)S(1)} %get-tuple-element.113) | copy-start | bytes 3932164
  202.6 2.9 copy-start.25
  205.5 3.7 copy-start.28
  213.7 13.6 %copy-start.8 = (bf16[640,256]{1,0:T(8,128)(2,1)S(1)}, bf16[640,256]{1,0:T(8,128)(2,1)}, u32[]{:S(2)}) copy-start(bf16[640,256]{1,0:T(8,128)(2,1)} %fusion.54.q) | copy-start | bytes 983044
  260.1 5.1 %copy-start.24 = (bf16[4,256,1024]{2,1,0:T(8,128)(2,1)S(1)}, bf16[4,256,1024]{2,1,0:T(8,128)(2,1)}, u32[]{:S(2)}) copy-start(bf16[4,256,1024]{2,1,0:T(8,128)(2,1)} %get-tuple-element.48) | copy-start | bytes 6291460
  265.2 3.8 copy-start.30
  265.2 20.0 %copy-start.5 = (f32[640,256]{1,0:T(8,128)S(1)}, f32[640,256]{1,0:T(8,128)}, u32[]{:S(2)}) copy-start(f32[640,256]{1,0:T(8,128)} %shard_map.285) | copy-start | bytes 1966084
  265.2 20.0 %copy-start.11 = (bf16[640,256]{1,0:T(8,128)(2,1)S(1)}, bf16[640,256]{1,0:T(8,128)(2,1)}, u32[]{:S(2)}) copy-start(bf16[640,256]{1,0:T(8,128)(2,1)} %get-tuple-element.84.q) | copy-start | bytes 983044
  314.4 4.6 copy-start.7
  319.0 2.8 copy-start.15
  319.0 2.8 copy-start.34
  321.8 2.6 copy-start.19
  321.8 2.6 copy-start.31
  324.4 3.2 copy-start.4
  324.4 3.2 copy-start.29
  327.6 3.5 copy-start.22
  331.1 16.8 %copy-start.16 = (bf16[2,256,256]{2,1,0:T(8,128)(2,1)S(1)}, bf16[2,256,256]{2,1,0:T(8,128)(2,1)}, u32[]{:S(2)}) copy-start(bf16[2,256,256]{2,1,0:T(8,128)(2,1)} %convolution_convert_fusion.8) | copy-start | bytes 786436
  474.9 7.1 %copy-start.13 = (bf16[256,4096]{1,0:T(8,128)(2,1)S(1)}, bf16[256,4096]{1,0:T(8,128)(2,1)}, u32[]{:S(2)}) copy-start(bf16[256,4096]{1,0:T(8,128)(2,1)} %get-tuple-element.69) | copy-start | bytes 6291460
  482.0 2.5 copy-start.14
  482.0 2.5 copy-start.27
  484.5 3.9 copy-start.12
  488.4 2.5 copy-start.10
  488.4 2.5 copy-start.33
  490.9 4.0 copy-start.18
  490.9 4.8 copy-start.20
  490.9 5.4 %copy-start.17 = (f32[128,1024]{1,0:T(8,128)S(1)}, f32[128,1024]{1,0:T(8,128)}, u32[]{:S(2)}) copy-start(f32[128,1024]{1,0:T(8,128)} %get-tuple-element.144) | copy-start | bytes 1572868
  490.9 6.2 %copy-start.1 = (bf16[1,1024,1024]{2,1,0:T(8,128)(2,1)S(1)}, bf16[1,1024,1024]{2,1,0:T(8,128)(2,1)}, u32[]{:S(2)}) copy-start(bf16[1,1024,1024]{2,1,0:T(8,128)(2,1)} %param.33) | copy-start | bytes 6291460
